TPU v7x, 32 devices: a whole 2x2x4 slice. The times are simulated.
32 devices in a mesh: groups: 2 (over y), tiles: 4 (over z), heads: 2 (over x), kv: 2 (over core).
Axes of the slice: x: 2, y: 2, z: 4, core: 2. Of those that a mesh axis runs over, the one named last changes fastest.
Arguments:
- features: bfloat16 [12288, 1536], P(('groups', 'tiles')), parts along dimension 0, may hold values from -6 to 6
- counts: int32 [8], P(('groups', 'tiles')), parts along dimension 0, may hold values from 1 to 6
- tile_mask: int32 [48, 256], P(('groups', 'tiles')), parts along dimension 0, may hold values from 0 to 1, as said below
- queries: bfloat16 [256, 768], P(('heads', 'kv')), may hold values from -6 to 6
- norm_gain: float32 [2, 768], replicated, may hold values from 0.5 to 1.5
- head_scale: float32 [12], P('heads'), may hold values from 1 to 4
- w_query: bfloat16 [2, 768, 768], P(None, None, ('heads', 'kv')), may hold values from -0.21875 to 0.21875
- w_kv: bfloat16 [2, 1536, 2, 768], P(None, None, 'kv', 'heads'), may hold values from -0.15625 to 0.15625
- w_out: bfloat16 [2, 768, 768], P(None, ('heads', 'kv')), may hold values from -0.21875 to 0.21875
Outputs:
- query_states: float32 [512, 768], P(('groups', 'heads', 'kv')), parts along dimension 0
There are 2 independent parts, one for each index of `groups`. A program takes and returns all parts, laid end to end along the dimension named above; an argument that names none is the same for every part. Nothing has to cross between parts.
Inputs may be any that keep to these rules, and one draw needn't show every extreme that they name: `tile_mask`: the first tile of every block slot is 1.
All inputs are finite; a program needn't handle non-finite values.
Results may differ from a plain program's by a relative error of at most 0.012.
The roundings to bfloat16 on the way count: a program that leaves them out, or rounds other values in their place, can miss the bound.
Values may be sent and summed in bfloat16 or wider, within the bound.
No kernel may reach another device: no remote copies, remote signals or barrier semaphores. Data moves between devices by JAX's collectives and lax.ppermute only.
A program may use at most 64 MiB of HBM per device.

v0:
```python
import functools
import math

import jax
import jax.numpy as jnp
from jax import lax
from jax.experimental import pallas as pl
from jax.experimental.pallas import tpu as pltpu
from jax.sharding import PartitionSpec as P


SOFT_CAP = 50.0
NORM_EPS = 1e-06
LANES = 128
SPLIT = 16
ROOM = 4 << 20


def normalize(hidden, gain_row):
    return (
        hidden * lax.rsqrt(jnp.mean(hidden * hidden, axis=-1, keepdims=True) + NORM_EPS) * gain_row
    )


def generic_body(features, counts, tile_mask, queries, norm_gain, head_scale, w_query, w_kv, w_out):
    slot_count = tile_mask.shape[0]
    block_rows = tile_mask.shape[1]
    total_rows = slot_count * block_rows
    half_rows = total_rows // 2
    layer_count = w_kv.shape[0]
    head_cols = w_kv.shape[3]
    heads_local = head_scale.shape[0]
    head_dim = head_cols // heads_local
    kv_side = lax.axis_index("kv")
    kv_weights = w_kv[:, :, 0, :]
    slot_ids = jnp.arange(slot_count, dtype=jnp.int32)

    def add_block(slot_at, current):
        block_feats = lax.dynamic_slice_in_dim(features, slot_at * block_rows, block_rows, 0)
        result = jnp.einsum(
            "rf,lfc->lrc", block_feats, kv_weights, preferred_element_type=jnp.float32
        )
        return lax.dynamic_update_slice_in_dim(
            current, result.astype(jnp.bfloat16), slot_at * block_rows, 1
        )

    own_count = counts[0]
    projected = jnp.zeros((layer_count, total_rows, head_cols), jnp.bfloat16)
    projected = lax.fori_loop(jnp.int32(0), own_count, add_block, projected)
    live_mask = tile_mask * (slot_ids < own_count).astype(jnp.int32)[:, None]
    kv_local = lax.all_to_all(projected, "kv", split_axis=1, concat_axis=2, tiled=True)
    valid_tiles = lax.dynamic_slice_in_dim(
        live_mask.reshape(total_rows).astype(jnp.float32), kv_side * half_rows, half_rows, 0
    )
    states = queries.astype(jnp.float32)
    scale_vec = head_scale / math.sqrt(head_dim)
    for layer_at in range(layer_count):
        normed = lax.all_gather(
            normalize(states, norm_gain[layer_at]).astype(jnp.bfloat16),
            ("heads", "kv"),
            axis=0,
            tiled=True,
        )
        query_part = jnp.dot(normed, w_query[layer_at], preferred_element_type=jnp.float32).astype(
            jnp.bfloat16
        )
        query_cols = lax.all_gather(query_part, "kv", axis=1, tiled=True)
        n_queries = query_cols.shape[0]
        query_heads = query_cols.reshape(n_queries, heads_local, head_dim)
        key_heads = kv_local[layer_at, :, :head_cols].reshape(half_rows, heads_local, head_dim)
        value_heads = kv_local[layer_at, :, head_cols:].reshape(half_rows, heads_local, head_dim)
        scores = jnp.einsum(
            "qhd,khd->hqk", query_heads, key_heads, preferred_element_type=jnp.float32
        )
        scores = scores * scale_vec[:, None, None]
        capped = SOFT_CAP * jnp.tanh(scores / SOFT_CAP)
        weights_p = jnp.exp(capped) * valid_tiles[None, None, :]
        totals = jnp.sum(weights_p, axis=2)
        partial_value = jnp.einsum(
            "hqk,khd->qhd",
            weights_p.astype(jnp.bfloat16),
            value_heads,
            preferred_element_type=jnp.float32,
        )
        totals, partial_value = lax.psum((totals, partial_value), ("tiles", "kv"))
        attended = (
            (partial_value / jnp.transpose(totals)[:, :, None])
            .reshape(n_queries, head_cols)
            .astype(jnp.bfloat16)
        )
        own_cols = lax.dynamic_slice_in_dim(attended, kv_side * (head_cols // 2), head_cols // 2, 1)
        states = states + lax.psum_scatter(
            jnp.dot(own_cols, w_out[layer_at], preferred_element_type=jnp.float32),
            ("heads", "kv"),
            scatter_dimension=0,
            tiled=True,
        )
    return states


class Plan:
    def __init__(self, mesh, queries, head_scale, w_kv):
        self.n_t, self.n_h, self.n_k = (mesh.shape[a] for a in ("tiles", "heads", "kv"))
        self.q_rows, self.dq = queries.shape
        self.n_q = self.q_rows * self.n_h * self.n_k
        self.cols = w_kv.shape[3]
        self.heads = head_scale.shape[0] // self.n_k
        self.head_dim = self.cols // head_scale.shape[0]
        self.half = self.heads * self.head_dim
        self.width = -(-self.half // LANES) * LANES
        self.start = [k * self.half // LANES * LANES for k in range(self.n_k)]
        self.off = [k * self.half - s for k, s in enumerate(self.start)]
        offsets = [(t, h) for t in range(self.n_t) for h in range(self.n_h)][1:]
        offsets = sorted(offsets, reverse=True)
        offsets += [None] * (-len(offsets) % self.n_k)
        self.rounds = [
            tuple(offsets[i + k] for k in range(self.n_k))
            for i in range(0, len(offsets), self.n_k)
        ]

    def usable(self):
        return (
            self.n_k == 2
            and self.n_h == 2
            and self.n_t == self.n_h * self.n_k
            and self.half * self.n_k == self.cols
            and self.cols % LANES == 0
            and self.q_rows % 16 == 0
            and self.off[0] == 0
            and all(s + self.width <= self.cols for s in self.start)
            and all(o == 0 or o + self.half == self.width for o in self.off)
            and self.width - self.half >= 2 * SPLIT
            and self.heads <= SPLIT
        )


def place():
    return lax.axis_index("tiles"), lax.axis_index("heads"), lax.axis_index("kv")


def rows_at(index, size):
    return pl.ds(pl.multiple_of(index * size, size), size)


def project_rows(plan, count_ref, mask_ref, feats, weights, own_ref, other_ref, low, high):
    first = lax.axis_index("kv") == 0
    rows = mask_ref.shape[1]
    lane = lax.broadcasted_iota(jnp.int32, (1, plan.width), 1)
    acc = jnp.dot(feats[low:high, :], weights[...], preferred_element_type=jnp.float32)
    for slot in range(low // rows, high // rows):
        marks = mask_ref[slot : slot + 1, :].astype(jnp.float32)
        marks = jnp.where(slot < count_ref[0], marks, 0.0)
        valid = jnp.broadcast_to(marks, (LANES, rows)).T
        valid = jnp.concatenate([valid] * (plan.width // LANES), axis=1)
        part = acc[slot * rows - low : slot * rows - low + rows]
        pieces = []
        for start, off in zip(plan.start, plan.off):
            inside = (lane >= off) & (lane < off + plan.half)
            block = part[:, start : start + plan.width]
            pieces.append(jnp.where(inside, block * valid, valid).astype(jnp.bfloat16))
        at = slice(slot * rows, slot * rows + rows)
        own_ref[at, :] = jnp.where(first, pieces[0], pieces[1])
        other_ref[at, :] = jnp.where(first, pieces[1], pieces[0])


def group_of(mask_ref):
    slots, rows = mask_ref.shape
    return rows * (2 if slots % 2 == 0 else 1)


def load_project_kernel(
    plan,
    count_ref,
    mask_ref,
    feats_hbm,
    weights_hbm,
    own_ref,
    other_ref,
    feats_ref,
    later_ref,
    weights_ref,
    sems,
):
    size = group_of(mask_ref)
    groups = feats_ref.shape[0] // size
    copies = [pltpu.make_async_copy(weights_hbm.at[0], weights_ref, sems.at[groups])]
    for index in range(groups):
        at = pl.ds(index * size, size)
        copies.append(
            pltpu.make_async_copy(feats_hbm.at[at], feats_ref.at[at], sems.at[index])
        )
    copies.append(pltpu.make_async_copy(weights_hbm.at[1], later_ref, sems.at[groups + 1]))
    for copy in copies:
        copy.start()
    copies[0].wait()
    for index in range(groups):
        copies[1 + index].wait()
        low = index * size
        project_rows(
            plan, count_ref, mask_ref, feats_ref, weights_ref, own_ref, other_ref, low, low + size
        )
    copies[-1].wait()


def project_kernel(plan, count_ref, mask_ref, feats_ref, weights_ref, own_ref, other_ref):
    size = group_of(mask_ref)
    for low in range(0, feats_ref.shape[0], size):
        project_rows(
            plan, count_ref, mask_ref, feats_ref, weights_ref, own_ref, other_ref, low, low + size
        )


def attend(plan, query, scale_ref, own_ref, recv_ref, chunk_refs, mix):
    me_t, _, side = place()
    first = side == 0
    off = jnp.where(first, plan.off[0], plan.off[1])
    pad = jnp.where(first, plan.half if plan.off[0] == 0 else 0, plan.half if plan.off[1] == 0 else 0)
    lane = lax.broadcasted_iota(jnp.int32, (1, plan.width), 1)
    factor = SOFT_CAP * math.log2(math.e)
    n_keys = own_ref.shape[0]
    block = min(n_keys, 512)
    masked, scales, totals = [], [], []
    for head in range(plan.heads):
        low = off + head * plan.head_dim
        masked.append(
            jnp.where((lane >= low) & (lane < low + plan.head_dim), query, jnp.zeros_like(query))
        )
        scales.append(
            scale_ref[side * plan.heads + head] * (1.0 / (SOFT_CAP * math.sqrt(plan.head_dim)))
        )
        totals.append(None)
    for at in range(0, n_keys, block):
        mine = own_ref[at : at + block, :]
        theirs = recv_ref[at : at + block, :]
        keys = jnp.where(first, mine, theirs)
        values = jnp.where(first, theirs, mine)
        for head in range(plan.heads):
            scores = lax.dot_general(
                masked[head], keys, (((1,), (1,)), ((), ())), preferred_element_type=jnp.float32
            )
            weight = jnp.exp2(jnp.tanh(scores * scales[head]) * factor)
            part = jnp.dot(
                weight.astype(jnp.bfloat16), values, preferred_element_type=jnp.float32
            )
            totals[head] = part if totals[head] is None else totals[head] + part
    result = jnp.zeros((plan.n_q, plan.width), jnp.float32)
    spot = lane - pad
    spare = (spot >= 0) & (spot < 2 * SPLIT)
    for head in range(plan.heads):
        low = off + head * plan.head_dim
        keep = (lane >= low) & (lane < low + plan.head_dim)
        keep = keep | (spare & (jnp.bitwise_and(spot, SPLIT - 1) == head))
        result = jnp.where(keep, totals[head], result)
    rounded = result.astype(jnp.bfloat16).astype(jnp.float32)
    late = spare & (spot >= SPLIT)
    mix[...] = jnp.where(late, result - rounded, rounded)
    for index, ref in enumerate(chunk_refs):
        rows = plan.n_q // plan.n_t
        ref[...] = mix[rows_at(jnp.bitwise_xor(me_t, index), rows), :].astype(ref.dtype)


def query_of(plan, states, gain, wq, wq_pad):
    side = lax.axis_index("kv")
    mean = jnp.mean(states * states, axis=-1, keepdims=True)
    normed = (states * lax.rsqrt(mean + NORM_EPS) * gain).astype(jnp.bfloat16)
    wq_pad[...] = jnp.zeros_like(wq_pad)
    step = max(plan.off)
    wq_pad[pl.ds(pl.multiple_of(side * step, step), plan.half), :] = wq
    return lax.dot_general(
        normed, wq_pad[...], (((1,), (1,)), ((), ())), preferred_element_type=jnp.float32
    ).astype(jnp.bfloat16)


def first_kernel(
    plan, scale_ref, q_ref, qk_ref, qx_ref, qxk_ref, gain_ref, wq_ref, own_ref, recv_ref, *rest
):
    chunks, (all_ref, wq_pad, mix) = rest[: plan.n_t], rest[plan.n_t :]
    _, me_h, me_k = place()
    for dh, row in enumerate(((q_ref, qk_ref), (qx_ref, qxk_ref))):
        for dk, ref in enumerate(row):
            index = jnp.bitwise_xor(me_h, dh) * plan.n_k + jnp.bitwise_xor(me_k, dk)
            all_ref[rows_at(index, plan.q_rows), :] = ref[...]
    states = all_ref[...].astype(jnp.float32)
    query = query_of(plan, states, gain_ref[0:1, :], wq_ref[0], wq_pad)
    attend(plan, query, scale_ref, own_ref, recv_ref, chunks, mix)


def fill_out(plan, layer, wo_refs, wo_all):
    me_k = lax.axis_index("kv")
    for dh in range(plan.n_h):
        for dk in range(plan.n_k):
            index = dh * plan.n_k + jnp.bitwise_xor(me_k, dk)
            wo_all[rows_at(index, plan.half), :] = wo_refs[dh * plan.n_k + dk][layer]


def layer_kernel(
    plan,
    layer,
    scale_ref,
    all_ref,
    block_ref,
    near_ref,
    far_ref,
    wo0,
    wo1,
    wo2,
    wo3,
    gain_ref,
    wq_ref,
    own_ref,
    recv_ref,
    *rest,
):
    chunks, (kept_ref, att, wo_all, states_ref, wq_pad, mix) = rest[: plan.n_t], rest[plan.n_t :]
    me_t, me_h, me_k = place()
    rows = plan.n_q // plan.n_t
    fill_out(plan, layer - 1, (wo0, wo1, wo2, wo3), wo_all)
    for index, pair in enumerate(plan.rounds):
        for ref, flip in ((near_ref, 0), (far_ref, 1)):
            choice = [pair[k ^ flip] or (0, 0) for k in range(2)]
            dt = jnp.where(me_k == 0, choice[0][0], choice[1][0])
            dh = jnp.where(me_k == 0, choice[0][1], choice[1][1])
            att[dh, rows_at(jnp.bitwise_xor(me_t, dt), rows), :] = ref[
                index * rows : index * rows + rows, :
            ]
    att[0, rows_at(me_t, rows), :] = block_ref[...]
    out = jnp.dot(att[0], wo_all[: plan.cols, :], preferred_element_type=jnp.float32)
    out = out + jnp.dot(att[1], wo_all[plan.cols :, :], preferred_element_type=jnp.float32)
    states = all_ref[...].astype(jnp.float32) + out
    states_ref[...] = states
    kept_ref[...] = states_ref[rows_at(me_h * plan.n_k + me_k, plan.q_rows), :]
    query = query_of(plan, states, gain_ref[layer : layer + 1, :], wq_ref[layer], wq_pad)
    attend(plan, query, scale_ref, own_ref, recv_ref, chunks, mix)


def last_kernel(plan, layer, kept_ref, near_ref, far_ref, wo0, wo1, wo2, wo3, out_ref, att, wo_all):
    me_t = lax.axis_index("tiles")
    fill_out(plan, layer, (wo0, wo1, wo2, wo3), wo_all)
    for index, ref in enumerate((near_ref, far_ref)):
        att[(me_t + index) % plan.n_h] = ref[...]
    out = jnp.dot(att[0], wo_all[: plan.cols, :], preferred_element_type=jnp.float32)
    out = out + jnp.dot(att[1], wo_all[plan.cols :, :], preferred_element_type=jnp.float32)
    out_ref[...] = kept_ref[...] + out


def combine_kernel(plan, *refs):
    *parts, out_ref = refs
    side = lax.axis_index("kv")
    first = side == 0
    off = jnp.where(first, plan.off[0], plan.off[1])
    pad = jnp.where(first, plan.half if plan.off[0] == 0 else 0, plan.half if plan.off[1] == 0 else 0)
    lane = lax.broadcasted_iota(jnp.int32, (1, plan.width), 1)
    spot = lane - pad
    spare = (spot >= 0) & (spot < 2 * SPLIT)
    total = sum(ref[...].astype(jnp.float32) for ref in parts)
    below = jnp.ones_like(total)
    for head in range(plan.heads):
        low = off + head * plan.head_dim
        mine = spare & (jnp.bitwise_and(spot, SPLIT - 1) == head)
        weight = jnp.sum(jnp.where(mine, total, 0.0), axis=1, keepdims=True)
        below = jnp.where((lane >= low) & (lane < low + plan.head_dim), weight, below)
    out_ref[...] = (total / below).astype(jnp.bfloat16)


def vmem_call(kernel, out_shape, scalars, arrays, scratch, flops, far=(), sems=0):
    specs = [pl.BlockSpec(memory_space=pltpu.SMEM)] * len(scalars)
    specs += [pl.BlockSpec(memory_space=pltpu.VMEM)] * len(arrays)
    specs += [pl.BlockSpec(memory_space=pltpu.HBM)] * len(far)
    held = [*arrays, *jax.tree.leaves(out_shape), *scratch]
    scratch = scratch + ([pltpu.SemaphoreType.DMA((sems,))] if sems else [])
    grant = sum(math.prod(a.shape) * jnp.dtype(a.dtype).itemsize for a in held) + ROOM
    return pl.pallas_call(
        kernel,
        out_shape=out_shape,
        in_specs=specs,
        out_specs=jax.tree.map(lambda _: pl.BlockSpec(memory_space=pltpu.VMEM), out_shape),
        scratch_shapes=scratch,
        cost_estimate=pl.CostEstimate(flops=flops, bytes_accessed=1 << 20, transcendentals=0),
        compiler_params=pltpu.CompilerParams(vmem_limit_bytes=grant),
    )(*scalars, *arrays, *far)


def fast_body(plan, features, counts, tile_mask, queries, norm_gain, head_scale, w_query, w_kv, w_out):
    layer_count = w_kv.shape[0]
    rows = plan.n_q // plan.n_t
    axes = ("tiles", "heads", "kv")
    devices = [
        (t, h, k) for t in range(plan.n_t) for h in range(plan.n_h) for k in range(plan.n_k)
    ]
    side = lax.axis_index("kv")

    def number(t, h, k):
        return (t * plan.n_h + h) * plan.n_k + k

    def swap(value, axis):
        size = {"heads": plan.n_h, "kv": plan.n_k}[axis]
        return lax.ppermute(value, axis, [(i, i ^ 1) for i in range(size)])

    def exchange(chunks):
        received = []
        for d in range(plan.n_t - 1, 0, -1):
            received.append(lax.ppermute(chunks[d], "tiles", [(i, i ^ d) for i in range(plan.n_t)]))
        shape = jax.ShapeDtypeStruct((rows, plan.width), jnp.bfloat16)
        attended = vmem_call(
            functools.partial(combine_kernel, plan), shape, [], [chunks[0], *received], [], 1 << 20
        )
        partner = swap(attended, "kv")
        low = jnp.where(side == 0, attended, partner)
        high = jnp.where(side == 0, partner, attended)
        lead = plan.start[1]
        overlap = jnp.where(
            lax.broadcasted_iota(jnp.int32, (1, plan.width - lead), 1) < plan.half - lead,
            low[:, lead:],
            high[:, : plan.width - lead],
        )
        return jnp.concatenate([low[:, :lead], overlap, high[:, plan.width - lead :]], axis=1)

    def spread(block):
        received = []
        for pair in plan.rounds:
            links = [
                (number(t, h, k), number(t ^ pair[k][0], h ^ pair[k][1], k))
                for t, h, k in devices
                if pair[k] is not None
            ]
            received.append(lax.ppermute(block, axes, links))
        near = jnp.concatenate(received, axis=0)
        return near, swap(near, "kv")

    def collect(block):
        received = []
        for turn in range(plan.n_h):
            links = []
            for t, h, k in devices:
                source_t, source_h = h * plan.n_k + k, h ^ ((turn + t) % plan.n_h)
                links.append((number(source_t, source_h, (t // plan.n_h) % plan.n_k), number(t, h, k)))
            received.append(lax.ppermute(block, axes, links))
        return received

    weights = w_kv.reshape(layer_count, w_kv.shape[1], plan.cols)
    wq = jnp.swapaxes(w_query, 1, 2)
    q_x = swap(queries, "heads")
    q_k = swap(queries, "kv")
    q_xk = swap(q_x, "kv")
    tied, _ = lax.optimization_barrier((w_out, q_x))
    wo_x = swap(tied, "heads")
    wo = [w_out, swap(w_out, "kv"), wo_x, swap(wo_x, "kv")]
    tiles = features.shape[0]
    bf16, f32 = jnp.bfloat16, jnp.float32
    feat = features.shape[1]
    piece = jax.ShapeDtypeStruct((tiles, plan.width), bf16)
    cost = 2 * tiles * feat * plan.cols
    own, other, near_tiles, later = vmem_call(
        functools.partial(load_project_kernel, plan),
        [
            piece,
            piece,
            jax.ShapeDtypeStruct((tiles, feat), bf16),
            jax.ShapeDtypeStruct((feat, plan.cols), bf16),
        ],
        [counts],
        [tile_mask],
        [pltpu.VMEM((feat, plan.cols), bf16)],
        cost,
        tuple(pltpu.with_memory_space_constraint(a, pltpu.HBM) for a in (features, weights)),
        tile_mask.shape[0] + 2,
    )
    pairs = [(own, swap(other, "kv"))]
    own, other = vmem_call(
        functools.partial(project_kernel, plan),
        [piece, piece],
        [counts],
        [tile_mask, near_tiles, later],
        [],
        cost,
    )
    pairs.append((own, swap(other, "kv")))
    chunk_shapes = [jax.ShapeDtypeStruct((rows, plan.width), f32)]
    chunk_shapes += [jax.ShapeDtypeStruct((rows, plan.width), bf16)] * (plan.n_t - 1)
    wq_scratch = pltpu.VMEM((plan.width, plan.dq), bf16)
    mix_scratch = pltpu.VMEM((plan.n_q, plan.width), f32)
    wo_scratch = pltpu.VMEM((plan.n_h * plan.cols, plan.dq), bf16)

    work = 4 * plan.n_q * tiles * plan.width
    outs = vmem_call(
        functools.partial(first_kernel, plan),
        chunk_shapes + [jax.ShapeDtypeStruct((plan.n_q, plan.dq), bf16)],
        [head_scale],
        [queries, q_k, q_x, q_xk, norm_gain, wq, *pairs[0]],
        [wq_scratch, mix_scratch],
        work,
    )
    chunks, states = outs[: plan.n_t], outs[plan.n_t]
    block = exchange(chunks)
    near, far = spread(block)
    outs = vmem_call(
        functools.partial(layer_kernel, plan, 1),
        chunk_shapes + [jax.ShapeDtypeStruct((plan.q_rows, plan.dq), f32)],
        [head_scale],
        [states, block, near, far, *wo, norm_gain, wq, *pairs[1]],
        [
            pltpu.VMEM((plan.n_h, plan.n_q, plan.cols), bf16),
            wo_scratch,
            pltpu.VMEM((plan.n_q, plan.dq), f32),
            wq_scratch,
            mix_scratch,
        ],
        work,
    )
    chunks, kept = outs[: plan.n_t], outs[plan.n_t]
    block = exchange(chunks)
    near, far = collect(block)
    return vmem_call(
        functools.partial(last_kernel, plan, 1),
        jax.ShapeDtypeStruct((plan.q_rows, plan.dq), f32),
        [],
        [kept, near, far, *wo],
        [pltpu.VMEM((plan.n_h, plan.q_rows, plan.cols), bf16), wo_scratch],
        2 * plan.q_rows * plan.dq * plan.dq,
    )


def solution(mesh):
    def body(features, counts, tile_mask, queries, norm_gain, head_scale, w_query, w_kv, w_out):
        args = (features, counts, tile_mask, queries, norm_gain, head_scale, w_query, w_kv, w_out)
        plan = Plan(mesh, queries, head_scale, w_kv)
        if w_kv.shape[0] == 2 and plan.usable():
            return fast_body(plan, *args)
        return generic_body(*args)

    return jax.shard_map(
        body,
        mesh=mesh,
        in_specs=(
            P(("groups", "tiles"), None),
            P(("groups", "tiles")),
            P(("groups", "tiles"), None),
            P(("heads", "kv"), None),
            P(),
            P("heads"),
            P(None, None, ("heads", "kv")),
            P(None, None, "kv", "heads"),
            P(None, ("heads", "kv"), None),
        ),
        out_specs=P(("groups", "heads", "kv"), None),
        check_vma=False,
    )
```

profile of v0, /device:TPU:7, one launch (start us, length us, event | category | flops | bytes accessed | tf_op | source)
XLA Modules:
  0.0 81.3 jit_solution(10910135495672682352)
XLA Ops:
  0.0 0.0 copy-start.2
  0.0 0.0 copy-start
  0.7 0.0 copy-start.4
  0.7 0.7 copy-done.4
  1.4 4.8 %shard_map.91 = (bf16[1536,256]{1,0:T(8,128)(2,1)S(1)}, bf16[1536,256]{1,0:T(8,128)(2,1)S(1)}, bf16[1536,1536]{1,0:T(8,128)(2,1)S(1)}, bf16[1536,384]{1,0:T(8,128)(2,1)S(1)}) custom-call(s32[1]{0:T(128)S(6)} %copy.13.count_ref, s32[6,256]{1,0:T(8,128)S(1)} %copy-done.4, bf16[1536,1536]{1,0:T(8,128)(2,1)} %feats_hbm.1, bf16[2,1536,384]{2,1,0:T(8,128)(2,1)} %bitcast.4), custom_call_target="tpu_custom_call" | custom-call | flops 1811939328 | bytes 1048576 | tf_op jit(solution)/shard_map/pallas_call | solution.py:372
  6.2 0.7 collective-permute-start.3
  7.0 0.0 copy-done.2
  7.0 0.3 collective-permute-start.1
  7.2 0.4 collective-permute-start
  7.6 3.6 %collective-permute-done.1.qx_ref = bf16[64,768]{1,0:T(8,128)(2,1)S(1)} collective-permute-done((bf16[64,768]{1,0:T(8,128)(2,1)S(1)}, bf16[64,768]{1,0:T(8,128)(2,1)S(1)}, u32[]{:S(2)}, u32[]{:S(2)}) %collective-permute-start.1) | collective-permute-done | bytes 98336 | tf_op jit(solution)/shard_map/ppermute | solution.py:397
  11.3 0.9 %collective-permute-start.2 = (bf16[64,768]{1,0:T(8,128)(2,1)S(1)}, bf16[64,768]{1,0:T(8,128)(2,1)S(1)}, u32[]{:S(2)}, u32[]{:S(2)}) collective-permute-start(bf16[64,768]{1,0:T(8,128)(2,1)S(1)} %collective-permute-done.1.qx_ref), channel_id=1, source_target_pairs={{0,1},{1,0},{2,3},{3,2},{4,5},{5,4},{6,7},{7,6},{8,9},{9,8},{10,11... | collective-permute-start | bytes 294920 | tf_op jit(solution)/shard_map/ppermute | solution.py:397
  12.2 0.0 collective-permute-done.qk_ref
  12.2 0.9 %collective-permute-done.2.qxk_ref = bf16[64,768]{1,0:T(8,128)(2,1)S(1)} collective-permute-done((bf16[64,768]{1,0:T(8,128)(2,1)S(1)}, bf16[64,768]{1,0:T(8,128)(2,1)S(1)}, u32[]{:S(2)}, u32[]{:S(2)}) %collective-permute-start.2) | collective-permute-done | bytes 98336 | tf_op jit(solution)/shard_map/ppermute | solution.py:397
  13.1 0.0 collective-permute-done.3.recv_ref
  13.1 0.0 copy-done
  13.2 0.0 copy-done.3
  13.2 0.0 copy-done.6
  13.2 0.0 copy-start.1
  13.2 3.0 %shard_map.92 = (f32[64,256]{1,0:T(8,128)S(1)}, bf16[64,256]{1,0:T(8,128)(2,1)S(1)}, bf16[64,256]{1,0:T(8,128)(2,1)S(1)}, bf16[64,256]{1,0:T(8,128)(2,1)S(1)}, bf16[256,768]{1,0:T(8,128)(2,1)S(1)}) custom-call(f32[6]{0:T(128)S(1)} %copy-done.6, bf16[64,768]{1,0:T(8,128)(2,1)S(1)} %copy-done.2, bf16[64,768]{1,0:T(8,128)(2,1)S(1)} %collective-permute-done.qk_ref, ...), custom_call_target="tpu_custom_call" | custom-call | flops 402653184 | bytes 1048576 | tf_op jit(solution)/shard_map/pallas_call | solution.py:372
  16.2 3.4 %collective-permute-start.4 = (bf16[64,256]{1,0:T(8,128)(2,1)S(1)}, bf16[64,256]{1,0:T(8,128)(2,1)S(1)}, u32[]{:S(2)}, u32[]{:S(2)}) collective-permute-start(bf16[64,256]{1,0:T(8,128)(2,1)S(1)} %get-tuple-element.26), channel_id=1, source_target_pairs={{0,12},{4,8},{8,4},{12,0},{1,13},{5,9},{9,5},{13,1},{2,14},{6,10},... | collective-permute-start | bytes 98312 | tf_op jit(solution)/shard_map/ppermute | solution.py:402
  19.6 0.0 collective-permute-start.5
  19.6 0.4 collective-permute-start.6
  20.0 0.0 copy-done.5
  20.0 3.5 %shard_map.94 = (bf16[1536,256]{1,0:T(8,128)(2,1)S(1)}, bf16[1536,256]{1,0:T(8,128)(2,1)}) custom-call(s32[1]{0:T(128)S(6)} %copy.13.count_ref, s32[6,256]{1,0:T(8,128)S(1)} %copy-done.5, bf16[1536,1536]{1,0:T(8,128)(2,1)S(1)} %get-tuple-element.30.feats_ref, bf16[1536,384]{1,0:T(8,128)(2,1)S(1)} %get-tuple-element.31.weights_ref), custom_call_target="tpu_custom_call" | custom-call | flops 1811939328 | bytes 1048576 | tf_op jit(solution)/shard_map/pallas_call | solution.py:372
  23.5 1.1 %collective-permute-start.16 = (bf16[1536,256]{1,0:T(8,128)(2,1)}, bf16[1536,256]{1,0:T(8,128)(2,1)S(1)}, u32[]{:S(2)}, u32[]{:S(2)}) collective-permute-start(bf16[1536,256]{1,0:T(8,128)(2,1)} %get-tuple-element.33), channel_id=1, source_target_pairs={{0,1},{1,0},{2,3},{3,2},{4,5},{5,4},{6,7},{7,6},{8,9},{9,8},{10,11... | collective-permute-start | bytes 2359304 | tf_op jit(solution)/shard_map/ppermute | solution.py:397
  24.5 0.0 collective-permute-done.4.refs_1_
  24.5 0.0 collective-permute-done.5.refs_2_
  24.5 0.0 collective-permute-done.6.refs_3_
  24.5 0.1 shard_map.93
  24.7 0.6 collective-permute-start.7
  25.3 0.0 copy-done.1
  25.3 0.3 collective-permute-start.14
  25.5 1.2 %collective-permute-done.7 = bf16[64,256]{1,0:T(8,128)(2,1)S(1)} collective-permute-done((bf16[64,256]{1,0:T(8,128)(2,1)S(1)}, bf16[64,256]{1,0:T(8,128)(2,1)S(1)}, u32[]{:S(2)}, u32[]{:S(2)}) %collective-permute-start.7) | collective-permute-done | bytes 32800 | tf_op jit(solution)/shard_map/ppermute | solution.py:397
  26.7 3.4 %collective-permute-start.8 = (bf16[64,384]{1,0:T(8,128)(2,1)S(1)}, bf16[64,384]{1,0:T(8,128)(2,1)S(1)}, u32[]{:S(2)}, u32[]{:S(2)}) collective-permute-start(bf16[64,384]{1,0:T(8,128)(2,1)S(1)} %pad_maximum_fusion.block_ref), channel_id=1, source_target_pairs={{0,14},{1,13},{2,12},{3,15},{4,10},{5,9},{6,8},{7,11},{8,6},{9,5},... | collective-permute-start | bytes 147464 | tf_op jit(solution)/shard_map/ppermute | solution.py:426
  30.1 0.6 collective-permute-start.13
  30.8 9.8 %collective-permute-done.14.wo2 = bf16[2,192,768]{2,1,0:T(8,128)(2,1)S(1)} collective-permute-done((bf16[2,192,768]{2,1,0:T(8,128)(2,1)S(1)}, bf16[2,192,768]{2,1,0:T(8,128)(2,1)S(1)}, u32[]{:S(2)}, u32[]{:S(2)}) %collective-permute-start.14) | collective-permute-done | bytes 589856 | tf_op jit(solution)/shard_map/ppermute | solution.py:397
  40.6 1.0 %collective-permute-start.15 = (bf16[2,192,768]{2,1,0:T(8,128)(2,1)S(1)}, bf16[2,192,768]{2,1,0:T(8,128)(2,1)S(1)}, u32[]{:S(2)}, u32[]{:S(2)}) collective-permute-start(bf16[2,192,768]{2,1,0:T(8,128)(2,1)S(1)} %collective-permute-done.14.wo2), channel_id=1, source_target_pairs={{0,1},{1,0},{2,3},{3,2},{4,5},{5,4},{6,7},{7,6},{8,9},{9,8},{10,11... | collective-permute-start | bytes 1769480 | tf_op jit(solution)/shard_map/ppermute | solution.py:397
  41.5 1.7 %collective-permute-start.9 = (bf16[64,384]{1,0:T(8,128)(2,1)S(1)}, bf16[64,384]{1,0:T(8,128)(2,1)S(1)}, u32[]{:S(2)}, u32[]{:S(2)}) collective-permute-start(bf16[64,384]{1,0:T(8,128)(2,1)S(1)} %pad_maximum_fusion.block_ref), channel_id=1, source_target_pairs={{0,10},{1,9},{2,8},{3,11},{4,14},{5,13},{6,12},{7,15},{8,2},{9,1},... | collective-permute-start | bytes 147464 | tf_op jit(solution)/shard_map/ppermute | solution.py:426
  43.3 0.0 collective-permute-done.8
  43.3 1.4 %collective-permute-start.10 = (bf16[64,384]{1,0:T(8,128)(2,1)S(1)}, bf16[64,384]{1,0:T(8,128)(2,1)S(1)}, u32[]{:S(2)}, u32[]{:S(2)}) collective-permute-start(bf16[64,384]{1,0:T(8,128)(2,1)S(1)} %pad_maximum_fusion.block_ref), channel_id=1, source_target_pairs={{0,6},{1,5},{2,4},{3,7},{4,2},{5,1},{6,0},{7,3},{8,14},{9,13},{10,... | collective-permute-start | bytes 147464 | tf_op jit(solution)/shard_map/ppermute | solution.py:426
  44.7 0.8 collective-permute-done.9
  45.5 0.7 collective-permute-start.11
  46.2 0.4 collective-permute-done.10
  46.5 0.0 collective-permute-done.11
  46.6 7.4 %collective-permute-start.12 = (bf16[256,384]{1,0:T(8,128)(2,1)S(1)}, bf16[256,384]{1,0:T(8,128)(2,1)S(1)}, u32[]{:S(2)}, u32[]{:S(2)}) collective-permute-start(bf16[256,384]{1,0:T(8,128)(2,1)S(1)} %constant_dynamic-update-slice_fusion.near_ref), channel_id=1, source_target_pairs={{0,1},{1,0},{2,3},{3,2},{4,5},{5,4},{6,7},{7,6},{8,9},{9,8},{10,11... | collective-permute-start | bytes 589832 | tf_op jit(solution)/shard_map/ppermute | solution.py:397
  54.0 0.0 collective-permute-done.13.wo1
  54.0 0.0 collective-permute-done.16.recv_ref
  54.0 1.1 %collective-permute-done.12.far_ref = bf16[256,384]{1,0:T(8,128)(2,1)S(1)} collective-permute-done((bf16[256,384]{1,0:T(8,128)(2,1)S(1)}, bf16[256,384]{1,0:T(8,128)(2,1)S(1)}, u32[]{:S(2)}, u32[]{:S(2)}) %collective-permute-start.12) | collective-permute-done | bytes 196640 | tf_op jit(solution)/shard_map/ppermute | solution.py:397
  55.1 0.0 collective-permute-done.15.wo3
  55.1 3.6 %shard_map.95 = (f32[64,256]{1,0:T(8,128)S(1)}, bf16[64,256]{1,0:T(8,128)(2,1)S(1)}, bf16[64,256]{1,0:T(8,128)(2,1)S(1)}, bf16[64,256]{1,0:T(8,128)(2,1)S(1)}, f32[64,768]{1,0:T(8,128)S(1)}) custom-call(f32[6]{0:T(128)S(1)} %copy-done.6, bf16[256,768]{1,0:T(8,128)(2,1)S(1)} %get-tuple-element.24.all_ref, bf16[64,384]{1,0:T(8,128)(2,1)S(1)} %pad_maximum_fusion.block_ref, ...), custom_call_target="tpu_custom_call" | custom-call | flops 402653184 | bytes 1048576 | tf_op jit(solution)/shard_map/pallas_call | solution.py:372
  58.7 2.8 %collective-permute-start.17 = (bf16[64,256]{1,0:T(8,128)(2,1)S(1)}, bf16[64,256]{1,0:T(8,128)(2,1)S(1)}, u32[]{:S(2)}, u32[]{:S(2)}) collective-permute-start(bf16[64,256]{1,0:T(8,128)(2,1)S(1)} %get-tuple-element.36), channel_id=1, source_target_pairs={{0,12},{4,8},{8,4},{12,0},{1,13},{5,9},{9,5},{13,1},{2,14},{6,10},... | collective-permute-start | bytes 98312 | tf_op jit(solution)/shard_map/ppermute | solution.py:402
  61.5 0.0 collective-permute-start.18
  61.5 0.8 collective-permute-start.19
  62.3 1.0 %collective-permute-done.17.refs_1_ = bf16[64,256]{1,0:T(8,128)(2,1)S(1)} collective-permute-done((bf16[64,256]{1,0:T(8,128)(2,1)S(1)}, bf16[64,256]{1,0:T(8,128)(2,1)S(1)}, u32[]{:S(2)}, u32[]{:S(2)}) %collective-permute-start.17) | collective-permute-done | bytes 32800 | tf_op jit(solution)/shard_map/ppermute | solution.py:402
  63.3 2.2 %collective-permute-done.18.refs_2_ = bf16[64,256]{1,0:T(8,128)(2,1)S(1)} collective-permute-done((bf16[64,256]{1,0:T(8,128)(2,1)S(1)}, bf16[64,256]{1,0:T(8,128)(2,1)S(1)}, u32[]{:S(2)}, u32[]{:S(2)}) %collective-permute-start.18) | collective-permute-done | bytes 32800 | tf_op jit(solution)/shard_map/ppermute | solution.py:402
  65.6 0.0 collective-permute-done.19.refs_3_
  65.6 0.1 shard_map.96
  65.7 1.5 %collective-permute-start.20 = (bf16[64,256]{1,0:T(8,128)(2,1)S(1)}, bf16[64,256]{1,0:T(8,128)(2,1)S(1)}, u32[]{:S(2)}, u32[]{:S(2)}) collective-permute-start(bf16[64,256]{1,0:T(8,128)(2,1)S(1)} %shard_map.96), channel_id=1, source_target_pairs={{0,1},{1,0},{2,3},{3,2},{4,5},{5,4},{6,7},{7,6},{8,9},{9,8},{10,11... | collective-permute-start | bytes 98312 | tf_op jit(solution)/shard_map/ppermute | solution.py:397
  67.2 0.9 %collective-permute-done.20 = bf16[64,256]{1,0:T(8,128)(2,1)S(1)} collective-permute-done((bf16[64,256]{1,0:T(8,128)(2,1)S(1)}, bf16[64,256]{1,0:T(8,128)(2,1)S(1)}, u32[]{:S(2)}, u32[]{:S(2)}) %collective-permute-start.20) | collective-permute-done | bytes 32800 | tf_op jit(solution)/shard_map/ppermute | solution.py:397
  68.1 4.0 %collective-permute-start.21 = (bf16[64,384]{1,0:T(8,128)(2,1)S(1)}, bf16[64,384]{1,0:T(8,128)(2,1)S(1)}, u32[]{:S(2)}, u32[]{:S(2)}) collective-permute-start(bf16[64,384]{1,0:T(8,128)(2,1)S(1)} %pad_maximum_fusion.1), channel_id=1, source_target_pairs={{0,0},{4,1},{10,2},{14,3},{2,4},{6,5},{8,6},{12,7},{1,8},{5,9},{11... | collective-permute-start | bytes 147464 | tf_op jit(solution)/shard_map/ppermute | solution.py:437
  72.1 2.6 %collective-permute-start.22 = (bf16[64,384]{1,0:T(8,128)(2,1)S(1)}, bf16[64,384]{1,0:T(8,128)(2,1)S(1)}, u32[]{:S(2)}, u32[]{:S(2)}) collective-permute-start(bf16[64,384]{1,0:T(8,128)(2,1)S(1)} %pad_maximum_fusion.1), channel_id=1, source_target_pairs={{2,0},{6,1},{8,2},{12,3},{0,4},{4,5},{10,6},{14,7},{3,8},{7,9},{9,... | collective-permute-start | bytes 147464 | tf_op jit(solution)/shard_map/ppermute | solution.py:437
  74.7 0.6 collective-permute-done.21.near_ref
  75.3 4.9 %collective-permute-done.22.far_ref = bf16[64,384]{1,0:T(8,128)(2,1)S(1)} collective-permute-done((bf16[64,384]{1,0:T(8,128)(2,1)S(1)}, bf16[64,384]{1,0:T(8,128)(2,1)S(1)}, u32[]{:S(2)}, u32[]{:S(2)}) %collective-permute-start.22) | collective-permute-done | bytes 49184 | tf_op jit(solution)/shard_map/ppermute | solution.py:437
  80.2 1.1 %shard_map.97 = f32[64,768]{1,0:T(8,128)} custom-call(f32[64,768]{1,0:T(8,128)S(1)} %get-tuple-element.34.kept_ref, bf16[64,384]{1,0:T(8,128)(2,1)S(1)} %collective-permute-done.21.near_ref, bf16[64,384]{1,0:T(8,128)(2,1)S(1)} %collective-permute-done.22.far_ref, bf16[2,192,768]{2,1,0:T(8,128)(2,1)S(1)} %copy-done.1, ...), custom_call_target="tpu_custom_call" | custom-call | flops 75497472 | bytes 1048576 | tf_op jit(solution)/shard_map/pallas_call | solution.py:372
  (14 shorter events, 0.1 us)
Async XLA Ops:
  0.0 7.0 %copy-start.2 = (bf16[64,768]{1,0:T(8,128)(2,1)S(1)}, bf16[64,768]{1,0:T(8,128)(2,1)}, u32[]{:S(2)}) copy-start(bf16[64,768]{1,0:T(8,128)(2,1)} %q_ref.1) | copy-start | bytes 294916
  0.0 13.1 %copy-start = (bf16[2,768,192]{1,2,0:T(8,128)(2,1)S(1)}, bf16[2,768,192]{1,2,0:T(8,128)(2,1)}, u32[]{:S(2)}) copy-start(bf16[2,768,192]{1,2,0:T(8,128)(2,1)} %param.15) | copy-start | bytes 1769476
  0.0 13.1 %copy-start.3 = (f32[2,768]{1,0:T(2,128)S(1)}, f32[2,768]{1,0:T(2,128)}, u32[]{:S(2)}) copy-start(f32[2,768]{1,0:T(2,128)} %gain_ref.3) | copy-start | bytes 18436
  0.7 0.7 copy-start.4
  1.4 11.7 %copy-start.6 = (f32[6]{0:T(128)S(1)}, f32[6]{0:T(128)}, u32[]{:S(2)}) copy-start(f32[6]{0:T(128)} %scale_ref.3) | copy-start | bytes 76
  1.4 18.5 %copy-start.5 = (s32[6,256]{1,0:T(8,128)S(1)}, s32[6,256]{1,0:T(8,128)}, u32[]{:S(2)}) copy-start(s32[6,256]{1,0:T(8,128)} %mask_ref.3) | copy-start | bytes 18436
  6.2 6.9 %collective-permute-start.3 = (bf16[1536,256]{1,0:T(8,128)(2,1)S(1)}, bf16[1536,256]{1,0:T(8,128)(2,1)S(1)}, u32[]{:S(2)}, u32[]{:S(2)}) collective-permute-start(bf16[1536,256]{1,0:T(8,128)(2,1)S(1)} %get-tuple-element.23), channel_id=1, source_target_pairs={{0,1},{1,0},{2,3},{3,2},{4,5},{5,4},{6,7},{7,6},{8,9},{9,8},{10,11... | collective-permute-start | bytes 2359304 | tf_op jit(solution)/shard_map/ppermute | solution.py:397
  7.0 4.3 %collective-permute-start.1 = (bf16[64,768]{1,0:T(8,128)(2,1)S(1)}, bf16[64,768]{1,0:T(8,128)(2,1)S(1)}, u32[]{:S(2)}, u32[]{:S(2)}) collective-permute-start(bf16[64,768]{1,0:T(8,128)(2,1)S(1)} %copy-done.2), channel_id=1, source_target_pairs={{0,2},{2,0},{1,3},{3,1},{4,6},{6,4},{5,7},{7,5},{8,10},{10,8},{9,1... | collective-permute-start | bytes 294920 | tf_op jit(solution)/shard_map/ppermute | solution.py:397
  7.2 5.0 %collective-permute-start = (bf16[64,768]{1,0:T(8,128)(2,1)S(1)}, bf16[64,768]{1,0:T(8,128)(2,1)S(1)}, u32[]{:S(2)}, u32[]{:S(2)}) collective-permute-start(bf16[64,768]{1,0:T(8,128)(2,1)S(1)} %copy-done.2), channel_id=1, source_target_pairs={{0,1},{1,0},{2,3},{3,2},{4,5},{5,4},{6,7},{7,6},{8,9},{9,8},{10,11... | collective-permute-start | bytes 294920 | tf_op jit(solution)/shard_map/ppermute | solution.py:397
  11.3 1.9 %collective-permute-start.2 = (bf16[64,768]{1,0:T(8,128)(2,1)S(1)}, bf16[64,768]{1,0:T(8,128)(2,1)S(1)}, u32[]{:S(2)}, u32[]{:S(2)}) collective-permute-start(bf16[64,768]{1,0:T(8,128)(2,1)S(1)} %collective-permute-done.1.qx_ref), channel_id=1, source_target_pairs={{0,1},{1,0},{2,3},{3,2},{4,5},{5,4},{6,7},{7,6},{8,9},{9,8},{10,11... | collective-permute-start | bytes 294920 | tf_op jit(solution)/shard_map/ppermute | solution.py:397
  13.2 12.1 %copy-start.1 = (bf16[2,192,768]{2,1,0:T(8,128)(2,1)S(1)}, bf16[2,192,768]{2,1,0:T(8,128)(2,1)}, u32[]{:S(2)}) copy-start(bf16[2,192,768]{2,1,0:T(8,128)(2,1)} %wo0.3) | copy-start | bytes 1769476
  16.2 8.3 %collective-permute-start.4 = (bf16[64,256]{1,0:T(8,128)(2,1)S(1)}, bf16[64,256]{1,0:T(8,128)(2,1)S(1)}, u32[]{:S(2)}, u32[]{:S(2)}) collective-permute-start(bf16[64,256]{1,0:T(8,128)(2,1)S(1)} %get-tuple-element.26), channel_id=1, source_target_pairs={{0,12},{4,8},{8,4},{12,0},{1,13},{5,9},{9,5},{13,1},{2,14},{6,10},... | collective-permute-start | bytes 98312 | tf_op jit(solution)/shard_map/ppermute | solution.py:402
  19.6 4.9 %collective-permute-start.5 = (bf16[64,256]{1,0:T(8,128)(2,1)S(1)}, bf16[64,256]{1,0:T(8,128)(2,1)S(1)}, u32[]{:S(2)}, u32[]{:S(2)}) collective-permute-start(bf16[64,256]{1,0:T(8,128)(2,1)S(1)} %get-tuple-element.27), channel_id=1, source_target_pairs={{0,8},{4,12},{8,0},{12,4},{1,9},{5,13},{9,1},{13,5},{2,10},{6,14},... | collective-permute-start | bytes 98312 | tf_op jit(solution)/shard_map/ppermute | solution.py:402
  19.6 4.9 %collective-permute-start.6 = (bf16[64,256]{1,0:T(8,128)(2,1)S(1)}, bf16[64,256]{1,0:T(8,128)(2,1)S(1)}, u32[]{:S(2)}, u32[]{:S(2)}) collective-permute-start(bf16[64,256]{1,0:T(8,128)(2,1)S(1)} %get-tuple-element.28), channel_id=1, source_target_pairs={{0,4},{4,0},{8,12},{12,8},{1,5},{5,1},{9,13},{13,9},{2,6},{6,2},{1... | collective-permute-start | bytes 98312 | tf_op jit(solution)/shard_map/ppermute | solution.py:402
  23.5 30.6 %collective-permute-start.16 = (bf16[1536,256]{1,0:T(8,128)(2,1)}, bf16[1536,256]{1,0:T(8,128)(2,1)S(1)}, u32[]{:S(2)}, u32[]{:S(2)}) collective-permute-start(bf16[1536,256]{1,0:T(8,128)(2,1)} %get-tuple-element.33), channel_id=1, source_target_pairs={{0,1},{1,0},{2,3},{3,2},{4,5},{5,4},{6,7},{7,6},{8,9},{9,8},{10,11... | collective-permute-start | bytes 2359304 | tf_op jit(solution)/shard_map/ppermute | solution.py:397
  24.7 2.0 %collective-permute-start.7 = (bf16[64,256]{1,0:T(8,128)(2,1)S(1)}, bf16[64,256]{1,0:T(8,128)(2,1)S(1)}, u32[]{:S(2)}, u32[]{:S(2)}) collective-permute-start(bf16[64,256]{1,0:T(8,128)(2,1)S(1)} %shard_map.93), channel_id=1, source_target_pairs={{0,1},{1,0},{2,3},{3,2},{4,5},{5,4},{6,7},{7,6},{8,9},{9,8},{10,11... | collective-permute-start | bytes 98312 | tf_op jit(solution)/shard_map/ppermute | solution.py:397
  25.3 15.3 %collective-permute-start.14 = (bf16[2,192,768]{2,1,0:T(8,128)(2,1)S(1)}, bf16[2,192,768]{2,1,0:T(8,128)(2,1)S(1)}, u32[]{:S(2)}, u32[]{:S(2)}) collective-permute-start(bf16[2,192,768]{2,1,0:T(8,128)(2,1)S(1)} %copy-done.1), channel_id=1, source_target_pairs={{0,2},{2,0},{1,3},{3,1},{4,6},{6,4},{5,7},{7,5},{8,10},{10,8},{9,1... | collective-permute-start | bytes 1769480 | tf_op jit(solution)/shard_map/ppermute | solution.py:397
  26.7 16.6 %collective-permute-start.8 = (bf16[64,384]{1,0:T(8,128)(2,1)S(1)}, bf16[64,384]{1,0:T(8,128)(2,1)S(1)}, u32[]{:S(2)}, u32[]{:S(2)}) collective-permute-start(bf16[64,384]{1,0:T(8,128)(2,1)S(1)} %pad_maximum_fusion.block_ref), channel_id=1, source_target_pairs={{0,14},{1,13},{2,12},{3,15},{4,10},{5,9},{6,8},{7,11},{8,6},{9,5},... | collective-permute-start | bytes 147464 | tf_op jit(solution)/shard_map/ppermute | solution.py:426
  30.1 23.9 %collective-permute-start.13 = (bf16[2,192,768]{2,1,0:T(8,128)(2,1)S(1)}, bf16[2,192,768]{2,1,0:T(8,128)(2,1)S(1)}, u32[]{:S(2)}, u32[]{:S(2)}) collective-permute-start(bf16[2,192,768]{2,1,0:T(8,128)(2,1)S(1)} %copy-done.1), channel_id=1, source_target_pairs={{0,1},{1,0},{2,3},{3,2},{4,5},{5,4},{6,7},{7,6},{8,9},{9,8},{10,11... | collective-permute-start | bytes 1769480 | tf_op jit(solution)/shard_map/ppermute | solution.py:397
  40.6 14.5 %collective-permute-start.15 = (bf16[2,192,768]{2,1,0:T(8,128)(2,1)S(1)}, bf16[2,192,768]{2,1,0:T(8,128)(2,1)S(1)}, u32[]{:S(2)}, u32[]{:S(2)}) collective-permute-start(bf16[2,192,768]{2,1,0:T(8,128)(2,1)S(1)} %collective-permute-done.14.wo2), channel_id=1, source_target_pairs={{0,1},{1,0},{2,3},{3,2},{4,5},{5,4},{6,7},{7,6},{8,9},{9,8},{10,11... | collective-permute-start | bytes 1769480 | tf_op jit(solution)/shard_map/ppermute | solution.py:397
  41.5 3.9 %collective-permute-start.9 = (bf16[64,384]{1,0:T(8,128)(2,1)S(1)}, bf16[64,384]{1,0:T(8,128)(2,1)S(1)}, u32[]{:S(2)}, u32[]{:S(2)}) collective-permute-start(bf16[64,384]{1,0:T(8,128)(2,1)S(1)} %pad_maximum_fusion.block_ref), channel_id=1, source_target_pairs={{0,10},{1,9},{2,8},{3,11},{4,14},{5,13},{6,12},{7,15},{8,2},{9,1},... | collective-permute-start | bytes 147464 | tf_op jit(solution)/shard_map/ppermute | solution.py:426
  43.3 3.2 %collective-permute-start.10 = (bf16[64,384]{1,0:T(8,128)(2,1)S(1)}, bf16[64,384]{1,0:T(8,128)(2,1)S(1)}, u32[]{:S(2)}, u32[]{:S(2)}) collective-permute-start(bf16[64,384]{1,0:T(8,128)(2,1)S(1)} %pad_maximum_fusion.block_ref), channel_id=1, source_target_pairs={{0,6},{1,5},{2,4},{3,7},{4,2},{5,1},{6,0},{7,3},{8,14},{9,13},{10,... | collective-permute-start | bytes 147464 | tf_op jit(solution)/shard_map/ppermute | solution.py:426
  45.5 1.1 %collective-permute-start.11 = (bf16[64,384]{1,0:T(8,128)(2,1)S(1)}, bf16[64,384]{1,0:T(8,128)(2,1)S(1)}, u32[]{:S(2)}, u32[]{:S(2)}) collective-permute-start(bf16[64,384]{1,0:T(8,128)(2,1)S(1)} %pad_maximum_fusion.block_ref), channel_id=1, source_target_pairs={{0,2},{2,0},{4,6},{6,4},{8,10},{10,8},{12,14},{14,12},{16,18},{18,... | collective-permute-start | bytes 147464 | tf_op jit(solution)/shard_map/ppermute | solution.py:426
  46.6 8.5 %collective-permute-start.12 = (bf16[256,384]{1,0:T(8,128)(2,1)S(1)}, bf16[256,384]{1,0:T(8,128)(2,1)S(1)}, u32[]{:S(2)}, u32[]{:S(2)}) collective-permute-start(bf16[256,384]{1,0:T(8,128)(2,1)S(1)} %constant_dynamic-update-slice_fusion.near_ref), channel_id=1, source_target_pairs={{0,1},{1,0},{2,3},{3,2},{4,5},{5,4},{6,7},{7,6},{8,9},{9,8},{10,11... | collective-permute-start | bytes 589832 | tf_op jit(solution)/shard_map/ppermute | solution.py:397
  58.7 4.6 %collective-permute-start.17 = (bf16[64,256]{1,0:T(8,128)(2,1)S(1)}, bf16[64,256]{1,0:T(8,128)(2,1)S(1)}, u32[]{:S(2)}, u32[]{:S(2)}) collective-permute-start(bf16[64,256]{1,0:T(8,128)(2,1)S(1)} %get-tuple-element.36), channel_id=1, source_target_pairs={{0,12},{4,8},{8,4},{12,0},{1,13},{5,9},{9,5},{13,1},{2,14},{6,10},... | collective-permute-start | bytes 98312 | tf_op jit(solution)/shard_map/ppermute | solution.py:402
  61.5 4.1 %collective-permute-start.18 = (bf16[64,256]{1,0:T(8,128)(2,1)S(1)}, bf16[64,256]{1,0:T(8,128)(2,1)S(1)}, u32[]{:S(2)}, u32[]{:S(2)}) collective-permute-start(bf16[64,256]{1,0:T(8,128)(2,1)S(1)} %get-tuple-element.37), channel_id=1, source_target_pairs={{0,8},{4,12},{8,0},{12,4},{1,9},{5,13},{9,1},{13,5},{2,10},{6,14},... | collective-permute-start | bytes 98312 | tf_op jit(solution)/shard_map/ppermute | solution.py:402
  61.5 4.1 %collective-permute-start.19 = (bf16[64,256]{1,0:T(8,128)(2,1)S(1)}, bf16[64,256]{1,0:T(8,128)(2,1)S(1)}, u32[]{:S(2)}, u32[]{:S(2)}) collective-permute-start(bf16[64,256]{1,0:T(8,128)(2,1)S(1)} %get-tuple-element.38), channel_id=1, source_target_pairs={{0,4},{4,0},{8,12},{12,8},{1,5},{5,1},{9,13},{13,9},{2,6},{6,2},{1... | collective-permute-start | bytes 98312 | tf_op jit(solution)/shard_map/ppermute | solution.py:402
  65.7 2.3 %collective-permute-start.20 = (bf16[64,256]{1,0:T(8,128)(2,1)S(1)}, bf16[64,256]{1,0:T(8,128)(2,1)S(1)}, u32[]{:S(2)}, u32[]{:S(2)}) collective-permute-start(bf16[64,256]{1,0:T(8,128)(2,1)S(1)} %shard_map.96), channel_id=1, source_target_pairs={{0,1},{1,0},{2,3},{3,2},{4,5},{5,4},{6,7},{7,6},{8,9},{9,8},{10,11... | collective-permute-start | bytes 98312 | tf_op jit(solution)/shard_map/ppermute | solution.py:397
  68.1 7.2 %collective-permute-start.21 = (bf16[64,384]{1,0:T(8,128)(2,1)S(1)}, bf16[64,384]{1,0:T(8,128)(2,1)S(1)}, u32[]{:S(2)}, u32[]{:S(2)}) collective-permute-start(bf16[64,384]{1,0:T(8,128)(2,1)S(1)} %pad_maximum_fusion.1), channel_id=1, source_target_pairs={{0,0},{4,1},{10,2},{14,3},{2,4},{6,5},{8,6},{12,7},{1,8},{5,9},{11... | collective-permute-start | bytes 147464 | tf_op jit(solution)/shard_map/ppermute | solution.py:437
  72.1 8.1 %collective-permute-start.22 = (bf16[64,384]{1,0:T(8,128)(2,1)S(1)}, bf16[64,384]{1,0:T(8,128)(2,1)S(1)}, u32[]{:S(2)}, u32[]{:S(2)}) collective-permute-start(bf16[64,384]{1,0:T(8,128)(2,1)S(1)} %pad_maximum_fusion.1), channel_id=1, source_target_pairs={{2,0},{6,1},{8,2},{12,3},{0,4},{4,5},{10,6},{14,7},{3,8},{7,9},{9,... | collective-permute-start | bytes 147464 | tf_op jit(solution)/shard_map/ppermute | solution.py:437
where the time goes:
time: 81.5 us; the launch traced here: 81.3 us
  starting transfers between devices  35.9 us (44%)
  waiting for transfers between devices  27.4 us (34%)
  Pallas kernels  16.3 us (20%)
  between operations  0.89 us (1%)
    ppermute x11, waiting for transfers between devices, swap(): return lax.ppermute(value, axis, [(i, i ^ 1) for i in range(size)])  17.5 us
    pallas_call x7, Pallas kernels, vmem_call(): pl.pallas_call(kernel, out_shape=out_shape, in_specs=specs, out_specs=jax...  16.3 us
    ppermute x11, starting transfers between devices, swap(): return lax.ppermute(value, axis, [(i, i ^ 1) for i in range(size)])  14.7 us
    ppermute x6, starting transfers between devices, exchange(): lax.ppermute(chunks[d], 'tiles', [(i, i ^ d) for i in range(plan.n_t)])  7.37 us
    ppermute x4, starting transfers between devices, spread(): received.append(lax.ppermute(block, axes, links))  7.23 us
    ppermute x2, starting transfers between devices, collect(): received.append(lax.ppermute(block, axes, links))  6.58 us
    ppermute x2, waiting for transfers between devices, collect(): received.append(lax.ppermute(block, axes, links))  5.5 us
    ppermute x6, waiting for transfers between devices, exchange(): lax.ppermute(chunks[d], 'tiles', [(i, i ^ d) for i in range(plan.n_t)])  3.27 us
  transfers between devices with their start and end apart: 23, of which 12 were waited for; matrix products, arithmetic and copies ran while one was open for 0% of the time, Pallas kernels for 4%

commit v1 on v0

--- a/solution.py
+++ b/solution.py
@@ -114,7 +114,7 @@
         offsets = sorted(offsets, reverse=True)
         offsets += [None] * (-len(offsets) % self.n_k)
         self.rounds = [
-            tuple(offsets[i + k] for k in range(self.n_k))
+            tuple(offsets[i + (k + i // self.n_k) % self.n_k] for k in range(self.n_k))
             for i in range(0, len(offsets), self.n_k)
         ]
 
@@ -142,15 +142,13 @@
     return pl.ds(pl.multiple_of(index * size, size), size)
 
 
-def project_rows(plan, count_ref, mask_ref, feats, weights, own_ref, other_ref, low, high):
+def project_rows(plan, live_ref, feats, weights, own_ref, other_ref, low, high):
     first = lax.axis_index("kv") == 0
-    rows = mask_ref.shape[1]
+    rows = live_ref.shape[1]
     lane = lax.broadcasted_iota(jnp.int32, (1, plan.width), 1)
     acc = jnp.dot(feats[low:high, :], weights[...], preferred_element_type=jnp.float32)
     for slot in range(low // rows, high // rows):
-        marks = mask_ref[slot : slot + 1, :].astype(jnp.float32)
-        marks = jnp.where(slot < count_ref[0], marks, 0.0)
-        valid = jnp.broadcast_to(marks, (LANES, rows)).T
+        valid = jnp.broadcast_to(live_ref[slot : slot + 1, :], (LANES, rows)).T
         valid = jnp.concatenate([valid] * (plan.width // LANES), axis=1)
         part = acc[slot * rows - low : slot * rows - low + rows]
         pieces = []
@@ -163,27 +161,32 @@
         other_ref[at, :] = jnp.where(first, pieces[1], pieces[0])
 
 
-def group_of(mask_ref):
-    slots, rows = mask_ref.shape
+def group_of(live_ref):
+    slots, rows = live_ref.shape
     return rows * (2 if slots % 2 == 0 else 1)
 
 
 def load_project_kernel(
     plan,
     count_ref,
-    mask_ref,
     feats_hbm,
     weights_hbm,
+    mask_hbm,
     own_ref,
     other_ref,
     feats_ref,
     later_ref,
+    live_ref,
     weights_ref,
+    mask_ref,
     sems,
 ):
-    size = group_of(mask_ref)
+    size = group_of(live_ref)
     groups = feats_ref.shape[0] // size
-    copies = [pltpu.make_async_copy(weights_hbm.at[0], weights_ref, sems.at[groups])]
+    copies = [
+        pltpu.make_async_copy(mask_hbm, mask_ref, sems.at[groups + 2]),
+        pltpu.make_async_copy(weights_hbm.at[0], weights_ref, sems.at[groups]),
+    ]
     for index in range(groups):
         at = pl.ds(index * size, size)
         copies.append(
@@ -193,21 +196,21 @@
     for copy in copies:
         copy.start()
     copies[0].wait()
+    marks = mask_ref[...].astype(jnp.float32)
+    slot_ids = lax.broadcasted_iota(jnp.int32, marks.shape, 0)
+    live_ref[...] = jnp.where(slot_ids < count_ref[0], marks, 0.0)
+    copies[1].wait()
     for index in range(groups):
-        copies[1 + index].wait()
+        copies[2 + index].wait()
         low = index * size
-        project_rows(
-            plan, count_ref, mask_ref, feats_ref, weights_ref, own_ref, other_ref, low, low + size
-        )
+        project_rows(plan, live_ref, feats_ref, weights_ref, own_ref, other_ref, low, low + size)
     copies[-1].wait()
 
 
-def project_kernel(plan, count_ref, mask_ref, feats_ref, weights_ref, own_ref, other_ref):
-    size = group_of(mask_ref)
+def project_kernel(plan, live_ref, feats_ref, weights_ref, own_ref, other_ref):
+    size = group_of(live_ref)
     for low in range(0, feats_ref.shape[0], size):
-        project_rows(
-            plan, count_ref, mask_ref, feats_ref, weights_ref, own_ref, other_ref, low, low + size
-        )
+        project_rows(plan, live_ref, feats_ref, weights_ref, own_ref, other_ref, low, low + size)
 
 
 def attend(plan, query, scale_ref, own_ref, recv_ref, chunk_refs, mix):
@@ -219,7 +222,7 @@
     factor = SOFT_CAP * math.log2(math.e)
     n_keys = own_ref.shape[0]
     block = min(n_keys, 512)
-    masked, scales, totals = [], [], []
+    masked, scales = [], []
     for head in range(plan.heads):
         low = off + head * plan.head_dim
         masked.append(
@@ -228,21 +231,24 @@
         scales.append(
             scale_ref[side * plan.heads + head] * (1.0 / (SOFT_CAP * math.sqrt(plan.head_dim)))
         )
-        totals.append(None)
+    stacked = jnp.concatenate(masked, axis=0)
     for at in range(0, n_keys, block):
         mine = own_ref[at : at + block, :]
         theirs = recv_ref[at : at + block, :]
         keys = jnp.where(first, mine, theirs)
         values = jnp.where(first, theirs, mine)
-        for head in range(plan.heads):
-            scores = lax.dot_general(
-                masked[head], keys, (((1,), (1,)), ((), ())), preferred_element_type=jnp.float32
-            )
-            weight = jnp.exp2(jnp.tanh(scores * scales[head]) * factor)
-            part = jnp.dot(
-                weight.astype(jnp.bfloat16), values, preferred_element_type=jnp.float32
-            )
-            totals[head] = part if totals[head] is None else totals[head] + part
+        scores = lax.dot_general(
+            stacked, keys, (((1,), (1,)), ((), ())), preferred_element_type=jnp.float32
+        )
+        weights = []
+        for head, scale in enumerate(scales):
+            part = scores[head * plan.n_q : head * plan.n_q + plan.n_q]
+            weights.append(jnp.exp2(jnp.tanh(part * scale) * factor).astype(jnp.bfloat16))
+        part = jnp.dot(
+            jnp.concatenate(weights, axis=0), values, preferred_element_type=jnp.float32
+        )
+        mix[...] = part if at == 0 else mix[...] + part
+    totals = [mix[head * plan.n_q : head * plan.n_q + plan.n_q, :] for head in range(plan.heads)]
     result = jnp.zeros((plan.n_q, plan.width), jnp.float32)
     spot = lane - pad
     spare = (spot >= 0) & (spot < 2 * SPLIT)
@@ -253,7 +259,7 @@
         result = jnp.where(keep, totals[head], result)
     rounded = result.astype(jnp.bfloat16).astype(jnp.float32)
     late = spare & (spot >= SPLIT)
-    mix[...] = jnp.where(late, result - rounded, rounded)
+    mix[: plan.n_q, :] = jnp.where(late, result - rounded, rounded)
     for index, ref in enumerate(chunk_refs):
         rows = plan.n_q // plan.n_t
         ref[...] = mix[rows_at(jnp.bitwise_xor(me_t, index), rows), :].astype(ref.dtype)
@@ -271,17 +277,21 @@
     ).astype(jnp.bfloat16)
 
 
+def gather_queries(plan, refs, states_ref):
+    _, me_h, me_k = place()
+    for dh in range(plan.n_h):
+        for dk in range(plan.n_k):
+            index = jnp.bitwise_xor(me_h, dh) * plan.n_k + jnp.bitwise_xor(me_k, dk)
+            block = refs[dh * plan.n_k + dk][...]
+            states_ref[rows_at(index, plan.q_rows), :] = block.astype(jnp.float32)
+
+
 def first_kernel(
     plan, scale_ref, q_ref, qk_ref, qx_ref, qxk_ref, gain_ref, wq_ref, own_ref, recv_ref, *rest
 ):
-    chunks, (all_ref, wq_pad, mix) = rest[: plan.n_t], rest[plan.n_t :]
-    _, me_h, me_k = place()
-    for dh, row in enumerate(((q_ref, qk_ref), (qx_ref, qxk_ref))):
-        for dk, ref in enumerate(row):
-            index = jnp.bitwise_xor(me_h, dh) * plan.n_k + jnp.bitwise_xor(me_k, dk)
-            all_ref[rows_at(index, plan.q_rows), :] = ref[...]
-    states = all_ref[...].astype(jnp.float32)
-    query = query_of(plan, states, gain_ref[0:1, :], wq_ref[0], wq_pad)
+    chunks, (states_ref, wq_pad, mix) = rest[: plan.n_t], rest[plan.n_t :]
+    gather_queries(plan, (q_ref, qk_ref, qx_ref, qxk_ref), states_ref)
+    query = query_of(plan, states_ref[...], gain_ref[0:1, :], wq_ref[0], wq_pad)
     attend(plan, query, scale_ref, own_ref, recv_ref, chunks, mix)
 
 
@@ -297,7 +307,10 @@
     plan,
     layer,
     scale_ref,
-    all_ref,
+    q_ref,
+    qk_ref,
+    qx_ref,
+    qxk_ref,
     block_ref,
     near_ref,
     far_ref,
@@ -307,11 +320,18 @@
     wo3,
     gain_ref,
     wq_ref,
-    own_ref,
-    recv_ref,
+    own_hbm,
+    recv_hbm,
     *rest,
 ):
-    chunks, (kept_ref, att, wo_all, states_ref, wq_pad, mix) = rest[: plan.n_t], rest[plan.n_t :]
+    chunks, rest = rest[: plan.n_t], rest[plan.n_t :]
+    kept_ref, att, wo_all, states_ref, wq_pad, mix, own_ref, recv_ref, sems = rest
+    copies = [
+        pltpu.make_async_copy(own_hbm, own_ref, sems.at[0]),
+        pltpu.make_async_copy(recv_hbm, recv_ref, sems.at[1]),
+    ]
+    for copy in copies:
+        copy.start()
     me_t, me_h, me_k = place()
     rows = plan.n_q // plan.n_t
     fill_out(plan, layer - 1, (wo0, wo1, wo2, wo3), wo_all)
@@ -320,16 +340,18 @@
             choice = [pair[k ^ flip] or (0, 0) for k in range(2)]
             dt = jnp.where(me_k == 0, choice[0][0], choice[1][0])
             dh = jnp.where(me_k == 0, choice[0][1], choice[1][1])
-            att[dh, rows_at(jnp.bitwise_xor(me_t, dt), rows), :] = ref[
+            att[rows_at(jnp.bitwise_xor(me_t, dt), rows), rows_at(dh, plan.cols)] = ref[
                 index * rows : index * rows + rows, :
             ]
-    att[0, rows_at(me_t, rows), :] = block_ref[...]
-    out = jnp.dot(att[0], wo_all[: plan.cols, :], preferred_element_type=jnp.float32)
-    out = out + jnp.dot(att[1], wo_all[plan.cols :, :], preferred_element_type=jnp.float32)
-    states = all_ref[...].astype(jnp.float32) + out
+    att[rows_at(me_t, rows), : plan.cols] = block_ref[...]
+    out = jnp.dot(att[...], wo_all[...], preferred_element_type=jnp.float32)
+    gather_queries(plan, (q_ref, qk_ref, qx_ref, qxk_ref), states_ref)
+    states = states_ref[...] + out
     states_ref[...] = states
     kept_ref[...] = states_ref[rows_at(me_h * plan.n_k + me_k, plan.q_rows), :]
     query = query_of(plan, states, gain_ref[layer : layer + 1, :], wq_ref[layer], wq_pad)
+    for copy in copies:
+        copy.wait()
     attend(plan, query, scale_ref, own_ref, recv_ref, chunks, mix)
 
 
@@ -337,9 +359,8 @@
     me_t = lax.axis_index("tiles")
     fill_out(plan, layer, (wo0, wo1, wo2, wo3), wo_all)
     for index, ref in enumerate((near_ref, far_ref)):
-        att[(me_t + index) % plan.n_h] = ref[...]
-    out = jnp.dot(att[0], wo_all[: plan.cols, :], preferred_element_type=jnp.float32)
-    out = out + jnp.dot(att[1], wo_all[plan.cols :, :], preferred_element_type=jnp.float32)
+        att[:, rows_at((me_t + index) % plan.n_h, plan.cols)] = ref[...]
+    out = jnp.dot(att[...], wo_all[...], preferred_element_type=jnp.float32)
     out_ref[...] = kept_ref[...] + out
 
 
@@ -442,70 +463,82 @@
     q_x = swap(queries, "heads")
     q_k = swap(queries, "kv")
     q_xk = swap(q_x, "kv")
-    tied, _ = lax.optimization_barrier((w_out, q_x))
-    wo_x = swap(tied, "heads")
+    wo_x = swap(w_out, "heads")
     wo = [w_out, swap(w_out, "kv"), wo_x, swap(wo_x, "kv")]
     tiles = features.shape[0]
     bf16, f32 = jnp.bfloat16, jnp.float32
     feat = features.shape[1]
     piece = jax.ShapeDtypeStruct((tiles, plan.width), bf16)
     cost = 2 * tiles * feat * plan.cols
-    own, other, near_tiles, later = vmem_call(
+    live_shape = jax.ShapeDtypeStruct(tile_mask.shape, f32)
+    own, other, near_tiles, later, live = vmem_call(
         functools.partial(load_project_kernel, plan),
         [
             piece,
             piece,
             jax.ShapeDtypeStruct((tiles, feat), bf16),
             jax.ShapeDtypeStruct((feat, plan.cols), bf16),
+            live_shape,
         ],
         [counts],
-        [tile_mask],
-        [pltpu.VMEM((feat, plan.cols), bf16)],
+        [],
+        [
+            pltpu.VMEM((feat, plan.cols), bf16),
+            pltpu.VMEM(tile_mask.shape, jnp.int32),
+        ],
         cost,
-        tuple(pltpu.with_memory_space_constraint(a, pltpu.HBM) for a in (features, weights)),
-        tile_mask.shape[0] + 2,
+        [
+            pltpu.with_memory_space_constraint(a, pltpu.HBM)
+            for a in (features, weights, tile_mask)
+        ],
+        tile_mask.shape[0] + 3,
     )
     pairs = [(own, swap(other, "kv"))]
     own, other = vmem_call(
         functools.partial(project_kernel, plan),
         [piece, piece],
-        [counts],
-        [tile_mask, near_tiles, later],
+        [],
+        [live, near_tiles, later],
         [],
         cost,
     )
     pairs.append((own, swap(other, "kv")))
+
     chunk_shapes = [jax.ShapeDtypeStruct((rows, plan.width), f32)]
     chunk_shapes += [jax.ShapeDtypeStruct((rows, plan.width), bf16)] * (plan.n_t - 1)
     wq_scratch = pltpu.VMEM((plan.width, plan.dq), bf16)
-    mix_scratch = pltpu.VMEM((plan.n_q, plan.width), f32)
+    states_scratch = pltpu.VMEM((plan.n_q, plan.dq), f32)
+    mix_scratch = pltpu.VMEM((plan.heads * plan.n_q, plan.width), f32)
     wo_scratch = pltpu.VMEM((plan.n_h * plan.cols, plan.dq), bf16)
 
     work = 4 * plan.n_q * tiles * plan.width
-    outs = vmem_call(
+    chunks = vmem_call(
         functools.partial(first_kernel, plan),
-        chunk_shapes + [jax.ShapeDtypeStruct((plan.n_q, plan.dq), bf16)],
+        chunk_shapes,
         [head_scale],
         [queries, q_k, q_x, q_xk, norm_gain, wq, *pairs[0]],
-        [wq_scratch, mix_scratch],
+        [states_scratch, wq_scratch, mix_scratch],
         work,
     )
-    chunks, states = outs[: plan.n_t], outs[plan.n_t]
     block = exchange(chunks)
     near, far = spread(block)
     outs = vmem_call(
         functools.partial(layer_kernel, plan, 1),
         chunk_shapes + [jax.ShapeDtypeStruct((plan.q_rows, plan.dq), f32)],
         [head_scale],
-        [states, block, near, far, *wo, norm_gain, wq, *pairs[1]],
+        [queries, q_k, q_x, q_xk, block, near, far, *wo, norm_gain, wq],
         [
-            pltpu.VMEM((plan.n_h, plan.n_q, plan.cols), bf16),
+            pltpu.VMEM((plan.n_q, plan.n_h * plan.cols), bf16),
             wo_scratch,
-            pltpu.VMEM((plan.n_q, plan.dq), f32),
+            states_scratch,
             wq_scratch,
             mix_scratch,
+            pltpu.VMEM((tiles, plan.width), bf16),
+            pltpu.VMEM((tiles, plan.width), bf16),
         ],
         work,
+        [pltpu.with_memory_space_constraint(a, pltpu.HBM) for a in pairs[1]],
+        2,
     )
     chunks, kept = outs[: plan.n_t], outs[plan.n_t]
     block = exchange(chunks)
@@ -515,7 +548,7 @@
         jax.ShapeDtypeStruct((plan.q_rows, plan.dq), f32),
         [],
         [kept, near, far, *wo],
-        [pltpu.VMEM((plan.n_h, plan.q_rows, plan.cols), bf16), wo_scratch],
+        [pltpu.VMEM((plan.q_rows, plan.n_h * plan.cols), bf16), wo_scratch],
         2 * plan.q_rows * plan.dq * plan.dq,
     )
 

time: 81.5 us -> 78.8 us (0.967)
  starting transfers between devices: 35.9 us -> 30.4 us
  waiting for transfers between devices: 27.4 us -> 30.5 us
    ppermute x11, starting transfers between devices: 14.7 us -> 7.56 us  [swap(): return lax.ppermute(value, axis, [(i, i ^ 1) for i in range(size)])]
    ppermute x4, waiting for transfers between devices: 1.12 us -> 5.23 us  [spread(): received.append(lax.ppermute(block, axes, links))]
    ppermute x4, starting transfers between devices: 7.23 us -> 8.89 us  [spread(): received.append(lax.ppermute(block, axes, links))]
  transfers between devices with their start and end apart: 23 -> 23, of which waited for: 12 -> 12; matrix products, arithmetic and copies ran while one was open for 0% -> 0% of each run, Pallas kernels for 4% -> 3%
where the time goes in v1:
time: 78.8 us; the launch traced here: 78.5 us
  waiting for transfers between devices  30.5 us (39%)
  starting transfers between devices  30.4 us (39%)
  Pallas kernels  15.7 us (20%)
  local copies, waits for them, and re-layouts  0.95 us (1%)
  between operations  0.92 us (1%)
    ppermute x11, waiting for transfers between devices, swap(): return lax.ppermute(value, axis, [(i, i ^ 1) for i in range(size)])  17 us
    pallas_call x7, Pallas kernels, vmem_call(): pl.pallas_call(kernel, out_shape=out_shape, in_specs=specs, out_specs=jax...  15.7 us
    ppermute x4, starting transfers between devices, spread(): received.append(lax.ppermute(block, axes, links))  8.89 us
    ppermute x11, starting transfers between devices, swap(): return lax.ppermute(value, axis, [(i, i ^ 1) for i in range(size)])  7.56 us
    ppermute x6, starting transfers between devices, exchange(): lax.ppermute(chunks[d], 'tiles', [(i, i ^ d) for i in range(plan.n_t)])  7.37 us
    ppermute x2, starting transfers between devices, collect(): received.append(lax.ppermute(block, axes, links))  6.56 us
    ppermute x2, waiting for transfers between devices, collect(): received.append(lax.ppermute(block, axes, links))  5.3 us
    ppermute x4, waiting for transfers between devices, spread(): received.append(lax.ppermute(block, axes, links))  5.23 us
  transfers between devices with their start and end apart: 23, of which 12 were waited for; matrix products, arithmetic and copies ran while one was open for 0% of the time, Pallas kernels for 3%

profile of v1, /device:TPU:7, one launch (start us, length us, event | category | flops | bytes accessed | tf_op | source)
XLA Modules:
  0.0 78.5 jit_solution(13116762530395595338)
XLA Ops:
  0.0 0.0 copy-start.3
  0.0 0.0 copy-start
  0.0 0.0 copy-start.5
  0.7 4.8 %shard_map.91 = (bf16[1536,256]{1,0:T(8,128)(2,1)S(1)}, bf16[1536,256]{1,0:T(8,128)(2,1)S(1)}, bf16[1536,1536]{1,0:T(8,128)(2,1)S(1)}, bf16[1536,384]{1,0:T(8,128)(2,1)S(1)}, f32[6,256]{1,0:T(8,128)S(1)}) custom-call(s32[1]{0:T(128)S(6)} %copy.13.count_ref, bf16[1536,1536]{1,0:T(8,128)(2,1)} %feats_hbm.1, bf16[2,1536,384]{2,1,0:T(8,128)(2,1)} %bitcast.4, ...), custom_call_target="tpu_custom_call" | custom-call | flops 1811939328 | bytes 1048576 | tf_op jit(solution)/shard_map/pallas_call | solution.py:393
  5.6 0.0 copy-start.1
  5.6 0.7 collective-permute-start.3
  6.3 0.0 copy-done.3
  6.3 0.3 collective-permute-start.1
  6.6 0.4 collective-permute-start
  7.0 3.6 %collective-permute-done.1.qx_ref = bf16[64,768]{1,0:T(8,128)(2,1)S(1)} collective-permute-done((bf16[64,768]{1,0:T(8,128)(2,1)S(1)}, bf16[64,768]{1,0:T(8,128)(2,1)S(1)}, u32[]{:S(2)}, u32[]{:S(2)}) %collective-permute-start.1) | collective-permute-done | bytes 98336 | tf_op jit(solution)/shard_map/ppermute | solution.py:418
  10.6 0.9 %collective-permute-start.2 = (bf16[64,768]{1,0:T(8,128)(2,1)S(1)}, bf16[64,768]{1,0:T(8,128)(2,1)S(1)}, u32[]{:S(2)}, u32[]{:S(2)}) collective-permute-start(bf16[64,768]{1,0:T(8,128)(2,1)S(1)} %collective-permute-done.1.qx_ref), channel_id=1, source_target_pairs={{0,1},{1,0},{2,3},{3,2},{4,5},{5,4},{6,7},{7,6},{8,9},{9,8},{10,11... | collective-permute-start | bytes 294920 | tf_op jit(solution)/shard_map/ppermute | solution.py:418
  11.5 0.0 collective-permute-done.qk_ref
  11.5 0.9 %collective-permute-done.2.qxk_ref = bf16[64,768]{1,0:T(8,128)(2,1)S(1)} collective-permute-done((bf16[64,768]{1,0:T(8,128)(2,1)S(1)}, bf16[64,768]{1,0:T(8,128)(2,1)S(1)}, u32[]{:S(2)}, u32[]{:S(2)}) %collective-permute-start.2) | collective-permute-done | bytes 98336 | tf_op jit(solution)/shard_map/ppermute | solution.py:418
  12.5 0.0 collective-permute-done.3.recv_ref
  12.5 0.0 copy-done
  12.5 0.0 copy-done.4
  12.5 0.0 copy-done.5
  12.5 2.7 %shard_map.92 = (f32[64,256]{1,0:T(8,128)S(1)}, bf16[64,256]{1,0:T(8,128)(2,1)S(1)}, bf16[64,256]{1,0:T(8,128)(2,1)S(1)}, bf16[64,256]{1,0:T(8,128)(2,1)S(1)}) custom-call(f32[6]{0:T(128)S(1)} %copy-done.5, bf16[64,768]{1,0:T(8,128)(2,1)S(1)} %copy-done.3, bf16[64,768]{1,0:T(8,128)(2,1)S(1)} %collective-permute-done.qk_ref, ...), custom_call_target="tpu_custom_call" | custom-call | flops 402653184 | bytes 1048576 | tf_op jit(solution)/shard_map/pallas_call | solution.py:393
  15.2 3.4 %collective-permute-start.4 = (bf16[64,256]{1,0:T(8,128)(2,1)S(1)}, bf16[64,256]{1,0:T(8,128)(2,1)S(1)}, u32[]{:S(2)}, u32[]{:S(2)}) collective-permute-start(bf16[64,256]{1,0:T(8,128)(2,1)S(1)} %get-tuple-element.24), channel_id=1, source_target_pairs={{0,12},{4,8},{8,4},{12,0},{1,13},{5,9},{9,5},{13,1},{2,14},{6,10},... | collective-permute-start | bytes 98312 | tf_op jit(solution)/shard_map/ppermute | solution.py:423
  18.6 0.0 collective-permute-start.5
  18.6 0.4 collective-permute-start.6
  18.9 2.6 %shard_map.94 = (bf16[1536,256]{1,0:T(8,128)(2,1)S(1)}, bf16[1536,256]{1,0:T(8,128)(2,1)S(1)}) custom-call(f32[6,256]{1,0:T(8,128)S(1)} %get-tuple-element.27.live_ref, bf16[1536,1536]{1,0:T(8,128)(2,1)S(1)} %get-tuple-element.28.feats_ref, bf16[1536,384]{1,0:T(8,128)(2,1)S(1)} %get-tuple-element.29.weights_ref), custom_call_target="tpu_custom_call" | custom-call | flops 1811939328 | bytes 1048576 | tf_op jit(solution)/shard_map/pallas_call | solution.py:393
  21.6 0.0 copy-start.2
  21.6 0.9 %copy-done.2 = bf16[1536,256]{1,0:T(8,128)(2,1)} copy-done((bf16[1536,256]{1,0:T(8,128)(2,1)}, bf16[1536,256]{1,0:T(8,128)(2,1)S(1)}, u32[]{:S(2)}) %copy-start.2) | copy-done | bytes 786456
  22.4 1.1 %collective-permute-start.16 = (bf16[1536,256]{1,0:T(8,128)(2,1)S(1)}, bf16[1536,256]{1,0:T(8,128)(2,1)}, u32[]{:S(2)}, u32[]{:S(2)}) collective-permute-start(bf16[1536,256]{1,0:T(8,128)(2,1)S(1)} %get-tuple-element.31), channel_id=1, source_target_pairs={{0,1},{1,0},{2,3},{3,2},{4,5},{5,4},{6,7},{7,6},{8,9},{9,8},{10,11... | collective-permute-start | bytes 2359304 | tf_op jit(solution)/shard_map/ppermute | solution.py:418
  23.5 0.0 copy-done.1
  23.5 0.3 collective-permute-start.14
  23.8 0.0 collective-permute-done.4.refs_1_
  23.8 0.0 collective-permute-done.5.refs_2_
  23.8 0.0 collective-permute-done.6.refs_3_
  23.8 0.1 shard_map.93
  23.9 0.3 collective-permute-start.7
  24.3 1.3 %collective-permute-done.7 = bf16[64,256]{1,0:T(8,128)(2,1)S(1)} collective-permute-done((bf16[64,256]{1,0:T(8,128)(2,1)S(1)}, bf16[64,256]{1,0:T(8,128)(2,1)S(1)}, u32[]{:S(2)}, u32[]{:S(2)}) %collective-permute-start.7) | collective-permute-done | bytes 32800 | tf_op jit(solution)/shard_map/ppermute | solution.py:418
  25.6 3.4 %collective-permute-start.8 = (bf16[64,384]{1,0:T(8,128)(2,1)S(1)}, bf16[64,384]{1,0:T(8,128)(2,1)S(1)}, u32[]{:S(2)}, u32[]{:S(2)}) collective-permute-start(bf16[64,384]{1,0:T(8,128)(2,1)S(1)} %pad_maximum_fusion.block_ref), channel_id=1, source_target_pairs={{0,14},{1,13},{2,12},{3,15},{4,10},{5,9},{6,8},{7,11},{8,6},{9,5},... | collective-permute-start | bytes 147464 | tf_op jit(solution)/shard_map/ppermute | solution.py:447
  29.0 1.1 %collective-permute-start.13 = (bf16[2,192,768]{2,1,0:T(8,128)(2,1)S(1)}, bf16[2,192,768]{2,1,0:T(8,128)(2,1)S(1)}, u32[]{:S(2)}, u32[]{:S(2)}) collective-permute-start(bf16[2,192,768]{2,1,0:T(8,128)(2,1)S(1)} %copy-done.1), channel_id=1, source_target_pairs={{0,1},{1,0},{2,3},{3,2},{4,5},{5,4},{6,7},{7,6},{8,9},{9,8},{10,11... | collective-permute-start | bytes 1769480 | tf_op jit(solution)/shard_map/ppermute | solution.py:418
  30.1 8.8 %collective-permute-done.14.wo2 = bf16[2,192,768]{2,1,0:T(8,128)(2,1)S(1)} collective-permute-done((bf16[2,192,768]{2,1,0:T(8,128)(2,1)S(1)}, bf16[2,192,768]{2,1,0:T(8,128)(2,1)S(1)}, u32[]{:S(2)}, u32[]{:S(2)}) %collective-permute-start.14) | collective-permute-done | bytes 589856 | tf_op jit(solution)/shard_map/ppermute | solution.py:418
  38.9 0.9 %collective-permute-start.15 = (bf16[2,192,768]{2,1,0:T(8,128)(2,1)S(1)}, bf16[2,192,768]{2,1,0:T(8,128)(2,1)S(1)}, u32[]{:S(2)}, u32[]{:S(2)}) collective-permute-start(bf16[2,192,768]{2,1,0:T(8,128)(2,1)S(1)} %collective-permute-done.14.wo2), channel_id=1, source_target_pairs={{0,1},{1,0},{2,3},{3,2},{4,5},{5,4},{6,7},{7,6},{8,9},{9,8},{10,11... | collective-permute-start | bytes 1769480 | tf_op jit(solution)/shard_map/ppermute | solution.py:418
  39.8 1.8 %collective-permute-start.9 = (bf16[64,384]{1,0:T(8,128)(2,1)S(1)}, bf16[64,384]{1,0:T(8,128)(2,1)S(1)}, u32[]{:S(2)}, u32[]{:S(2)}) collective-permute-start(bf16[64,384]{1,0:T(8,128)(2,1)S(1)} %pad_maximum_fusion.block_ref), channel_id=1, source_target_pairs={{0,8},{1,11},{2,10},{3,9},{4,12},{5,15},{6,14},{7,13},{8,0},{9,3},... | collective-permute-start | bytes 147464 | tf_op jit(solution)/shard_map/ppermute | solution.py:447
  41.6 0.0 collective-permute-done.8
  41.6 1.7 %collective-permute-start.10 = (bf16[64,384]{1,0:T(8,128)(2,1)S(1)}, bf16[64,384]{1,0:T(8,128)(2,1)S(1)}, u32[]{:S(2)}, u32[]{:S(2)}) collective-permute-start(bf16[64,384]{1,0:T(8,128)(2,1)S(1)} %pad_maximum_fusion.block_ref), channel_id=1, source_target_pairs={{0,6},{1,5},{2,4},{3,7},{4,2},{5,1},{6,0},{7,3},{8,14},{9,13},{10,... | collective-permute-start | bytes 147464 | tf_op jit(solution)/shard_map/ppermute | solution.py:447
  43.4 2.4 %collective-permute-done.9 = bf16[64,384]{1,0:T(8,128)(2,1)S(1)} collective-permute-done((bf16[64,384]{1,0:T(8,128)(2,1)S(1)}, bf16[64,384]{1,0:T(8,128)(2,1)S(1)}, u32[]{:S(2)}, u32[]{:S(2)}) %collective-permute-start.9) | collective-permute-done | bytes 49184 | tf_op jit(solution)/shard_map/ppermute | solution.py:447
  45.7 1.9 %collective-permute-start.11 = (bf16[64,384]{1,0:T(8,128)(2,1)S(1)}, bf16[64,384]{1,0:T(8,128)(2,1)S(1)}, u32[]{:S(2)}, u32[]{:S(2)}) collective-permute-start(bf16[64,384]{1,0:T(8,128)(2,1)S(1)} %pad_maximum_fusion.block_ref), channel_id=1, source_target_pairs={{1,3},{3,1},{5,7},{7,5},{9,11},{11,9},{13,15},{15,13},{17,19},{19,... | collective-permute-start | bytes 147464 | tf_op jit(solution)/shard_map/ppermute | solution.py:447
  47.7 0.0 collective-permute-done.10
  47.7 2.9 %collective-permute-done.11 = bf16[64,384]{1,0:T(8,128)(2,1)S(1)} collective-permute-done((bf16[64,384]{1,0:T(8,128)(2,1)S(1)}, bf16[64,384]{1,0:T(8,128)(2,1)S(1)}, u32[]{:S(2)}, u32[]{:S(2)}) %collective-permute-start.11) | collective-permute-done | bytes 49184 | tf_op jit(solution)/shard_map/ppermute | solution.py:447
  50.6 0.1 collective-permute-start.12
  50.7 0.0 collective-permute-done.13.wo1
  50.7 0.0 collective-permute-done.16.recv_hbm
  50.7 1.4 %collective-permute-done.12.far_ref = bf16[256,384]{1,0:T(8,128)(2,1)S(1)} collective-permute-done((bf16[256,384]{1,0:T(8,128)(2,1)S(1)}, bf16[256,384]{1,0:T(8,128)(2,1)S(1)}, u32[]{:S(2)}, u32[]{:S(2)}) %collective-permute-start.12) | collective-permute-done | bytes 196640 | tf_op jit(solution)/shard_map/ppermute | solution.py:418
  52.1 0.0 collective-permute-done.15.wo3
  52.1 4.3 %shard_map.95 = (f32[64,256]{1,0:T(8,128)S(1)}, bf16[64,256]{1,0:T(8,128)(2,1)S(1)}, bf16[64,256]{1,0:T(8,128)(2,1)S(1)}, bf16[64,256]{1,0:T(8,128)(2,1)S(1)}, f32[64,768]{1,0:T(8,128)S(1)}) custom-call(f32[6]{0:T(128)S(1)} %copy-done.5, bf16[64,768]{1,0:T(8,128)(2,1)S(1)} %copy-done.3, bf16[64,768]{1,0:T(8,128)(2,1)S(1)} %collective-permute-done.qk_ref, ...), custom_call_target="tpu_custom_call" | custom-call | flops 402653184 | bytes 1048576 | tf_op jit(solution)/shard_map/pallas_call | solution.py:393
  56.4 2.8 %collective-permute-start.17 = (bf16[64,256]{1,0:T(8,128)(2,1)S(1)}, bf16[64,256]{1,0:T(8,128)(2,1)S(1)}, u32[]{:S(2)}, u32[]{:S(2)}) collective-permute-start(bf16[64,256]{1,0:T(8,128)(2,1)S(1)} %get-tuple-element.34), channel_id=1, source_target_pairs={{0,12},{4,8},{8,4},{12,0},{1,13},{5,9},{9,5},{13,1},{2,14},{6,10},... | collective-permute-start | bytes 98312 | tf_op jit(solution)/shard_map/ppermute | solution.py:423
  59.2 0.0 collective-permute-start.18
  59.2 0.8 collective-permute-start.19
  60.0 1.0 %collective-permute-done.17.refs_1_ = bf16[64,256]{1,0:T(8,128)(2,1)S(1)} collective-permute-done((bf16[64,256]{1,0:T(8,128)(2,1)S(1)}, bf16[64,256]{1,0:T(8,128)(2,1)S(1)}, u32[]{:S(2)}, u32[]{:S(2)}) %collective-permute-start.17) | collective-permute-done | bytes 32800 | tf_op jit(solution)/shard_map/ppermute | solution.py:423
  61.0 2.0 %collective-permute-done.18.refs_2_ = bf16[64,256]{1,0:T(8,128)(2,1)S(1)} collective-permute-done((bf16[64,256]{1,0:T(8,128)(2,1)S(1)}, bf16[64,256]{1,0:T(8,128)(2,1)S(1)}, u32[]{:S(2)}, u32[]{:S(2)}) %collective-permute-start.18) | collective-permute-done | bytes 32800 | tf_op jit(solution)/shard_map/ppermute | solution.py:423
  63.0 0.0 collective-permute-done.19.refs_3_
  63.0 0.1 shard_map.96
  63.1 1.5 %collective-permute-start.20 = (bf16[64,256]{1,0:T(8,128)(2,1)S(1)}, bf16[64,256]{1,0:T(8,128)(2,1)S(1)}, u32[]{:S(2)}, u32[]{:S(2)}) collective-permute-start(bf16[64,256]{1,0:T(8,128)(2,1)S(1)} %shard_map.96), channel_id=1, source_target_pairs={{0,1},{1,0},{2,3},{3,2},{4,5},{5,4},{6,7},{7,6},{8,9},{9,8},{10,11... | collective-permute-start | bytes 98312 | tf_op jit(solution)/shard_map/ppermute | solution.py:418
  64.6 0.9 %collective-permute-done.20 = bf16[64,256]{1,0:T(8,128)(2,1)S(1)} collective-permute-done((bf16[64,256]{1,0:T(8,128)(2,1)S(1)}, bf16[64,256]{1,0:T(8,128)(2,1)S(1)}, u32[]{:S(2)}, u32[]{:S(2)}) %collective-permute-start.20) | collective-permute-done | bytes 32800 | tf_op jit(solution)/shard_map/ppermute | solution.py:418
  65.5 3.8 %collective-permute-start.21 = (bf16[64,384]{1,0:T(8,128)(2,1)S(1)}, bf16[64,384]{1,0:T(8,128)(2,1)S(1)}, u32[]{:S(2)}, u32[]{:S(2)}) collective-permute-start(bf16[64,384]{1,0:T(8,128)(2,1)S(1)} %pad_maximum_fusion.1), channel_id=1, source_target_pairs={{0,0},{4,1},{10,2},{14,3},{2,4},{6,5},{8,6},{12,7},{1,8},{5,9},{11... | collective-permute-start | bytes 147464 | tf_op jit(solution)/shard_map/ppermute | solution.py:458
  69.3 2.8 %collective-permute-start.22 = (bf16[64,384]{1,0:T(8,128)(2,1)S(1)}, bf16[64,384]{1,0:T(8,128)(2,1)S(1)}, u32[]{:S(2)}, u32[]{:S(2)}) collective-permute-start(bf16[64,384]{1,0:T(8,128)(2,1)S(1)} %pad_maximum_fusion.1), channel_id=1, source_target_pairs={{2,0},{6,1},{8,2},{12,3},{0,4},{4,5},{10,6},{14,7},{3,8},{7,9},{9,... | collective-permute-start | bytes 147464 | tf_op jit(solution)/shard_map/ppermute | solution.py:458
  72.1 0.6 collective-permute-done.21.near_ref
  72.8 4.7 %collective-permute-done.22.far_ref = bf16[64,384]{1,0:T(8,128)(2,1)S(1)} collective-permute-done((bf16[64,384]{1,0:T(8,128)(2,1)S(1)}, bf16[64,384]{1,0:T(8,128)(2,1)S(1)}, u32[]{:S(2)}, u32[]{:S(2)}) %collective-permute-start.22) | collective-permute-done | bytes 49184 | tf_op jit(solution)/shard_map/ppermute | solution.py:458
  77.4 1.1 %shard_map.97 = f32[64,768]{1,0:T(8,128)} custom-call(f32[64,768]{1,0:T(8,128)S(1)} %get-tuple-element.32.kept_ref, bf16[64,384]{1,0:T(8,128)(2,1)S(1)} %collective-permute-done.21.near_ref, bf16[64,384]{1,0:T(8,128)(2,1)S(1)} %collective-permute-done.22.far_ref, bf16[2,192,768]{2,1,0:T(8,128)(2,1)S(1)} %copy-done.1, ...), custom_call_target="tpu_custom_call" | custom-call | flops 75497472 | bytes 1048576 | tf_op jit(solution)/shard_map/pallas_call | solution.py:393
  (12 shorter events, 0.1 us)
Async XLA Ops:
  0.0 6.3 %copy-start.3 = (bf16[64,768]{1,0:T(8,128)(2,1)S(1)}, bf16[64,768]{1,0:T(8,128)(2,1)}, u32[]{:S(2)}) copy-start(bf16[64,768]{1,0:T(8,128)(2,1)} %q_ref.3) | copy-start | bytes 294916
  0.0 12.5 %copy-start = (bf16[2,768,192]{1,2,0:T(8,128)(2,1)S(1)}, bf16[2,768,192]{1,2,0:T(8,128)(2,1)}, u32[]{:S(2)}) copy-start(bf16[2,768,192]{1,2,0:T(8,128)(2,1)} %param.15) | copy-start | bytes 1769476
  0.0 12.5 %copy-start.4 = (f32[2,768]{1,0:T(2,128)S(1)}, f32[2,768]{1,0:T(2,128)}, u32[]{:S(2)}) copy-start(f32[2,768]{1,0:T(2,128)} %gain_ref.3) | copy-start | bytes 18436
  0.0 12.5 %copy-start.5 = (f32[6]{0:T(128)S(1)}, f32[6]{0:T(128)}, u32[]{:S(2)}) copy-start(f32[6]{0:T(128)} %scale_ref.3) | copy-start | bytes 76
  5.6 17.9 %copy-start.1 = (bf16[2,192,768]{2,1,0:T(8,128)(2,1)S(1)}, bf16[2,192,768]{2,1,0:T(8,128)(2,1)}, u32[]{:S(2)}) copy-start(bf16[2,192,768]{2,1,0:T(8,128)(2,1)} %wo0.3) | copy-start | bytes 1769476
  5.6 6.9 %collective-permute-start.3 = (bf16[1536,256]{1,0:T(8,128)(2,1)S(1)}, bf16[1536,256]{1,0:T(8,128)(2,1)S(1)}, u32[]{:S(2)}, u32[]{:S(2)}) collective-permute-start(bf16[1536,256]{1,0:T(8,128)(2,1)S(1)} %get-tuple-element.22), channel_id=1, source_target_pairs={{0,1},{1,0},{2,3},{3,2},{4,5},{5,4},{6,7},{7,6},{8,9},{9,8},{10,11... | collective-permute-start | bytes 2359304 | tf_op jit(solution)/shard_map/ppermute | solution.py:418
  6.3 4.3 %collective-permute-start.1 = (bf16[64,768]{1,0:T(8,128)(2,1)S(1)}, bf16[64,768]{1,0:T(8,128)(2,1)S(1)}, u32[]{:S(2)}, u32[]{:S(2)}) collective-permute-start(bf16[64,768]{1,0:T(8,128)(2,1)S(1)} %copy-done.3), channel_id=1, source_target_pairs={{0,2},{2,0},{1,3},{3,1},{4,6},{6,4},{5,7},{7,5},{8,10},{10,8},{9,1... | collective-permute-start | bytes 294920 | tf_op jit(solution)/shard_map/ppermute | solution.py:418
  6.6 5.0 %collective-permute-start = (bf16[64,768]{1,0:T(8,128)(2,1)S(1)}, bf16[64,768]{1,0:T(8,128)(2,1)S(1)}, u32[]{:S(2)}, u32[]{:S(2)}) collective-permute-start(bf16[64,768]{1,0:T(8,128)(2,1)S(1)} %copy-done.3), channel_id=1, source_target_pairs={{0,1},{1,0},{2,3},{3,2},{4,5},{5,4},{6,7},{7,6},{8,9},{9,8},{10,11... | collective-permute-start | bytes 294920 | tf_op jit(solution)/shard_map/ppermute | solution.py:418
  10.6 1.9 %collective-permute-start.2 = (bf16[64,768]{1,0:T(8,128)(2,1)S(1)}, bf16[64,768]{1,0:T(8,128)(2,1)S(1)}, u32[]{:S(2)}, u32[]{:S(2)}) collective-permute-start(bf16[64,768]{1,0:T(8,128)(2,1)S(1)} %collective-permute-done.1.qx_ref), channel_id=1, source_target_pairs={{0,1},{1,0},{2,3},{3,2},{4,5},{5,4},{6,7},{7,6},{8,9},{9,8},{10,11... | collective-permute-start | bytes 294920 | tf_op jit(solution)/shard_map/ppermute | solution.py:418
  15.2 8.6 %collective-permute-start.4 = (bf16[64,256]{1,0:T(8,128)(2,1)S(1)}, bf16[64,256]{1,0:T(8,128)(2,1)S(1)}, u32[]{:S(2)}, u32[]{:S(2)}) collective-permute-start(bf16[64,256]{1,0:T(8,128)(2,1)S(1)} %get-tuple-element.24), channel_id=1, source_target_pairs={{0,12},{4,8},{8,4},{12,0},{1,13},{5,9},{9,5},{13,1},{2,14},{6,10},... | collective-permute-start | bytes 98312 | tf_op jit(solution)/shard_map/ppermute | solution.py:423
  18.6 5.2 %collective-permute-start.5 = (bf16[64,256]{1,0:T(8,128)(2,1)S(1)}, bf16[64,256]{1,0:T(8,128)(2,1)S(1)}, u32[]{:S(2)}, u32[]{:S(2)}) collective-permute-start(bf16[64,256]{1,0:T(8,128)(2,1)S(1)} %get-tuple-element.25), channel_id=1, source_target_pairs={{0,8},{4,12},{8,0},{12,4},{1,9},{5,13},{9,1},{13,5},{2,10},{6,14},... | collective-permute-start | bytes 98312 | tf_op jit(solution)/shard_map/ppermute | solution.py:423
  18.6 5.2 %collective-permute-start.6 = (bf16[64,256]{1,0:T(8,128)(2,1)S(1)}, bf16[64,256]{1,0:T(8,128)(2,1)S(1)}, u32[]{:S(2)}, u32[]{:S(2)}) collective-permute-start(bf16[64,256]{1,0:T(8,128)(2,1)S(1)} %get-tuple-element.26), channel_id=1, source_target_pairs={{0,4},{4,0},{8,12},{12,8},{1,5},{5,1},{9,13},{13,9},{2,6},{6,2},{1... | collective-permute-start | bytes 98312 | tf_op jit(solution)/shard_map/ppermute | solution.py:423
  21.6 0.9 %copy-start.2 = (bf16[1536,256]{1,0:T(8,128)(2,1)}, bf16[1536,256]{1,0:T(8,128)(2,1)S(1)}, u32[]{:S(2)}) copy-start(bf16[1536,256]{1,0:T(8,128)(2,1)S(1)} %get-tuple-element.30.own_hbm) | copy-start | bytes 2359300
  22.4 28.2 %collective-permute-start.16 = (bf16[1536,256]{1,0:T(8,128)(2,1)S(1)}, bf16[1536,256]{1,0:T(8,128)(2,1)}, u32[]{:S(2)}, u32[]{:S(2)}) collective-permute-start(bf16[1536,256]{1,0:T(8,128)(2,1)S(1)} %get-tuple-element.31), channel_id=1, source_target_pairs={{0,1},{1,0},{2,3},{3,2},{4,5},{5,4},{6,7},{7,6},{8,9},{9,8},{10,11... | collective-permute-start | bytes 2359304 | tf_op jit(solution)/shard_map/ppermute | solution.py:418
  23.5 15.4 %collective-permute-start.14 = (bf16[2,192,768]{2,1,0:T(8,128)(2,1)S(1)}, bf16[2,192,768]{2,1,0:T(8,128)(2,1)S(1)}, u32[]{:S(2)}, u32[]{:S(2)}) collective-permute-start(bf16[2,192,768]{2,1,0:T(8,128)(2,1)S(1)} %copy-done.1), channel_id=1, source_target_pairs={{0,2},{2,0},{1,3},{3,1},{4,6},{6,4},{5,7},{7,5},{8,10},{10,8},{9,1... | collective-permute-start | bytes 1769480 | tf_op jit(solution)/shard_map/ppermute | solution.py:418
  23.9 1.6 %collective-permute-start.7 = (bf16[64,256]{1,0:T(8,128)(2,1)S(1)}, bf16[64,256]{1,0:T(8,128)(2,1)S(1)}, u32[]{:S(2)}, u32[]{:S(2)}) collective-permute-start(bf16[64,256]{1,0:T(8,128)(2,1)S(1)} %shard_map.93), channel_id=1, source_target_pairs={{0,1},{1,0},{2,3},{3,2},{4,5},{5,4},{6,7},{7,6},{8,9},{9,8},{10,11... | collective-permute-start | bytes 98312 | tf_op jit(solution)/shard_map/ppermute | solution.py:418
  25.6 16.0 %collective-permute-start.8 = (bf16[64,384]{1,0:T(8,128)(2,1)S(1)}, bf16[64,384]{1,0:T(8,128)(2,1)S(1)}, u32[]{:S(2)}, u32[]{:S(2)}) collective-permute-start(bf16[64,384]{1,0:T(8,128)(2,1)S(1)} %pad_maximum_fusion.block_ref), channel_id=1, source_target_pairs={{0,14},{1,13},{2,12},{3,15},{4,10},{5,9},{6,8},{7,11},{8,6},{9,5},... | collective-permute-start | bytes 147464 | tf_op jit(solution)/shard_map/ppermute | solution.py:447
  29.0 21.7 %collective-permute-start.13 = (bf16[2,192,768]{2,1,0:T(8,128)(2,1)S(1)}, bf16[2,192,768]{2,1,0:T(8,128)(2,1)S(1)}, u32[]{:S(2)}, u32[]{:S(2)}) collective-permute-start(bf16[2,192,768]{2,1,0:T(8,128)(2,1)S(1)} %copy-done.1), channel_id=1, source_target_pairs={{0,1},{1,0},{2,3},{3,2},{4,5},{5,4},{6,7},{7,6},{8,9},{9,8},{10,11... | collective-permute-start | bytes 1769480 | tf_op jit(solution)/shard_map/ppermute | solution.py:418
  38.9 13.2 %collective-permute-start.15 = (bf16[2,192,768]{2,1,0:T(8,128)(2,1)S(1)}, bf16[2,192,768]{2,1,0:T(8,128)(2,1)S(1)}, u32[]{:S(2)}, u32[]{:S(2)}) collective-permute-start(bf16[2,192,768]{2,1,0:T(8,128)(2,1)S(1)} %collective-permute-done.14.wo2), channel_id=1, source_target_pairs={{0,1},{1,0},{2,3},{3,2},{4,5},{5,4},{6,7},{7,6},{8,9},{9,8},{10,11... | collective-permute-start | bytes 1769480 | tf_op jit(solution)/shard_map/ppermute | solution.py:418
  39.8 6.0 %collective-permute-start.9 = (bf16[64,384]{1,0:T(8,128)(2,1)S(1)}, bf16[64,384]{1,0:T(8,128)(2,1)S(1)}, u32[]{:S(2)}, u32[]{:S(2)}) collective-permute-start(bf16[64,384]{1,0:T(8,128)(2,1)S(1)} %pad_maximum_fusion.block_ref), channel_id=1, source_target_pairs={{0,8},{1,11},{2,10},{3,9},{4,12},{5,15},{6,14},{7,13},{8,0},{9,3},... | collective-permute-start | bytes 147464 | tf_op jit(solution)/shard_map/ppermute | solution.py:447
  41.6 6.1 %collective-permute-start.10 = (bf16[64,384]{1,0:T(8,128)(2,1)S(1)}, bf16[64,384]{1,0:T(8,128)(2,1)S(1)}, u32[]{:S(2)}, u32[]{:S(2)}) collective-permute-start(bf16[64,384]{1,0:T(8,128)(2,1)S(1)} %pad_maximum_fusion.block_ref), channel_id=1, source_target_pairs={{0,6},{1,5},{2,4},{3,7},{4,2},{5,1},{6,0},{7,3},{8,14},{9,13},{10,... | collective-permute-start | bytes 147464 | tf_op jit(solution)/shard_map/ppermute | solution.py:447
  45.7 4.8 %collective-permute-start.11 = (bf16[64,384]{1,0:T(8,128)(2,1)S(1)}, bf16[64,384]{1,0:T(8,128)(2,1)S(1)}, u32[]{:S(2)}, u32[]{:S(2)}) collective-permute-start(bf16[64,384]{1,0:T(8,128)(2,1)S(1)} %pad_maximum_fusion.block_ref), channel_id=1, source_target_pairs={{1,3},{3,1},{5,7},{7,5},{9,11},{11,9},{13,15},{15,13},{17,19},{19,... | collective-permute-start | bytes 147464 | tf_op jit(solution)/shard_map/ppermute | solution.py:447
  50.6 1.5 %collective-permute-start.12 = (bf16[256,384]{1,0:T(8,128)(2,1)S(1)}, bf16[256,384]{1,0:T(8,128)(2,1)S(1)}, u32[]{:S(2)}, u32[]{:S(2)}) collective-permute-start(bf16[256,384]{1,0:T(8,128)(2,1)S(1)} %constant_dynamic-update-slice_fusion.near_ref), channel_id=1, source_target_pairs={{0,1},{1,0},{2,3},{3,2},{4,5},{5,4},{6,7},{7,6},{8,9},{9,8},{10,11... | collective-permute-start | bytes 589832 | tf_op jit(solution)/shard_map/ppermute | solution.py:418
  56.4 4.6 %collective-permute-start.17 = (bf16[64,256]{1,0:T(8,128)(2,1)S(1)}, bf16[64,256]{1,0:T(8,128)(2,1)S(1)}, u32[]{:S(2)}, u32[]{:S(2)}) collective-permute-start(bf16[64,256]{1,0:T(8,128)(2,1)S(1)} %get-tuple-element.34), channel_id=1, source_target_pairs={{0,12},{4,8},{8,4},{12,0},{1,13},{5,9},{9,5},{13,1},{2,14},{6,10},... | collective-permute-start | bytes 98312 | tf_op jit(solution)/shard_map/ppermute | solution.py:423
  59.2 3.8 %collective-permute-start.18 = (bf16[64,256]{1,0:T(8,128)(2,1)S(1)}, bf16[64,256]{1,0:T(8,128)(2,1)S(1)}, u32[]{:S(2)}, u32[]{:S(2)}) collective-permute-start(bf16[64,256]{1,0:T(8,128)(2,1)S(1)} %get-tuple-element.35), channel_id=1, source_target_pairs={{0,8},{4,12},{8,0},{12,4},{1,9},{5,13},{9,1},{13,5},{2,10},{6,14},... | collective-permute-start | bytes 98312 | tf_op jit(solution)/shard_map/ppermute | solution.py:423
  59.2 3.8 %collective-permute-start.19 = (bf16[64,256]{1,0:T(8,128)(2,1)S(1)}, bf16[64,256]{1,0:T(8,128)(2,1)S(1)}, u32[]{:S(2)}, u32[]{:S(2)}) collective-permute-start(bf16[64,256]{1,0:T(8,128)(2,1)S(1)} %get-tuple-element.36), channel_id=1, source_target_pairs={{0,4},{4,0},{8,12},{12,8},{1,5},{5,1},{9,13},{13,9},{2,6},{6,2},{1... | collective-permute-start | bytes 98312 | tf_op jit(solution)/shard_map/ppermute | solution.py:423
  63.1 2.4 %collective-permute-start.20 = (bf16[64,256]{1,0:T(8,128)(2,1)S(1)}, bf16[64,256]{1,0:T(8,128)(2,1)S(1)}, u32[]{:S(2)}, u32[]{:S(2)}) collective-permute-start(bf16[64,256]{1,0:T(8,128)(2,1)S(1)} %shard_map.96), channel_id=1, source_target_pairs={{0,1},{1,0},{2,3},{3,2},{4,5},{5,4},{6,7},{7,6},{8,9},{9,8},{10,11... | collective-permute-start | bytes 98312 | tf_op jit(solution)/shard_map/ppermute | solution.py:418
  65.5 7.2 %collective-permute-start.21 = (bf16[64,384]{1,0:T(8,128)(2,1)S(1)}, bf16[64,384]{1,0:T(8,128)(2,1)S(1)}, u32[]{:S(2)}, u32[]{:S(2)}) collective-permute-start(bf16[64,384]{1,0:T(8,128)(2,1)S(1)} %pad_maximum_fusion.1), channel_id=1, source_target_pairs={{0,0},{4,1},{10,2},{14,3},{2,4},{6,5},{8,6},{12,7},{1,8},{5,9},{11... | collective-permute-start | bytes 147464 | tf_op jit(solution)/shard_map/ppermute | solution.py:458
  69.3 8.1 %collective-permute-start.22 = (bf16[64,384]{1,0:T(8,128)(2,1)S(1)}, bf16[64,384]{1,0:T(8,128)(2,1)S(1)}, u32[]{:S(2)}, u32[]{:S(2)}) collective-permute-start(bf16[64,384]{1,0:T(8,128)(2,1)S(1)} %pad_maximum_fusion.1), channel_id=1, source_target_pairs={{2,0},{6,1},{8,2},{12,3},{0,4},{4,5},{10,6},{14,7},{3,8},{7,9},{9,... | collective-permute-start | bytes 147464 | tf_op jit(solution)/shard_map/ppermute | solution.py:458

commit v2 on v1

--- a/solution.py
+++ b/solution.py
@@ -117,6 +117,7 @@
             tuple(offsets[i + (k + i // self.n_k) % self.n_k] for k in range(self.n_k))
             for i in range(0, len(offsets), self.n_k)
         ]
+        self.rounds = self.rounds[-1:] + self.rounds[:-1]
 
     def usable(self):
         return (
@@ -166,8 +167,9 @@
     return rows * (2 if slots % 2 == 0 else 1)
 
 
-def load_project_kernel(
+def project_kernel(
     plan,
+    layer,
     count_ref,
     feats_hbm,
     weights_hbm,
@@ -175,24 +177,22 @@
     own_ref,
     other_ref,
     feats_ref,
-    later_ref,
-    live_ref,
     weights_ref,
     mask_ref,
+    live_ref,
     sems,
 ):
     size = group_of(live_ref)
     groups = feats_ref.shape[0] // size
     copies = [
-        pltpu.make_async_copy(mask_hbm, mask_ref, sems.at[groups + 2]),
-        pltpu.make_async_copy(weights_hbm.at[0], weights_ref, sems.at[groups]),
+        pltpu.make_async_copy(mask_hbm, mask_ref, sems.at[groups + 1]),
+        pltpu.make_async_copy(weights_hbm.at[layer], weights_ref, sems.at[groups]),
     ]
     for index in range(groups):
         at = pl.ds(index * size, size)
         copies.append(
             pltpu.make_async_copy(feats_hbm.at[at], feats_ref.at[at], sems.at[index])
         )
-    copies.append(pltpu.make_async_copy(weights_hbm.at[1], later_ref, sems.at[groups + 1]))
     for copy in copies:
         copy.start()
     copies[0].wait()
@@ -203,13 +203,6 @@
     for index in range(groups):
         copies[2 + index].wait()
         low = index * size
-        project_rows(plan, live_ref, feats_ref, weights_ref, own_ref, other_ref, low, low + size)
-    copies[-1].wait()
-
-
-def project_kernel(plan, live_ref, feats_ref, weights_ref, own_ref, other_ref):
-    size = group_of(live_ref)
-    for low in range(0, feats_ref.shape[0], size):
         project_rows(plan, live_ref, feats_ref, weights_ref, own_ref, other_ref, low, low + size)
 
 
@@ -320,18 +313,12 @@
     wo3,
     gain_ref,
     wq_ref,
-    own_hbm,
-    recv_hbm,
+    own_ref,
+    recv_ref,
     *rest,
 ):
     chunks, rest = rest[: plan.n_t], rest[plan.n_t :]
-    kept_ref, att, wo_all, states_ref, wq_pad, mix, own_ref, recv_ref, sems = rest
-    copies = [
-        pltpu.make_async_copy(own_hbm, own_ref, sems.at[0]),
-        pltpu.make_async_copy(recv_hbm, recv_ref, sems.at[1]),
-    ]
-    for copy in copies:
-        copy.start()
+    kept_ref, att, wo_all, states_ref, wq_pad, mix = rest
     me_t, me_h, me_k = place()
     rows = plan.n_q // plan.n_t
     fill_out(plan, layer - 1, (wo0, wo1, wo2, wo3), wo_all)
@@ -350,8 +337,6 @@
     states_ref[...] = states
     kept_ref[...] = states_ref[rows_at(me_h * plan.n_k + me_k, plan.q_rows), :]
     query = query_of(plan, states, gain_ref[layer : layer + 1, :], wq_ref[layer], wq_pad)
-    for copy in copies:
-        copy.wait()
     attend(plan, query, scale_ref, own_ref, recv_ref, chunks, mix)
 
 
@@ -359,7 +344,7 @@
     me_t = lax.axis_index("tiles")
     fill_out(plan, layer, (wo0, wo1, wo2, wo3), wo_all)
     for index, ref in enumerate((near_ref, far_ref)):
-        att[:, rows_at((me_t + index) % plan.n_h, plan.cols)] = ref[...]
+        att[:, rows_at((me_t // plan.n_k + index) % plan.n_h, plan.cols)] = ref[...]
     out = jnp.dot(att[...], wo_all[...], preferred_element_type=jnp.float32)
     out_ref[...] = kept_ref[...] + out
 
@@ -394,7 +379,9 @@
         kernel,
         out_shape=out_shape,
         in_specs=specs,
-        out_specs=jax.tree.map(lambda _: pl.BlockSpec(memory_space=pltpu.VMEM), out_shape),
+        out_specs=[pl.BlockSpec(memory_space=pltpu.VMEM) for _ in out_shape]
+        if isinstance(out_shape, list)
+        else pl.BlockSpec(memory_space=pltpu.VMEM),
         scratch_shapes=scratch,
         cost_estimate=pl.CostEstimate(flops=flops, bytes_accessed=1 << 20, transcendentals=0),
         compiler_params=pltpu.CompilerParams(vmem_limit_bytes=grant),
@@ -453,8 +440,10 @@
         for turn in range(plan.n_h):
             links = []
             for t, h, k in devices:
-                source_t, source_h = h * plan.n_k + k, h ^ ((turn + t) % plan.n_h)
-                links.append((number(source_t, source_h, (t // plan.n_h) % plan.n_k), number(t, h, k)))
+                source_t = h * plan.n_k + k
+                source_h = h ^ ((turn + t // plan.n_k) % plan.n_h)
+                source_k = plan.n_k - 1 - t % plan.n_k
+                links.append((number(source_t, source_h, source_k), number(t, h, k)))
             received.append(lax.ppermute(block, axes, links))
         return received
 
@@ -470,39 +459,27 @@
     feat = features.shape[1]
     piece = jax.ShapeDtypeStruct((tiles, plan.width), bf16)
     cost = 2 * tiles * feat * plan.cols
-    live_shape = jax.ShapeDtypeStruct(tile_mask.shape, f32)
-    own, other, near_tiles, later, live = vmem_call(
-        functools.partial(load_project_kernel, plan),
-        [
-            piece,
-            piece,
-            jax.ShapeDtypeStruct((tiles, feat), bf16),
-            jax.ShapeDtypeStruct((feat, plan.cols), bf16),
-            live_shape,
-        ],
-        [counts],
-        [],
-        [
-            pltpu.VMEM((feat, plan.cols), bf16),
-            pltpu.VMEM(tile_mask.shape, jnp.int32),
-        ],
-        cost,
-        [
-            pltpu.with_memory_space_constraint(a, pltpu.HBM)
-            for a in (features, weights, tile_mask)
-        ],
-        tile_mask.shape[0] + 3,
-    )
-    pairs = [(own, swap(other, "kv"))]
-    own, other = vmem_call(
-        functools.partial(project_kernel, plan),
-        [piece, piece],
-        [],
-        [live, near_tiles, later],
-        [],
-        cost,
-    )
-    pairs.append((own, swap(other, "kv")))
+    streamed = [
+        pltpu.with_memory_space_constraint(a, pltpu.HBM) for a in (features, weights, tile_mask)
+    ]
+    pairs = []
+    for layer in range(layer_count):
+        own, other = vmem_call(
+            functools.partial(project_kernel, plan, layer),
+            [piece, piece],
+            [counts],
+            [],
+            [
+                pltpu.VMEM((tiles, feat), bf16),
+                pltpu.VMEM((feat, plan.cols), bf16),
+                pltpu.VMEM(tile_mask.shape, jnp.int32),
+                pltpu.VMEM(tile_mask.shape, f32),
+            ],
+            cost,
+            streamed,
+            tile_mask.shape[0] + 2,
+        )
+        pairs.append((own, swap(other, "kv")))
 
     chunk_shapes = [jax.ShapeDtypeStruct((rows, plan.width), f32)]
     chunk_shapes += [jax.ShapeDtypeStruct((rows, plan.width), bf16)] * (plan.n_t - 1)
@@ -526,19 +503,16 @@
         functools.partial(layer_kernel, plan, 1),
         chunk_shapes + [jax.ShapeDtypeStruct((plan.q_rows, plan.dq), f32)],
         [head_scale],
-        [queries, q_k, q_x, q_xk, block, near, far, *wo, norm_gain, wq],
+        [queries, q_k, q_x, q_xk, block, near, far, *wo, norm_gain, wq]
+        + [pltpu.with_memory_space_constraint(a, pltpu.VMEM) for a in pairs[1]],
         [
             pltpu.VMEM((plan.n_q, plan.n_h * plan.cols), bf16),
             wo_scratch,
             states_scratch,
             wq_scratch,
             mix_scratch,
-            pltpu.VMEM((tiles, plan.width), bf16),
-            pltpu.VMEM((tiles, plan.width), bf16),
         ],
         work,
-        [pltpu.with_memory_space_constraint(a, pltpu.HBM) for a in pairs[1]],
-        2,
     )
     chunks, kept = outs[: plan.n_t], outs[plan.n_t]
     block = exchange(chunks)

time: 78.8 us -> 79.4 us (level)
  the two profiles are of different devices: /device:TPU:7 before, /device:TPU:0 now
where the time goes in v2:
time: 79.4 us; the launch traced here: 78 us
  waiting for transfers between devices  31.8 us (40%)
  starting transfers between devices  24.4 us (31%)
  Pallas kernels  18.2 us (23%)
  local copies, waits for them, and re-layouts  1.85 us (2%)
  between operations  0.91 us (1%)
  other arithmetic  0.83 us (1%)
    pallas_call x7, Pallas kernels, vmem_call(): pl.pallas_call(kernel, out_shape=out_shape, in_specs=specs, out_specs=[pl...  18.2 us
    ppermute x11, waiting for transfers between devices, swap(): return lax.ppermute(value, axis, [(i, i ^ 1) for i in range(size)])  17.7 us
    ppermute x6, starting transfers between devices, exchange(): lax.ppermute(chunks[d], 'tiles', [(i, i ^ d) for i in range(plan.n_t)])  9.19 us
    ppermute x4, waiting for transfers between devices, spread(): received.append(lax.ppermute(block, axes, links))  7.16 us
    ppermute x11, starting transfers between devices, swap(): return lax.ppermute(value, axis, [(i, i ^ 1) for i in range(size)])  6.91 us
    ppermute x4, starting transfers between devices, spread(): received.append(lax.ppermute(block, axes, links))  5.71 us
    ppermute x6, waiting for transfers between devices, exchange(): lax.ppermute(chunks[d], 'tiles', [(i, i ^ d) for i in range(plan.n_t)])  4.18 us
    ppermute x2, waiting for transfers between devices, collect(): received.append(lax.ppermute(block, axes, links))  2.75 us
  transfers between devices with their start and end apart: 23, of which 12 were waited for; matrix products, arithmetic and copies ran while one was open for 1% of the time, Pallas kernels for 8%

profile of v2, /device:TPU:0, one launch (start us, length us, event | category | flops | bytes accessed | tf_op | source)
XLA Modules:
  0.0 78.0 jit_solution(7478837491766141729)
XLA Ops:
  0.7 4.8 %shard_map.91 = (bf16[1536,256]{1,0:T(8,128)(2,1)S(1)}, bf16[1536,256]{1,0:T(8,128)(2,1)S(1)}) custom-call(s32[1]{0:T(128)S(6)} %copy.13.count_ref, bf16[1536,1536]{1,0:T(8,128)(2,1)} %feats_hbm.3, bf16[2,1536,384]{2,1,0:T(8,128)(2,1)} %bitcast.4, s32[6,256]{1,0:T(8,128)} %mask_hbm.3), custom_call_target="tpu_custom_call" | custom-call | flops 1811939328 | bytes 1048576 | tf_op jit(solution)/shard_map/pallas_call | solution.py:378
  5.5 0.6 collective-permute-start.3
  6.1 0.0 copy-done.2
  6.1 2.6 %collective-permute-start.1 = (bf16[64,768]{1,0:T(8,128)(2,1)S(1)}, bf16[64,768]{1,0:T(8,128)(2,1)S(1)}, u32[]{:S(2)}, u32[]{:S(2)}) collective-permute-start(bf16[64,768]{1,0:T(8,128)(2,1)S(1)} %copy-done.2), channel_id=1, source_target_pairs={{0,2},{2,0},{1,3},{3,1},{4,6},{6,4},{5,7},{7,5},{8,10},{10,8},{9,1... | collective-permute-start | bytes 294920 | tf_op jit(solution)/shard_map/ppermute | solution.py:405
  8.7 0.1 collective-permute-start
  8.8 3.2 %collective-permute-done.1.qx_ref = bf16[64,768]{1,0:T(8,128)(2,1)S(1)} collective-permute-done((bf16[64,768]{1,0:T(8,128)(2,1)S(1)}, bf16[64,768]{1,0:T(8,128)(2,1)S(1)}, u32[]{:S(2)}, u32[]{:S(2)}) %collective-permute-start.1) | collective-permute-done | bytes 98336 | tf_op jit(solution)/shard_map/ppermute | solution.py:405
  12.0 0.0 collective-permute-start.2
  12.0 0.0 collective-permute-done.qk_ref
  12.1 1.3 %collective-permute-done.2.qxk_ref = bf16[64,768]{1,0:T(8,128)(2,1)S(1)} collective-permute-done((bf16[64,768]{1,0:T(8,128)(2,1)S(1)}, bf16[64,768]{1,0:T(8,128)(2,1)S(1)}, u32[]{:S(2)}, u32[]{:S(2)}) %collective-permute-start.2) | collective-permute-done | bytes 98336 | tf_op jit(solution)/shard_map/ppermute | solution.py:405
  13.3 0.0 collective-permute-done.3.recv_ref
  13.4 0.0 copy-done
  13.4 0.0 copy-done.7
  13.4 0.0 copy-done.8
  13.4 0.0 copy-start.1
  13.4 2.7 %shard_map.92 = (f32[64,256]{1,0:T(8,128)S(1)}, bf16[64,256]{1,0:T(8,128)(2,1)S(1)}, bf16[64,256]{1,0:T(8,128)(2,1)S(1)}, bf16[64,256]{1,0:T(8,128)(2,1)S(1)}) custom-call(f32[6]{0:T(128)S(1)} %copy-done.8, bf16[64,768]{1,0:T(8,128)(2,1)S(1)} %copy-done.2, bf16[64,768]{1,0:T(8,128)(2,1)S(1)} %collective-permute-done.qk_ref, ...), custom_call_target="tpu_custom_call" | custom-call | flops 402653184 | bytes 1048576 | tf_op jit(solution)/shard_map/pallas_call | solution.py:378
  16.1 3.9 %collective-permute-start.4 = (bf16[64,256]{1,0:T(8,128)(2,1)S(1)}, bf16[64,256]{1,0:T(8,128)(2,1)S(1)}, u32[]{:S(2)}, u32[]{:S(2)}) collective-permute-start(bf16[64,256]{1,0:T(8,128)(2,1)S(1)} %get-tuple-element.21), channel_id=1, source_target_pairs={{0,12},{4,8},{8,4},{12,0},{1,13},{5,9},{9,5},{13,1},{2,14},{6,10},... | collective-permute-start | bytes 98312 | tf_op jit(solution)/shard_map/ppermute | solution.py:410
  20.0 0.0 collective-permute-start.5
  20.0 0.0 copy-done.3
  20.0 0.0 copy-done.5
  20.0 0.6 collective-permute-start.6
  20.7 5.7 %shard_map.94 = (bf16[1536,256]{1,0:T(8,128)(2,1)S(1)}, bf16[1536,256]{1,0:T(8,128)(2,1)}) custom-call(s32[1]{0:T(128)S(6)} %copy.13.count_ref, bf16[1536,1536]{1,0:T(8,128)(2,1)} %feats_hbm.3, bf16[2,1536,384]{2,1,0:T(8,128)(2,1)} %bitcast.5, s32[6,256]{1,0:T(8,128)} %mask_hbm.3), custom_call_target="tpu_custom_call" | custom-call | flops 1811939328 | bytes 1048576 | tf_op jit(solution)/shard_map/pallas_call | solution.py:378
  26.3 0.1 collective-permute-start.16
  26.4 0.0 copy-done.1
  26.4 1.7 %collective-permute-start.14 = (bf16[2,192,768]{2,1,0:T(8,128)(2,1)S(1)}, bf16[2,192,768]{2,1,0:T(8,128)(2,1)S(1)}, u32[]{:S(2)}, u32[]{:S(2)}) collective-permute-start(bf16[2,192,768]{2,1,0:T(8,128)(2,1)S(1)} %copy-done.1), channel_id=1, source_target_pairs={{0,2},{2,0},{1,3},{3,1},{4,6},{6,4},{5,7},{7,5},{8,10},{10,8},{9,1... | collective-permute-start | bytes 1769480 | tf_op jit(solution)/shard_map/ppermute | solution.py:405
  28.1 0.0 collective-permute-done.4.refs_1_
  28.1 0.0 collective-permute-done.5.refs_2_
  28.1 0.0 collective-permute-done.6.refs_3_
  28.1 0.7 shard_map.93
  28.9 0.1 collective-permute-start.7
  29.0 1.4 %collective-permute-done.7 = bf16[64,256]{1,0:T(8,128)(2,1)} collective-permute-done((bf16[64,256]{1,0:T(8,128)(2,1)}, bf16[64,256]{1,0:T(8,128)(2,1)}, u32[]{:S(2)}, u32[]{:S(2)}) %collective-permute-start.7) | collective-permute-done | bytes 32800 | tf_op jit(solution)/shard_map/ppermute | solution.py:405
  30.4 0.8 %broadcast_select_fusion.3 = (bf16[64,256]{1,0:T(8,128)(2,1)S(1)}, bf16[64,256]{1,0:T(8,128)(2,1)S(1)}) fusion(bf16[64,256]{1,0:T(8,128)(2,1)} %shard_map.93, bf16[64,256]{1,0:T(8,128)(2,1)} %collective-permute-done.7, pred[]{:T(512)S(6)} %eq.2), kind=kLoop, calls=%fused_computation.5 | loop fusion | flops 32768 | bytes 131073 | tf_op jit(solution)/shard_map/jit(_where)/select_n | solution.py:416
  31.2 0.7 collective-permute-start.8
  31.9 1.6 %collective-permute-start.13 = (bf16[2,192,768]{2,1,0:T(8,128)(2,1)S(1)}, bf16[2,192,768]{2,1,0:T(8,128)(2,1)S(1)}, u32[]{:S(2)}, u32[]{:S(2)}) collective-permute-start(bf16[2,192,768]{2,1,0:T(8,128)(2,1)S(1)} %copy-done.1), channel_id=1, source_target_pairs={{0,1},{1,0},{2,3},{3,2},{4,5},{5,4},{6,7},{7,6},{8,9},{9,8},{10,11... | collective-permute-start | bytes 1769480 | tf_op jit(solution)/shard_map/ppermute | solution.py:405
  33.5 9.2 %collective-permute-done.14.wo2 = bf16[2,192,768]{2,1,0:T(8,128)(2,1)S(1)} collective-permute-done((bf16[2,192,768]{2,1,0:T(8,128)(2,1)S(1)}, bf16[2,192,768]{2,1,0:T(8,128)(2,1)S(1)}, u32[]{:S(2)}, u32[]{:S(2)}) %collective-permute-start.14) | collective-permute-done | bytes 589856 | tf_op jit(solution)/shard_map/ppermute | solution.py:405
  42.7 0.0 collective-permute-start.15
  42.7 4.7 %collective-permute-start.9 = (bf16[64,384]{1,0:T(8,128)(2,1)S(1)}, bf16[64,384]{1,0:T(8,128)(2,1)S(1)}, u32[]{:S(2)}, u32[]{:S(2)}) collective-permute-start(bf16[64,384]{1,0:T(8,128)(2,1)S(1)} %pad_maximum_fusion.block_ref), channel_id=1, source_target_pairs={{0,14},{1,13},{2,12},{3,15},{4,10},{5,9},{6,8},{7,11},{8,6},{9,5},... | collective-permute-start | bytes 147464 | tf_op jit(solution)/shard_map/ppermute | solution.py:434
  47.4 0.0 collective-permute-done.8
  47.4 0.0 collective-permute-start.10
  47.4 2.6 %collective-permute-done.9 = bf16[64,384]{1,0:T(8,128)(2,1)S(1)} collective-permute-done((bf16[64,384]{1,0:T(8,128)(2,1)S(1)}, bf16[64,384]{1,0:T(8,128)(2,1)S(1)}, u32[]{:S(2)}, u32[]{:S(2)}) %collective-permute-start.9) | collective-permute-done | bytes 49184 | tf_op jit(solution)/shard_map/ppermute | solution.py:434
  49.9 0.4 collective-permute-start.11
  50.3 2.0 %collective-permute-done.10 = bf16[64,384]{1,0:T(8,128)(2,1)S(1)} collective-permute-done((bf16[64,384]{1,0:T(8,128)(2,1)S(1)}, bf16[64,384]{1,0:T(8,128)(2,1)S(1)}, u32[]{:S(2)}, u32[]{:S(2)}) %collective-permute-start.10) | collective-permute-done | bytes 49184 | tf_op jit(solution)/shard_map/ppermute | solution.py:434
  52.4 2.6 %collective-permute-done.11 = bf16[64,384]{1,0:T(8,128)(2,1)S(1)} collective-permute-done((bf16[64,384]{1,0:T(8,128)(2,1)S(1)}, bf16[64,384]{1,0:T(8,128)(2,1)S(1)}, u32[]{:S(2)}, u32[]{:S(2)}) %collective-permute-start.11) | collective-permute-done | bytes 49184 | tf_op jit(solution)/shard_map/ppermute | solution.py:434
  54.9 0.1 collective-permute-start.12
  55.0 0.0 collective-permute-done.13.wo1
  55.0 0.0 collective-permute-done.16.recv_ref
  55.0 1.4 %collective-permute-done.12.far_ref = bf16[256,384]{1,0:T(8,128)(2,1)S(1)} collective-permute-done((bf16[256,384]{1,0:T(8,128)(2,1)S(1)}, bf16[256,384]{1,0:T(8,128)(2,1)S(1)}, u32[]{:S(2)}, u32[]{:S(2)}) %collective-permute-start.12) | collective-permute-done | bytes 196640 | tf_op jit(solution)/shard_map/ppermute | solution.py:405
  56.4 0.0 collective-permute-done.15.wo3
  56.4 0.9 %copy-done.4 = bf16[64,768]{1,0:T(8,128)(2,1)S(1)} copy-done((bf16[64,768]{1,0:T(8,128)(2,1)S(1)}, bf16[64,768]{1,0:T(8,128)(2,1)}, u32[]{:S(2)}) %copy-start.4) | copy-done | bytes 98328
  57.3 0.9 %copy-done.6 = bf16[64,768]{1,0:T(8,128)(2,1)S(1)} copy-done((bf16[64,768]{1,0:T(8,128)(2,1)S(1)}, bf16[64,768]{1,0:T(8,128)(2,1)}, u32[]{:S(2)}) %copy-start.6) | copy-done | bytes 98328
  58.2 3.0 %shard_map.95 = (f32[64,256]{1,0:T(8,128)S(1)}, bf16[64,256]{1,0:T(8,128)(2,1)S(1)}, bf16[64,256]{1,0:T(8,128)(2,1)S(1)}, bf16[64,256]{1,0:T(8,128)(2,1)S(1)}, f32[64,768]{1,0:T(8,128)S(1)}) custom-call(f32[6]{0:T(128)S(1)} %copy-done.8, bf16[64,768]{1,0:T(8,128)(2,1)S(1)} %copy-done.2, bf16[64,768]{1,0:T(8,128)(2,1)S(1)} %copy-done.4, ...), custom_call_target="tpu_custom_call" | custom-call | flops 402653184 | bytes 1048576 | tf_op jit(solution)/shard_map/pallas_call | solution.py:378
  61.3 4.0 %collective-permute-start.17 = (bf16[64,256]{1,0:T(8,128)(2,1)S(1)}, bf16[64,256]{1,0:T(8,128)(2,1)S(1)}, u32[]{:S(2)}, u32[]{:S(2)}) collective-permute-start(bf16[64,256]{1,0:T(8,128)(2,1)S(1)} %get-tuple-element.28), channel_id=1, source_target_pairs={{0,12},{4,8},{8,4},{12,0},{1,13},{5,9},{9,5},{13,1},{2,14},{6,10},... | collective-permute-start | bytes 98312 | tf_op jit(solution)/shard_map/ppermute | solution.py:410
  65.3 0.0 collective-permute-start.18
  65.3 0.6 collective-permute-start.19
  65.9 1.4 %collective-permute-done.17.refs_1_ = bf16[64,256]{1,0:T(8,128)(2,1)S(1)} collective-permute-done((bf16[64,256]{1,0:T(8,128)(2,1)S(1)}, bf16[64,256]{1,0:T(8,128)(2,1)S(1)}, u32[]{:S(2)}, u32[]{:S(2)}) %collective-permute-start.17) | collective-permute-done | bytes 32800 | tf_op jit(solution)/shard_map/ppermute | solution.py:410
  67.3 2.7 %collective-permute-done.18.refs_2_ = bf16[64,256]{1,0:T(8,128)(2,1)S(1)} collective-permute-done((bf16[64,256]{1,0:T(8,128)(2,1)S(1)}, bf16[64,256]{1,0:T(8,128)(2,1)S(1)}, u32[]{:S(2)}, u32[]{:S(2)}) %collective-permute-start.18) | collective-permute-done | bytes 32800 | tf_op jit(solution)/shard_map/ppermute | solution.py:410
  70.1 0.0 collective-permute-done.19.refs_3_
  70.1 0.1 shard_map.96
  70.2 0.1 collective-permute-start.20
  70.3 1.2 %collective-permute-done.20 = bf16[64,256]{1,0:T(8,128)(2,1)S(1)} collective-permute-done((bf16[64,256]{1,0:T(8,128)(2,1)S(1)}, bf16[64,256]{1,0:T(8,128)(2,1)S(1)}, u32[]{:S(2)}, u32[]{:S(2)}) %collective-permute-start.20) | collective-permute-done | bytes 32800 | tf_op jit(solution)/shard_map/ppermute | solution.py:405
  71.5 0.1 collective-permute-start.21
  71.6 2.5 %collective-permute-start.22 = (bf16[64,384]{1,0:T(8,128)(2,1)S(1)}, bf16[64,384]{1,0:T(8,128)(2,1)S(1)}, u32[]{:S(2)}, u32[]{:S(2)}) collective-permute-start(bf16[64,384]{1,0:T(8,128)(2,1)S(1)} %pad_maximum_fusion.1), channel_id=1, source_target_pairs={{3,0},{7,1},{9,2},{13,3},{2,4},{6,5},{8,6},{12,7},{1,8},{5,9},{11,... | collective-permute-start | bytes 147464 | tf_op jit(solution)/shard_map/ppermute | solution.py:447
  74.1 0.0 collective-permute-done.21.near_ref
  74.1 2.8 %collective-permute-done.22.far_ref = bf16[64,384]{1,0:T(8,128)(2,1)S(1)} collective-permute-done((bf16[64,384]{1,0:T(8,128)(2,1)S(1)}, bf16[64,384]{1,0:T(8,128)(2,1)S(1)}, u32[]{:S(2)}, u32[]{:S(2)}) %collective-permute-start.22) | collective-permute-done | bytes 49184 | tf_op jit(solution)/shard_map/ppermute | solution.py:447
  76.9 1.1 %shard_map.97 = f32[64,768]{1,0:T(8,128)} custom-call(f32[64,768]{1,0:T(8,128)S(1)} %get-tuple-element.26.kept_ref, bf16[64,384]{1,0:T(8,128)(2,1)S(1)} %collective-permute-done.21.near_ref, bf16[64,384]{1,0:T(8,128)(2,1)S(1)} %collective-permute-done.22.far_ref, bf16[2,192,768]{2,1,0:T(8,128)(2,1)S(1)} %copy-done.1, ...), custom_call_target="tpu_custom_call" | custom-call | flops 75497472 | bytes 1048576 | tf_op jit(solution)/shard_map/pallas_call | solution.py:378
  (18 shorter events, 0.1 us)
Async XLA Ops:
  0.0 6.1 %copy-start.2 = (bf16[64,768]{1,0:T(8,128)(2,1)S(1)}, bf16[64,768]{1,0:T(8,128)(2,1)}, u32[]{:S(2)}) copy-start(bf16[64,768]{1,0:T(8,128)(2,1)} %q_ref.3) | copy-start | bytes 294916
  0.0 13.4 %copy-start = (bf16[2,768,192]{1,2,0:T(8,128)(2,1)S(1)}, bf16[2,768,192]{1,2,0:T(8,128)(2,1)}, u32[]{:S(2)}) copy-start(bf16[2,768,192]{1,2,0:T(8,128)(2,1)} %param.15) | copy-start | bytes 1769476
  0.0 13.4 %copy-start.7 = (f32[2,768]{1,0:T(2,128)S(1)}, f32[2,768]{1,0:T(2,128)}, u32[]{:S(2)}) copy-start(f32[2,768]{1,0:T(2,128)} %gain_ref.3) | copy-start | bytes 18436
  0.0 13.4 %copy-start.8 = (f32[6]{0:T(128)S(1)}, f32[6]{0:T(128)}, u32[]{:S(2)}) copy-start(f32[6]{0:T(128)} %scale_ref.3) | copy-start | bytes 76
  5.5 7.8 %collective-permute-start.3 = (bf16[1536,256]{1,0:T(8,128)(2,1)S(1)}, bf16[1536,256]{1,0:T(8,128)(2,1)S(1)}, u32[]{:S(2)}, u32[]{:S(2)}) collective-permute-start(bf16[1536,256]{1,0:T(8,128)(2,1)S(1)} %get-tuple-element.19), channel_id=1, source_target_pairs={{0,1},{1,0},{2,3},{3,2},{4,5},{5,4},{6,7},{7,6},{8,9},{9,8},{10,11... | collective-permute-start | bytes 2359304 | tf_op jit(solution)/shard_map/ppermute | solution.py:405
  6.1 5.9 %collective-permute-start.1 = (bf16[64,768]{1,0:T(8,128)(2,1)S(1)}, bf16[64,768]{1,0:T(8,128)(2,1)S(1)}, u32[]{:S(2)}, u32[]{:S(2)}) collective-permute-start(bf16[64,768]{1,0:T(8,128)(2,1)S(1)} %copy-done.2), channel_id=1, source_target_pairs={{0,2},{2,0},{1,3},{3,1},{4,6},{6,4},{5,7},{7,5},{8,10},{10,8},{9,1... | collective-permute-start | bytes 294920 | tf_op jit(solution)/shard_map/ppermute | solution.py:405
  8.7 3.4 %collective-permute-start = (bf16[64,768]{1,0:T(8,128)(2,1)S(1)}, bf16[64,768]{1,0:T(8,128)(2,1)S(1)}, u32[]{:S(2)}, u32[]{:S(2)}) collective-permute-start(bf16[64,768]{1,0:T(8,128)(2,1)S(1)} %copy-done.2), channel_id=1, source_target_pairs={{0,1},{1,0},{2,3},{3,2},{4,5},{5,4},{6,7},{7,6},{8,9},{9,8},{10,11... | collective-permute-start | bytes 294920 | tf_op jit(solution)/shard_map/ppermute | solution.py:405
  12.0 1.3 %collective-permute-start.2 = (bf16[64,768]{1,0:T(8,128)(2,1)S(1)}, bf16[64,768]{1,0:T(8,128)(2,1)S(1)}, u32[]{:S(2)}, u32[]{:S(2)}) collective-permute-start(bf16[64,768]{1,0:T(8,128)(2,1)S(1)} %collective-permute-done.1.qx_ref), channel_id=1, source_target_pairs={{0,1},{1,0},{2,3},{3,2},{4,5},{5,4},{6,7},{7,6},{8,9},{9,8},{10,11... | collective-permute-start | bytes 294920 | tf_op jit(solution)/shard_map/ppermute | solution.py:405
  12.1 8.0 %copy-start.3 = (bf16[64,768]{1,0:T(8,128)(2,1)}, bf16[64,768]{1,0:T(8,128)(2,1)S(1)}, u32[]{:S(2)}) copy-start(bf16[64,768]{1,0:T(8,128)(2,1)S(1)} %collective-permute-done.qk_ref) | copy-start | bytes 294916
  13.3 6.7 %copy-start.5 = (bf16[64,768]{1,0:T(8,128)(2,1)}, bf16[64,768]{1,0:T(8,128)(2,1)S(1)}, u32[]{:S(2)}) copy-start(bf16[64,768]{1,0:T(8,128)(2,1)S(1)} %collective-permute-done.2.qxk_ref) | copy-start | bytes 294916
  13.4 13.0 %copy-start.1 = (bf16[2,192,768]{2,1,0:T(8,128)(2,1)S(1)}, bf16[2,192,768]{2,1,0:T(8,128)(2,1)}, u32[]{:S(2)}) copy-start(bf16[2,192,768]{2,1,0:T(8,128)(2,1)} %wo0.3) | copy-start | bytes 1769476
  16.1 12.0 %collective-permute-start.4 = (bf16[64,256]{1,0:T(8,128)(2,1)S(1)}, bf16[64,256]{1,0:T(8,128)(2,1)S(1)}, u32[]{:S(2)}, u32[]{:S(2)}) collective-permute-start(bf16[64,256]{1,0:T(8,128)(2,1)S(1)} %get-tuple-element.21), channel_id=1, source_target_pairs={{0,12},{4,8},{8,4},{12,0},{1,13},{5,9},{9,5},{13,1},{2,14},{6,10},... | collective-permute-start | bytes 98312 | tf_op jit(solution)/shard_map/ppermute | solution.py:410
  20.0 8.1 %collective-permute-start.5 = (bf16[64,256]{1,0:T(8,128)(2,1)S(1)}, bf16[64,256]{1,0:T(8,128)(2,1)S(1)}, u32[]{:S(2)}, u32[]{:S(2)}) collective-permute-start(bf16[64,256]{1,0:T(8,128)(2,1)S(1)} %get-tuple-element.22), channel_id=1, source_target_pairs={{0,8},{4,12},{8,0},{12,4},{1,9},{5,13},{9,1},{13,5},{2,10},{6,14},... | collective-permute-start | bytes 98312 | tf_op jit(solution)/shard_map/ppermute | solution.py:410
  20.0 8.1 %collective-permute-start.6 = (bf16[64,256]{1,0:T(8,128)(2,1)S(1)}, bf16[64,256]{1,0:T(8,128)(2,1)S(1)}, u32[]{:S(2)}, u32[]{:S(2)}) collective-permute-start(bf16[64,256]{1,0:T(8,128)(2,1)S(1)} %get-tuple-element.23), channel_id=1, source_target_pairs={{0,4},{4,0},{8,12},{12,8},{1,5},{5,1},{9,13},{13,9},{2,6},{6,2},{1... | collective-permute-start | bytes 98312 | tf_op jit(solution)/shard_map/ppermute | solution.py:410
  26.3 28.7 %collective-permute-start.16 = (bf16[1536,256]{1,0:T(8,128)(2,1)}, bf16[1536,256]{1,0:T(8,128)(2,1)S(1)}, u32[]{:S(2)}, u32[]{:S(2)}) collective-permute-start(bf16[1536,256]{1,0:T(8,128)(2,1)} %get-tuple-element.25), channel_id=1, source_target_pairs={{0,1},{1,0},{2,3},{3,2},{4,5},{5,4},{6,7},{7,6},{8,9},{9,8},{10,11... | collective-permute-start | bytes 2359304 | tf_op jit(solution)/shard_map/ppermute | solution.py:405
  26.4 16.2 %collective-permute-start.14 = (bf16[2,192,768]{2,1,0:T(8,128)(2,1)S(1)}, bf16[2,192,768]{2,1,0:T(8,128)(2,1)S(1)}, u32[]{:S(2)}, u32[]{:S(2)}) collective-permute-start(bf16[2,192,768]{2,1,0:T(8,128)(2,1)S(1)} %copy-done.1), channel_id=1, source_target_pairs={{0,2},{2,0},{1,3},{3,1},{4,6},{6,4},{5,7},{7,5},{8,10},{10,8},{9,1... | collective-permute-start | bytes 1769480 | tf_op jit(solution)/shard_map/ppermute | solution.py:405
  28.9 1.6 %collective-permute-start.7 = (bf16[64,256]{1,0:T(8,128)(2,1)}, bf16[64,256]{1,0:T(8,128)(2,1)}, u32[]{:S(2)}, u32[]{:S(2)}) collective-permute-start(bf16[64,256]{1,0:T(8,128)(2,1)} %shard_map.93), channel_id=1, source_target_pairs={{0,1},{1,0},{2,3},{3,2},{4,5},{5,4},{6,7},{7,6},{8,9},{9,8},{10,11... | collective-permute-start | bytes 98312 | tf_op jit(solution)/shard_map/ppermute | solution.py:405
  31.2 16.1 %collective-permute-start.8 = (bf16[64,384]{1,0:T(8,128)(2,1)S(1)}, bf16[64,384]{1,0:T(8,128)(2,1)S(1)}, u32[]{:S(2)}, u32[]{:S(2)}) collective-permute-start(bf16[64,384]{1,0:T(8,128)(2,1)S(1)} %pad_maximum_fusion.block_ref), channel_id=1, source_target_pairs={{1,3},{3,1},{5,7},{7,5},{9,11},{11,9},{13,15},{15,13},{17,19},{19,... | collective-permute-start | bytes 147464 | tf_op jit(solution)/shard_map/ppermute | solution.py:434
  31.9 23.1 %collective-permute-start.13 = (bf16[2,192,768]{2,1,0:T(8,128)(2,1)S(1)}, bf16[2,192,768]{2,1,0:T(8,128)(2,1)S(1)}, u32[]{:S(2)}, u32[]{:S(2)}) collective-permute-start(bf16[2,192,768]{2,1,0:T(8,128)(2,1)S(1)} %copy-done.1), channel_id=1, source_target_pairs={{0,1},{1,0},{2,3},{3,2},{4,5},{5,4},{6,7},{7,6},{8,9},{9,8},{10,11... | collective-permute-start | bytes 1769480 | tf_op jit(solution)/shard_map/ppermute | solution.py:405
  42.7 13.8 %collective-permute-start.15 = (bf16[2,192,768]{2,1,0:T(8,128)(2,1)S(1)}, bf16[2,192,768]{2,1,0:T(8,128)(2,1)S(1)}, u32[]{:S(2)}, u32[]{:S(2)}) collective-permute-start(bf16[2,192,768]{2,1,0:T(8,128)(2,1)S(1)} %collective-permute-done.14.wo2), channel_id=1, source_target_pairs={{0,1},{1,0},{2,3},{3,2},{4,5},{5,4},{6,7},{7,6},{8,9},{9,8},{10,11... | collective-permute-start | bytes 1769480 | tf_op jit(solution)/shard_map/ppermute | solution.py:405
  42.7 7.2 %collective-permute-start.9 = (bf16[64,384]{1,0:T(8,128)(2,1)S(1)}, bf16[64,384]{1,0:T(8,128)(2,1)S(1)}, u32[]{:S(2)}, u32[]{:S(2)}) collective-permute-start(bf16[64,384]{1,0:T(8,128)(2,1)S(1)} %pad_maximum_fusion.block_ref), channel_id=1, source_target_pairs={{0,14},{1,13},{2,12},{3,15},{4,10},{5,9},{6,8},{7,11},{8,6},{9,5},... | collective-permute-start | bytes 147464 | tf_op jit(solution)/shard_map/ppermute | solution.py:434
  47.4 5.0 %collective-permute-start.10 = (bf16[64,384]{1,0:T(8,128)(2,1)S(1)}, bf16[64,384]{1,0:T(8,128)(2,1)S(1)}, u32[]{:S(2)}, u32[]{:S(2)}) collective-permute-start(bf16[64,384]{1,0:T(8,128)(2,1)S(1)} %pad_maximum_fusion.block_ref), channel_id=1, source_target_pairs={{0,8},{1,11},{2,10},{3,9},{4,12},{5,15},{6,14},{7,13},{8,0},{9,3},... | collective-permute-start | bytes 147464 | tf_op jit(solution)/shard_map/ppermute | solution.py:434
  49.9 5.0 %collective-permute-start.11 = (bf16[64,384]{1,0:T(8,128)(2,1)S(1)}, bf16[64,384]{1,0:T(8,128)(2,1)S(1)}, u32[]{:S(2)}, u32[]{:S(2)}) collective-permute-start(bf16[64,384]{1,0:T(8,128)(2,1)S(1)} %pad_maximum_fusion.block_ref), channel_id=1, source_target_pairs={{0,6},{1,5},{2,4},{3,7},{4,2},{5,1},{6,0},{7,3},{8,14},{9,13},{10,... | collective-permute-start | bytes 147464 | tf_op jit(solution)/shard_map/ppermute | solution.py:434
  54.9 1.5 %collective-permute-start.12 = (bf16[256,384]{1,0:T(8,128)(2,1)S(1)}, bf16[256,384]{1,0:T(8,128)(2,1)S(1)}, u32[]{:S(2)}, u32[]{:S(2)}) collective-permute-start(bf16[256,384]{1,0:T(8,128)(2,1)S(1)} %constant_dynamic-update-slice_fusion.near_ref), channel_id=1, source_target_pairs={{0,1},{1,0},{2,3},{3,2},{4,5},{5,4},{6,7},{7,6},{8,9},{9,8},{10,11... | collective-permute-start | bytes 589832 | tf_op jit(solution)/shard_map/ppermute | solution.py:405
  56.4 0.9 %copy-start.4 = (bf16[64,768]{1,0:T(8,128)(2,1)S(1)}, bf16[64,768]{1,0:T(8,128)(2,1)}, u32[]{:S(2)}) copy-start(bf16[64,768]{1,0:T(8,128)(2,1)} %copy-done.3) | copy-start | bytes 294916
  57.3 0.9 %copy-start.6 = (bf16[64,768]{1,0:T(8,128)(2,1)S(1)}, bf16[64,768]{1,0:T(8,128)(2,1)}, u32[]{:S(2)}) copy-start(bf16[64,768]{1,0:T(8,128)(2,1)} %copy-done.5) | copy-start | bytes 294916
  61.3 6.1 %collective-permute-start.17 = (bf16[64,256]{1,0:T(8,128)(2,1)S(1)}, bf16[64,256]{1,0:T(8,128)(2,1)S(1)}, u32[]{:S(2)}, u32[]{:S(2)}) collective-permute-start(bf16[64,256]{1,0:T(8,128)(2,1)S(1)} %get-tuple-element.28), channel_id=1, source_target_pairs={{0,12},{4,8},{8,4},{12,0},{1,13},{5,9},{9,5},{13,1},{2,14},{6,10},... | collective-permute-start | bytes 98312 | tf_op jit(solution)/shard_map/ppermute | solution.py:410
  65.3 4.8 %collective-permute-start.18 = (bf16[64,256]{1,0:T(8,128)(2,1)S(1)}, bf16[64,256]{1,0:T(8,128)(2,1)S(1)}, u32[]{:S(2)}, u32[]{:S(2)}) collective-permute-start(bf16[64,256]{1,0:T(8,128)(2,1)S(1)} %get-tuple-element.29), channel_id=1, source_target_pairs={{0,8},{4,12},{8,0},{12,4},{1,9},{5,13},{9,1},{13,5},{2,10},{6,14},... | collective-permute-start | bytes 98312 | tf_op jit(solution)/shard_map/ppermute | solution.py:410
  65.3 4.8 %collective-permute-start.19 = (bf16[64,256]{1,0:T(8,128)(2,1)S(1)}, bf16[64,256]{1,0:T(8,128)(2,1)S(1)}, u32[]{:S(2)}, u32[]{:S(2)}) collective-permute-start(bf16[64,256]{1,0:T(8,128)(2,1)S(1)} %get-tuple-element.30), channel_id=1, source_target_pairs={{0,4},{4,0},{8,12},{12,8},{1,5},{5,1},{9,13},{13,9},{2,6},{6,2},{1... | collective-permute-start | bytes 98312 | tf_op jit(solution)/shard_map/ppermute | solution.py:410
  70.2 1.3 %collective-permute-start.20 = (bf16[64,256]{1,0:T(8,128)(2,1)S(1)}, bf16[64,256]{1,0:T(8,128)(2,1)S(1)}, u32[]{:S(2)}, u32[]{:S(2)}) collective-permute-start(bf16[64,256]{1,0:T(8,128)(2,1)S(1)} %shard_map.96), channel_id=1, source_target_pairs={{0,1},{1,0},{2,3},{3,2},{4,5},{5,4},{6,7},{7,6},{8,9},{9,8},{10,11... | collective-permute-start | bytes 98312 | tf_op jit(solution)/shard_map/ppermute | solution.py:405
  71.5 2.6 %collective-permute-start.21 = (bf16[64,384]{1,0:T(8,128)(2,1)S(1)}, bf16[64,384]{1,0:T(8,128)(2,1)S(1)}, u32[]{:S(2)}, u32[]{:S(2)}) collective-permute-start(bf16[64,384]{1,0:T(8,128)(2,1)S(1)} %pad_maximum_fusion.1), channel_id=1, source_target_pairs={{1,0},{5,1},{11,2},{15,3},{0,4},{4,5},{10,6},{14,7},{3,8},{7,9},{9... | collective-permute-start | bytes 147464 | tf_op jit(solution)/shard_map/ppermute | solution.py:447
  71.6 5.2 %collective-permute-start.22 = (bf16[64,384]{1,0:T(8,128)(2,1)S(1)}, bf16[64,384]{1,0:T(8,128)(2,1)S(1)}, u32[]{:S(2)}, u32[]{:S(2)}) collective-permute-start(bf16[64,384]{1,0:T(8,128)(2,1)S(1)} %pad_maximum_fusion.1), channel_id=1, source_target_pairs={{3,0},{7,1},{9,2},{13,3},{2,4},{6,5},{8,6},{12,7},{1,8},{5,9},{11,... | collective-permute-start | bytes 147464 | tf_op jit(solution)/shard_map/ppermute | solution.py:447

commit v3 on v2

--- a/solution.py
+++ b/solution.py
@@ -110,14 +110,12 @@
         self.width = -(-self.half // LANES) * LANES
         self.start = [k * self.half // LANES * LANES for k in range(self.n_k)]
         self.off = [k * self.half - s for k, s in enumerate(self.start)]
-        offsets = [(t, h) for t in range(self.n_t) for h in range(self.n_h)][1:]
-        offsets = sorted(offsets, reverse=True)
-        offsets += [None] * (-len(offsets) % self.n_k)
+        steps = [1, *range(self.n_t - 1, 1, -1)]
         self.rounds = [
-            tuple(offsets[i + (k + i // self.n_k) % self.n_k] for k in range(self.n_k))
-            for i in range(0, len(offsets), self.n_k)
+            tuple((step, (k + index) % 2) for k in range(self.n_k))
+            for index, step in enumerate(steps)
         ]
-        self.rounds = self.rounds[-1:] + self.rounds[:-1]
+        self.rounds.append((None,) * (self.n_k - 1) + ((0, 1),))
 
     def usable(self):
         return (

time: 79.4 us -> 76.8 us (0.967)
  waiting for transfers between devices: 31.8 us -> 28.7 us
    ppermute x4, waiting for transfers between devices: 7.16 us -> 4.3 us  [spread(): received.append(lax.ppermute(block, axes, links))]
    ppermute x4, starting transfers between devices: 5.71 us -> 6.72 us  [spread(): received.append(lax.ppermute(block, axes, links))]
    ppermute x11, starting transfers between devices: 6.91 us -> 5.95 us  [swap(): return lax.ppermute(value, axis, [(i, i ^ 1) for i in range(size)])]
  transfers between devices with their start and end apart: 23 -> 23, of which waited for: 12 -> 11; matrix products, arithmetic and copies ran while one was open for 1% -> 1% of each run, Pallas kernels for 8% -> 9%
where the time goes in v3:
time: 76.8 us; the launch traced here: 75.3 us
  waiting for transfers between devices  28.7 us (37%)
  starting transfers between devices  24.9 us (32%)
  Pallas kernels  18.2 us (24%)
  local copies, waits for them, and re-layouts  1.86 us (2%)
  between operations  0.91 us (1%)
  other arithmetic  0.83 us (1%)
    ppermute x11, waiting for transfers between devices, swap(): return lax.ppermute(value, axis, [(i, i ^ 1) for i in range(size)])  18.3 us
    pallas_call x7, Pallas kernels, vmem_call(): pl.pallas_call(kernel, out_shape=out_shape, in_specs=specs, out_specs=[pl...  18.2 us
    ppermute x6, starting transfers between devices, exchange(): lax.ppermute(chunks[d], 'tiles', [(i, i ^ d) for i in range(plan.n_t)])  9.02 us
    ppermute x4, starting transfers between devices, spread(): received.append(lax.ppermute(block, axes, links))  6.72 us
    ppermute x11, starting transfers between devices, swap(): return lax.ppermute(value, axis, [(i, i ^ 1) for i in range(size)])  5.95 us
    ppermute x4, waiting for transfers between devices, spread(): received.append(lax.ppermute(block, axes, links))  4.3 us
    ppermute x6, waiting for transfers between devices, exchange(): lax.ppermute(chunks[d], 'tiles', [(i, i ^ d) for i in range(plan.n_t)])  3.98 us
    ppermute x2, starting transfers between devices, collect(): received.append(lax.ppermute(block, axes, links))  3.17 us
  transfers between devices with their start and end apart: 23, of which 11 were waited for; matrix products, arithmetic and copies ran while one was open for 1% of the time, Pallas kernels for 9%

profile of v3, /device:TPU:0, one launch (start us, length us, event | category | flops | bytes accessed | tf_op | source)
XLA Modules:
  0.0 75.3 jit_solution(8211239760751911496)
XLA Ops:
  0.7 4.8 %shard_map.91 = (bf16[1536,256]{1,0:T(8,128)(2,1)S(1)}, bf16[1536,256]{1,0:T(8,128)(2,1)S(1)}) custom-call(s32[1]{0:T(128)S(6)} %copy.13.count_ref, bf16[1536,1536]{1,0:T(8,128)(2,1)} %feats_hbm.3, bf16[2,1536,384]{2,1,0:T(8,128)(2,1)} %bitcast.4, s32[6,256]{1,0:T(8,128)} %mask_hbm.3), custom_call_target="tpu_custom_call" | custom-call | flops 1811939328 | bytes 1048576 | tf_op jit(solution)/shard_map/pallas_call | solution.py:376
  5.5 0.6 collective-permute-start.3
  6.1 0.0 copy-done.2
  6.1 2.6 %collective-permute-start.1 = (bf16[64,768]{1,0:T(8,128)(2,1)S(1)}, bf16[64,768]{1,0:T(8,128)(2,1)S(1)}, u32[]{:S(2)}, u32[]{:S(2)}) collective-permute-start(bf16[64,768]{1,0:T(8,128)(2,1)S(1)} %copy-done.2), channel_id=1, source_target_pairs={{0,2},{2,0},{1,3},{3,1},{4,6},{6,4},{5,7},{7,5},{8,10},{10,8},{9,1... | collective-permute-start | bytes 294920 | tf_op jit(solution)/shard_map/ppermute | solution.py:403
  8.7 0.1 collective-permute-start
  8.8 3.2 %collective-permute-done.1.qx_ref = bf16[64,768]{1,0:T(8,128)(2,1)S(1)} collective-permute-done((bf16[64,768]{1,0:T(8,128)(2,1)S(1)}, bf16[64,768]{1,0:T(8,128)(2,1)S(1)}, u32[]{:S(2)}, u32[]{:S(2)}) %collective-permute-start.1) | collective-permute-done | bytes 98336 | tf_op jit(solution)/shard_map/ppermute | solution.py:403
  12.0 0.0 collective-permute-start.2
  12.0 0.0 collective-permute-done.qk_ref
  12.1 1.3 %collective-permute-done.2.qxk_ref = bf16[64,768]{1,0:T(8,128)(2,1)S(1)} collective-permute-done((bf16[64,768]{1,0:T(8,128)(2,1)S(1)}, bf16[64,768]{1,0:T(8,128)(2,1)S(1)}, u32[]{:S(2)}, u32[]{:S(2)}) %collective-permute-start.2) | collective-permute-done | bytes 98336 | tf_op jit(solution)/shard_map/ppermute | solution.py:403
  13.3 0.0 collective-permute-done.3.recv_ref
  13.4 0.0 copy-done
  13.4 0.0 copy-done.7
  13.4 0.0 copy-done.8
  13.4 0.0 copy-start.1
  13.4 2.7 %shard_map.92 = (f32[64,256]{1,0:T(8,128)S(1)}, bf16[64,256]{1,0:T(8,128)(2,1)S(1)}, bf16[64,256]{1,0:T(8,128)(2,1)S(1)}, bf16[64,256]{1,0:T(8,128)(2,1)S(1)}) custom-call(f32[6]{0:T(128)S(1)} %copy-done.8, bf16[64,768]{1,0:T(8,128)(2,1)S(1)} %copy-done.2, bf16[64,768]{1,0:T(8,128)(2,1)S(1)} %collective-permute-done.qk_ref, ...), custom_call_target="tpu_custom_call" | custom-call | flops 402653184 | bytes 1048576 | tf_op jit(solution)/shard_map/pallas_call | solution.py:376
  16.1 3.9 %collective-permute-start.4 = (bf16[64,256]{1,0:T(8,128)(2,1)S(1)}, bf16[64,256]{1,0:T(8,128)(2,1)S(1)}, u32[]{:S(2)}, u32[]{:S(2)}) collective-permute-start(bf16[64,256]{1,0:T(8,128)(2,1)S(1)} %get-tuple-element.21), channel_id=1, source_target_pairs={{0,12},{4,8},{8,4},{12,0},{1,13},{5,9},{9,5},{13,1},{2,14},{6,10},... | collective-permute-start | bytes 98312 | tf_op jit(solution)/shard_map/ppermute | solution.py:408
  20.0 0.0 collective-permute-start.5
  20.0 0.0 copy-done.3
  20.0 0.0 copy-done.5
  20.0 0.6 collective-permute-start.6
  20.7 5.7 %shard_map.94 = (bf16[1536,256]{1,0:T(8,128)(2,1)S(1)}, bf16[1536,256]{1,0:T(8,128)(2,1)}) custom-call(s32[1]{0:T(128)S(6)} %copy.13.count_ref, bf16[1536,1536]{1,0:T(8,128)(2,1)} %feats_hbm.3, bf16[2,1536,384]{2,1,0:T(8,128)(2,1)} %bitcast.5, s32[6,256]{1,0:T(8,128)} %mask_hbm.3), custom_call_target="tpu_custom_call" | custom-call | flops 1811939328 | bytes 1048576 | tf_op jit(solution)/shard_map/pallas_call | solution.py:376
  26.3 0.1 collective-permute-start.16
  26.4 0.0 copy-done.1
  26.4 1.7 %collective-permute-start.14 = (bf16[2,192,768]{2,1,0:T(8,128)(2,1)S(1)}, bf16[2,192,768]{2,1,0:T(8,128)(2,1)S(1)}, u32[]{:S(2)}, u32[]{:S(2)}) collective-permute-start(bf16[2,192,768]{2,1,0:T(8,128)(2,1)S(1)} %copy-done.1), channel_id=1, source_target_pairs={{0,2},{2,0},{1,3},{3,1},{4,6},{6,4},{5,7},{7,5},{8,10},{10,8},{9,1... | collective-permute-start | bytes 1769480 | tf_op jit(solution)/shard_map/ppermute | solution.py:403
  28.1 0.0 collective-permute-done.4.refs_1_
  28.1 0.0 collective-permute-done.5.refs_2_
  28.1 0.0 collective-permute-done.6.refs_3_
  28.1 0.7 shard_map.93
  28.9 0.1 collective-permute-start.7
  29.0 1.4 %collective-permute-done.7 = bf16[64,256]{1,0:T(8,128)(2,1)} collective-permute-done((bf16[64,256]{1,0:T(8,128)(2,1)}, bf16[64,256]{1,0:T(8,128)(2,1)}, u32[]{:S(2)}, u32[]{:S(2)}) %collective-permute-start.7) | collective-permute-done | bytes 32800 | tf_op jit(solution)/shard_map/ppermute | solution.py:403
  30.4 0.8 %broadcast_select_fusion.3 = (bf16[64,256]{1,0:T(8,128)(2,1)S(1)}, bf16[64,256]{1,0:T(8,128)(2,1)S(1)}) fusion(bf16[64,256]{1,0:T(8,128)(2,1)} %shard_map.93, bf16[64,256]{1,0:T(8,128)(2,1)} %collective-permute-done.7, pred[]{:T(512)S(6)} %eq.2), kind=kLoop, calls=%fused_computation.5 | loop fusion | flops 32768 | bytes 131073 | tf_op jit(solution)/shard_map/jit(_where)/select_n | solution.py:414
  31.2 1.4 %collective-permute-start.8 = (bf16[64,384]{1,0:T(8,128)(2,1)S(1)}, bf16[64,384]{1,0:T(8,128)(2,1)S(1)}, u32[]{:S(2)}, u32[]{:S(2)}) collective-permute-start(bf16[64,384]{1,0:T(8,128)(2,1)S(1)} %pad_maximum_fusion.block_ref), channel_id=1, source_target_pairs={{0,4},{1,7},{2,6},{3,5},{4,0},{5,3},{6,2},{7,1},{8,12},{9,15},{10,... | collective-permute-start | bytes 147464 | tf_op jit(solution)/shard_map/ppermute | solution.py:432
  32.6 0.0 collective-permute-start.13
  32.6 10.1 %collective-permute-done.14.wo2 = bf16[2,192,768]{2,1,0:T(8,128)(2,1)S(1)} collective-permute-done((bf16[2,192,768]{2,1,0:T(8,128)(2,1)S(1)}, bf16[2,192,768]{2,1,0:T(8,128)(2,1)S(1)}, u32[]{:S(2)}, u32[]{:S(2)}) %collective-permute-start.14) | collective-permute-done | bytes 589856 | tf_op jit(solution)/shard_map/ppermute | solution.py:403
  42.7 0.0 collective-permute-start.15
  42.7 4.7 %collective-permute-start.9 = (bf16[64,384]{1,0:T(8,128)(2,1)S(1)}, bf16[64,384]{1,0:T(8,128)(2,1)S(1)}, u32[]{:S(2)}, u32[]{:S(2)}) collective-permute-start(bf16[64,384]{1,0:T(8,128)(2,1)S(1)} %pad_maximum_fusion.block_ref), channel_id=1, source_target_pairs={{0,14},{1,13},{2,12},{3,15},{4,10},{5,9},{6,8},{7,11},{8,6},{9,5},... | collective-permute-start | bytes 147464 | tf_op jit(solution)/shard_map/ppermute | solution.py:432
  47.4 0.0 collective-permute-done.8
  47.4 0.0 collective-permute-start.10
  47.4 2.6 %collective-permute-done.9 = bf16[64,384]{1,0:T(8,128)(2,1)S(1)} collective-permute-done((bf16[64,384]{1,0:T(8,128)(2,1)S(1)}, bf16[64,384]{1,0:T(8,128)(2,1)S(1)}, u32[]{:S(2)}, u32[]{:S(2)}) %collective-permute-start.9) | collective-permute-done | bytes 49184 | tf_op jit(solution)/shard_map/ppermute | solution.py:432
  49.9 0.7 collective-permute-start.11
  50.6 1.7 %collective-permute-done.10 = bf16[64,384]{1,0:T(8,128)(2,1)S(1)} collective-permute-done((bf16[64,384]{1,0:T(8,128)(2,1)S(1)}, bf16[64,384]{1,0:T(8,128)(2,1)S(1)}, u32[]{:S(2)}, u32[]{:S(2)}) %collective-permute-start.10) | collective-permute-done | bytes 49184 | tf_op jit(solution)/shard_map/ppermute | solution.py:432
  52.4 0.0 collective-permute-done.11
  52.4 0.7 collective-permute-start.12
  53.1 0.0 collective-permute-done.13.wo1
  53.1 0.0 collective-permute-done.16.recv_ref
  53.1 1.1 %collective-permute-done.12.far_ref = bf16[256,384]{1,0:T(8,128)(2,1)S(1)} collective-permute-done((bf16[256,384]{1,0:T(8,128)(2,1)S(1)}, bf16[256,384]{1,0:T(8,128)(2,1)S(1)}, u32[]{:S(2)}, u32[]{:S(2)}) %collective-permute-start.12) | collective-permute-done | bytes 196640 | tf_op jit(solution)/shard_map/ppermute | solution.py:403
  54.2 0.0 collective-permute-done.15.wo3
  54.2 0.9 %copy-done.4 = bf16[64,768]{1,0:T(8,128)(2,1)S(1)} copy-done((bf16[64,768]{1,0:T(8,128)(2,1)S(1)}, bf16[64,768]{1,0:T(8,128)(2,1)}, u32[]{:S(2)}) %copy-start.4) | copy-done | bytes 98328
  55.1 0.9 %copy-done.6 = bf16[64,768]{1,0:T(8,128)(2,1)S(1)} copy-done((bf16[64,768]{1,0:T(8,128)(2,1)S(1)}, bf16[64,768]{1,0:T(8,128)(2,1)}, u32[]{:S(2)}) %copy-start.6) | copy-done | bytes 98328
  56.0 3.0 %shard_map.95 = (f32[64,256]{1,0:T(8,128)S(1)}, bf16[64,256]{1,0:T(8,128)(2,1)S(1)}, bf16[64,256]{1,0:T(8,128)(2,1)S(1)}, bf16[64,256]{1,0:T(8,128)(2,1)S(1)}, f32[64,768]{1,0:T(8,128)S(1)}) custom-call(f32[6]{0:T(128)S(1)} %copy-done.8, bf16[64,768]{1,0:T(8,128)(2,1)S(1)} %copy-done.2, bf16[64,768]{1,0:T(8,128)(2,1)S(1)} %copy-done.4, ...), custom_call_target="tpu_custom_call" | custom-call | flops 402653184 | bytes 1048576 | tf_op jit(solution)/shard_map/pallas_call | solution.py:376
  59.0 3.6 %collective-permute-start.17 = (bf16[64,256]{1,0:T(8,128)(2,1)S(1)}, bf16[64,256]{1,0:T(8,128)(2,1)S(1)}, u32[]{:S(2)}, u32[]{:S(2)}) collective-permute-start(bf16[64,256]{1,0:T(8,128)(2,1)S(1)} %get-tuple-element.28), channel_id=1, source_target_pairs={{0,12},{4,8},{8,4},{12,0},{1,13},{5,9},{9,5},{13,1},{2,14},{6,10},... | collective-permute-start | bytes 98312 | tf_op jit(solution)/shard_map/ppermute | solution.py:408
  62.6 0.0 collective-permute-start.18
  62.6 0.8 %collective-permute-start.19 = (bf16[64,256]{1,0:T(8,128)(2,1)S(1)}, bf16[64,256]{1,0:T(8,128)(2,1)S(1)}, u32[]{:S(2)}, u32[]{:S(2)}) collective-permute-start(bf16[64,256]{1,0:T(8,128)(2,1)S(1)} %get-tuple-element.30), channel_id=1, source_target_pairs={{0,4},{4,0},{8,12},{12,8},{1,5},{5,1},{9,13},{13,9},{2,6},{6,2},{1... | collective-permute-start | bytes 98312 | tf_op jit(solution)/shard_map/ppermute | solution.py:408
  63.5 1.4 %collective-permute-done.17.refs_1_ = bf16[64,256]{1,0:T(8,128)(2,1)S(1)} collective-permute-done((bf16[64,256]{1,0:T(8,128)(2,1)S(1)}, bf16[64,256]{1,0:T(8,128)(2,1)S(1)}, u32[]{:S(2)}, u32[]{:S(2)}) %collective-permute-start.17) | collective-permute-done | bytes 32800 | tf_op jit(solution)/shard_map/ppermute | solution.py:408
  64.8 2.6 %collective-permute-done.18.refs_2_ = bf16[64,256]{1,0:T(8,128)(2,1)S(1)} collective-permute-done((bf16[64,256]{1,0:T(8,128)(2,1)S(1)}, bf16[64,256]{1,0:T(8,128)(2,1)S(1)}, u32[]{:S(2)}, u32[]{:S(2)}) %collective-permute-start.18) | collective-permute-done | bytes 32800 | tf_op jit(solution)/shard_map/ppermute | solution.py:408
  67.4 0.0 collective-permute-done.19.refs_3_
  67.4 0.1 shard_map.96
  67.6 0.1 collective-permute-start.20
  67.6 1.2 %collective-permute-done.20 = bf16[64,256]{1,0:T(8,128)(2,1)S(1)} collective-permute-done((bf16[64,256]{1,0:T(8,128)(2,1)S(1)}, bf16[64,256]{1,0:T(8,128)(2,1)S(1)}, u32[]{:S(2)}, u32[]{:S(2)}) %collective-permute-start.20) | collective-permute-done | bytes 32800 | tf_op jit(solution)/shard_map/ppermute | solution.py:403
  68.9 0.3 collective-permute-start.21
  69.2 2.9 %collective-permute-start.22 = (bf16[64,384]{1,0:T(8,128)(2,1)S(1)}, bf16[64,384]{1,0:T(8,128)(2,1)S(1)}, u32[]{:S(2)}, u32[]{:S(2)}) collective-permute-start(bf16[64,384]{1,0:T(8,128)(2,1)S(1)} %pad_maximum_fusion.1), channel_id=1, source_target_pairs={{3,0},{7,1},{9,2},{13,3},{2,4},{6,5},{8,6},{12,7},{1,8},{5,9},{11,... | collective-permute-start | bytes 147464 | tf_op jit(solution)/shard_map/ppermute | solution.py:445
  72.0 0.0 collective-permute-done.21.near_ref
  72.1 2.2 %collective-permute-done.22.far_ref = bf16[64,384]{1,0:T(8,128)(2,1)S(1)} collective-permute-done((bf16[64,384]{1,0:T(8,128)(2,1)S(1)}, bf16[64,384]{1,0:T(8,128)(2,1)S(1)}, u32[]{:S(2)}, u32[]{:S(2)}) %collective-permute-start.22) | collective-permute-done | bytes 49184 | tf_op jit(solution)/shard_map/ppermute | solution.py:445
  74.2 1.1 %shard_map.97 = f32[64,768]{1,0:T(8,128)} custom-call(f32[64,768]{1,0:T(8,128)S(1)} %get-tuple-element.26.kept_ref, bf16[64,384]{1,0:T(8,128)(2,1)S(1)} %collective-permute-done.21.near_ref, bf16[64,384]{1,0:T(8,128)(2,1)S(1)} %collective-permute-done.22.far_ref, bf16[2,192,768]{2,1,0:T(8,128)(2,1)S(1)} %copy-done.1, ...), custom_call_target="tpu_custom_call" | custom-call | flops 75497472 | bytes 1048576 | tf_op jit(solution)/shard_map/pallas_call | solution.py:376
  (18 shorter events, 0.1 us)
Async XLA Ops:
  0.0 6.1 %copy-start.2 = (bf16[64,768]{1,0:T(8,128)(2,1)S(1)}, bf16[64,768]{1,0:T(8,128)(2,1)}, u32[]{:S(2)}) copy-start(bf16[64,768]{1,0:T(8,128)(2,1)} %q_ref.3) | copy-start | bytes 294916
  0.0 13.4 %copy-start = (bf16[2,768,192]{1,2,0:T(8,128)(2,1)S(1)}, bf16[2,768,192]{1,2,0:T(8,128)(2,1)}, u32[]{:S(2)}) copy-start(bf16[2,768,192]{1,2,0:T(8,128)(2,1)} %param.15) | copy-start | bytes 1769476
  0.0 13.4 %copy-start.7 = (f32[2,768]{1,0:T(2,128)S(1)}, f32[2,768]{1,0:T(2,128)}, u32[]{:S(2)}) copy-start(f32[2,768]{1,0:T(2,128)} %gain_ref.3) | copy-start | bytes 18436
  0.0 13.4 %copy-start.8 = (f32[6]{0:T(128)S(1)}, f32[6]{0:T(128)}, u32[]{:S(2)}) copy-start(f32[6]{0:T(128)} %scale_ref.3) | copy-start | bytes 76
  5.5 7.8 %collective-permute-start.3 = (bf16[1536,256]{1,0:T(8,128)(2,1)S(1)}, bf16[1536,256]{1,0:T(8,128)(2,1)S(1)}, u32[]{:S(2)}, u32[]{:S(2)}) collective-permute-start(bf16[1536,256]{1,0:T(8,128)(2,1)S(1)} %get-tuple-element.19), channel_id=1, source_target_pairs={{0,1},{1,0},{2,3},{3,2},{4,5},{5,4},{6,7},{7,6},{8,9},{9,8},{10,11... | collective-permute-start | bytes 2359304 | tf_op jit(solution)/shard_map/ppermute | solution.py:403
  6.1 5.9 %collective-permute-start.1 = (bf16[64,768]{1,0:T(8,128)(2,1)S(1)}, bf16[64,768]{1,0:T(8,128)(2,1)S(1)}, u32[]{:S(2)}, u32[]{:S(2)}) collective-permute-start(bf16[64,768]{1,0:T(8,128)(2,1)S(1)} %copy-done.2), channel_id=1, source_target_pairs={{0,2},{2,0},{1,3},{3,1},{4,6},{6,4},{5,7},{7,5},{8,10},{10,8},{9,1... | collective-permute-start | bytes 294920 | tf_op jit(solution)/shard_map/ppermute | solution.py:403
  8.7 3.4 %collective-permute-start = (bf16[64,768]{1,0:T(8,128)(2,1)S(1)}, bf16[64,768]{1,0:T(8,128)(2,1)S(1)}, u32[]{:S(2)}, u32[]{:S(2)}) collective-permute-start(bf16[64,768]{1,0:T(8,128)(2,1)S(1)} %copy-done.2), channel_id=1, source_target_pairs={{0,1},{1,0},{2,3},{3,2},{4,5},{5,4},{6,7},{7,6},{8,9},{9,8},{10,11... | collective-permute-start | bytes 294920 | tf_op jit(solution)/shard_map/ppermute | solution.py:403
  12.0 1.3 %collective-permute-start.2 = (bf16[64,768]{1,0:T(8,128)(2,1)S(1)}, bf16[64,768]{1,0:T(8,128)(2,1)S(1)}, u32[]{:S(2)}, u32[]{:S(2)}) collective-permute-start(bf16[64,768]{1,0:T(8,128)(2,1)S(1)} %collective-permute-done.1.qx_ref), channel_id=1, source_target_pairs={{0,1},{1,0},{2,3},{3,2},{4,5},{5,4},{6,7},{7,6},{8,9},{9,8},{10,11... | collective-permute-start | bytes 294920 | tf_op jit(solution)/shard_map/ppermute | solution.py:403
  12.1 8.0 %copy-start.3 = (bf16[64,768]{1,0:T(8,128)(2,1)}, bf16[64,768]{1,0:T(8,128)(2,1)S(1)}, u32[]{:S(2)}) copy-start(bf16[64,768]{1,0:T(8,128)(2,1)S(1)} %collective-permute-done.qk_ref) | copy-start | bytes 294916
  13.3 6.7 %copy-start.5 = (bf16[64,768]{1,0:T(8,128)(2,1)}, bf16[64,768]{1,0:T(8,128)(2,1)S(1)}, u32[]{:S(2)}) copy-start(bf16[64,768]{1,0:T(8,128)(2,1)S(1)} %collective-permute-done.2.qxk_ref) | copy-start | bytes 294916
  13.4 13.0 %copy-start.1 = (bf16[2,192,768]{2,1,0:T(8,128)(2,1)S(1)}, bf16[2,192,768]{2,1,0:T(8,128)(2,1)}, u32[]{:S(2)}) copy-start(bf16[2,192,768]{2,1,0:T(8,128)(2,1)} %wo0.3) | copy-start | bytes 1769476
  16.1 12.0 %collective-permute-start.4 = (bf16[64,256]{1,0:T(8,128)(2,1)S(1)}, bf16[64,256]{1,0:T(8,128)(2,1)S(1)}, u32[]{:S(2)}, u32[]{:S(2)}) collective-permute-start(bf16[64,256]{1,0:T(8,128)(2,1)S(1)} %get-tuple-element.21), channel_id=1, source_target_pairs={{0,12},{4,8},{8,4},{12,0},{1,13},{5,9},{9,5},{13,1},{2,14},{6,10},... | collective-permute-start | bytes 98312 | tf_op jit(solution)/shard_map/ppermute | solution.py:408
  20.0 8.1 %collective-permute-start.5 = (bf16[64,256]{1,0:T(8,128)(2,1)S(1)}, bf16[64,256]{1,0:T(8,128)(2,1)S(1)}, u32[]{:S(2)}, u32[]{:S(2)}) collective-permute-start(bf16[64,256]{1,0:T(8,128)(2,1)S(1)} %get-tuple-element.22), channel_id=1, source_target_pairs={{0,8},{4,12},{8,0},{12,4},{1,9},{5,13},{9,1},{13,5},{2,10},{6,14},... | collective-permute-start | bytes 98312 | tf_op jit(solution)/shard_map/ppermute | solution.py:408
  20.0 8.1 %collective-permute-start.6 = (bf16[64,256]{1,0:T(8,128)(2,1)S(1)}, bf16[64,256]{1,0:T(8,128)(2,1)S(1)}, u32[]{:S(2)}, u32[]{:S(2)}) collective-permute-start(bf16[64,256]{1,0:T(8,128)(2,1)S(1)} %get-tuple-element.23), channel_id=1, source_target_pairs={{0,4},{4,0},{8,12},{12,8},{1,5},{5,1},{9,13},{13,9},{2,6},{6,2},{1... | collective-permute-start | bytes 98312 | tf_op jit(solution)/shard_map/ppermute | solution.py:408
  26.3 26.8 %collective-permute-start.16 = (bf16[1536,256]{1,0:T(8,128)(2,1)}, bf16[1536,256]{1,0:T(8,128)(2,1)S(1)}, u32[]{:S(2)}, u32[]{:S(2)}) collective-permute-start(bf16[1536,256]{1,0:T(8,128)(2,1)} %get-tuple-element.25), channel_id=1, source_target_pairs={{0,1},{1,0},{2,3},{3,2},{4,5},{5,4},{6,7},{7,6},{8,9},{9,8},{10,11... | collective-permute-start | bytes 2359304 | tf_op jit(solution)/shard_map/ppermute | solution.py:403
  26.4 16.2 %collective-permute-start.14 = (bf16[2,192,768]{2,1,0:T(8,128)(2,1)S(1)}, bf16[2,192,768]{2,1,0:T(8,128)(2,1)S(1)}, u32[]{:S(2)}, u32[]{:S(2)}) collective-permute-start(bf16[2,192,768]{2,1,0:T(8,128)(2,1)S(1)} %copy-done.1), channel_id=1, source_target_pairs={{0,2},{2,0},{1,3},{3,1},{4,6},{6,4},{5,7},{7,5},{8,10},{10,8},{9,1... | collective-permute-start | bytes 1769480 | tf_op jit(solution)/shard_map/ppermute | solution.py:403
  28.9 1.6 %collective-permute-start.7 = (bf16[64,256]{1,0:T(8,128)(2,1)}, bf16[64,256]{1,0:T(8,128)(2,1)}, u32[]{:S(2)}, u32[]{:S(2)}) collective-permute-start(bf16[64,256]{1,0:T(8,128)(2,1)} %shard_map.93), channel_id=1, source_target_pairs={{0,1},{1,0},{2,3},{3,2},{4,5},{5,4},{6,7},{7,6},{8,9},{9,8},{10,11... | collective-permute-start | bytes 98312 | tf_op jit(solution)/shard_map/ppermute | solution.py:403
  31.2 16.1 %collective-permute-start.8 = (bf16[64,384]{1,0:T(8,128)(2,1)S(1)}, bf16[64,384]{1,0:T(8,128)(2,1)S(1)}, u32[]{:S(2)}, u32[]{:S(2)}) collective-permute-start(bf16[64,384]{1,0:T(8,128)(2,1)S(1)} %pad_maximum_fusion.block_ref), channel_id=1, source_target_pairs={{0,4},{1,7},{2,6},{3,5},{4,0},{5,3},{6,2},{7,1},{8,12},{9,15},{10,... | collective-permute-start | bytes 147464 | tf_op jit(solution)/shard_map/ppermute | solution.py:432
  32.6 20.5 %collective-permute-start.13 = (bf16[2,192,768]{2,1,0:T(8,128)(2,1)S(1)}, bf16[2,192,768]{2,1,0:T(8,128)(2,1)S(1)}, u32[]{:S(2)}, u32[]{:S(2)}) collective-permute-start(bf16[2,192,768]{2,1,0:T(8,128)(2,1)S(1)} %copy-done.1), channel_id=1, source_target_pairs={{0,1},{1,0},{2,3},{3,2},{4,5},{5,4},{6,7},{7,6},{8,9},{9,8},{10,11... | collective-permute-start | bytes 1769480 | tf_op jit(solution)/shard_map/ppermute | solution.py:403
  42.7 11.5 %collective-permute-start.15 = (bf16[2,192,768]{2,1,0:T(8,128)(2,1)S(1)}, bf16[2,192,768]{2,1,0:T(8,128)(2,1)S(1)}, u32[]{:S(2)}, u32[]{:S(2)}) collective-permute-start(bf16[2,192,768]{2,1,0:T(8,128)(2,1)S(1)} %collective-permute-done.14.wo2), channel_id=1, source_target_pairs={{0,1},{1,0},{2,3},{3,2},{4,5},{5,4},{6,7},{7,6},{8,9},{9,8},{10,11... | collective-permute-start | bytes 1769480 | tf_op jit(solution)/shard_map/ppermute | solution.py:403
  42.7 7.2 %collective-permute-start.9 = (bf16[64,384]{1,0:T(8,128)(2,1)S(1)}, bf16[64,384]{1,0:T(8,128)(2,1)S(1)}, u32[]{:S(2)}, u32[]{:S(2)}) collective-permute-start(bf16[64,384]{1,0:T(8,128)(2,1)S(1)} %pad_maximum_fusion.block_ref), channel_id=1, source_target_pairs={{0,14},{1,13},{2,12},{3,15},{4,10},{5,9},{6,8},{7,11},{8,6},{9,5},... | collective-permute-start | bytes 147464 | tf_op jit(solution)/shard_map/ppermute | solution.py:432
  47.4 5.0 %collective-permute-start.10 = (bf16[64,384]{1,0:T(8,128)(2,1)S(1)}, bf16[64,384]{1,0:T(8,128)(2,1)S(1)}, u32[]{:S(2)}, u32[]{:S(2)}) collective-permute-start(bf16[64,384]{1,0:T(8,128)(2,1)S(1)} %pad_maximum_fusion.block_ref), channel_id=1, source_target_pairs={{0,8},{1,11},{2,10},{3,9},{4,12},{5,15},{6,14},{7,13},{8,0},{9,3},... | collective-permute-start | bytes 147464 | tf_op jit(solution)/shard_map/ppermute | solution.py:432
  49.9 2.4 %collective-permute-start.11 = (bf16[64,384]{1,0:T(8,128)(2,1)S(1)}, bf16[64,384]{1,0:T(8,128)(2,1)S(1)}, u32[]{:S(2)}, u32[]{:S(2)}) collective-permute-start(bf16[64,384]{1,0:T(8,128)(2,1)S(1)} %pad_maximum_fusion.block_ref), channel_id=1, source_target_pairs={{1,3},{3,1},{5,7},{7,5},{9,11},{11,9},{13,15},{15,13},{17,19},{19,... | collective-permute-start | bytes 147464 | tf_op jit(solution)/shard_map/ppermute | solution.py:432
  52.4 1.8 %collective-permute-start.12 = (bf16[256,384]{1,0:T(8,128)(2,1)S(1)}, bf16[256,384]{1,0:T(8,128)(2,1)S(1)}, u32[]{:S(2)}, u32[]{:S(2)}) collective-permute-start(bf16[256,384]{1,0:T(8,128)(2,1)S(1)} %constant_dynamic-update-slice_fusion.near_ref), channel_id=1, source_target_pairs={{0,1},{1,0},{2,3},{3,2},{4,5},{5,4},{6,7},{7,6},{8,9},{9,8},{10,11... | collective-permute-start | bytes 589832 | tf_op jit(solution)/shard_map/ppermute | solution.py:403
  54.2 0.9 %copy-start.4 = (bf16[64,768]{1,0:T(8,128)(2,1)S(1)}, bf16[64,768]{1,0:T(8,128)(2,1)}, u32[]{:S(2)}) copy-start(bf16[64,768]{1,0:T(8,128)(2,1)} %copy-done.3) | copy-start | bytes 294916
  55.1 0.9 %copy-start.6 = (bf16[64,768]{1,0:T(8,128)(2,1)S(1)}, bf16[64,768]{1,0:T(8,128)(2,1)}, u32[]{:S(2)}) copy-start(bf16[64,768]{1,0:T(8,128)(2,1)} %copy-done.5) | copy-start | bytes 294916
  59.0 5.8 %collective-permute-start.17 = (bf16[64,256]{1,0:T(8,128)(2,1)S(1)}, bf16[64,256]{1,0:T(8,128)(2,1)S(1)}, u32[]{:S(2)}, u32[]{:S(2)}) collective-permute-start(bf16[64,256]{1,0:T(8,128)(2,1)S(1)} %get-tuple-element.28), channel_id=1, source_target_pairs={{0,12},{4,8},{8,4},{12,0},{1,13},{5,9},{9,5},{13,1},{2,14},{6,10},... | collective-permute-start | bytes 98312 | tf_op jit(solution)/shard_map/ppermute | solution.py:408
  62.6 4.8 %collective-permute-start.18 = (bf16[64,256]{1,0:T(8,128)(2,1)S(1)}, bf16[64,256]{1,0:T(8,128)(2,1)S(1)}, u32[]{:S(2)}, u32[]{:S(2)}) collective-permute-start(bf16[64,256]{1,0:T(8,128)(2,1)S(1)} %get-tuple-element.29), channel_id=1, source_target_pairs={{0,8},{4,12},{8,0},{12,4},{1,9},{5,13},{9,1},{13,5},{2,10},{6,14},... | collective-permute-start | bytes 98312 | tf_op jit(solution)/shard_map/ppermute | solution.py:408
  62.6 4.8 %collective-permute-start.19 = (bf16[64,256]{1,0:T(8,128)(2,1)S(1)}, bf16[64,256]{1,0:T(8,128)(2,1)S(1)}, u32[]{:S(2)}, u32[]{:S(2)}) collective-permute-start(bf16[64,256]{1,0:T(8,128)(2,1)S(1)} %get-tuple-element.30), channel_id=1, source_target_pairs={{0,4},{4,0},{8,12},{12,8},{1,5},{5,1},{9,13},{13,9},{2,6},{6,2},{1... | collective-permute-start | bytes 98312 | tf_op jit(solution)/shard_map/ppermute | solution.py:408
  67.6 1.3 %collective-permute-start.20 = (bf16[64,256]{1,0:T(8,128)(2,1)S(1)}, bf16[64,256]{1,0:T(8,128)(2,1)S(1)}, u32[]{:S(2)}, u32[]{:S(2)}) collective-permute-start(bf16[64,256]{1,0:T(8,128)(2,1)S(1)} %shard_map.96), channel_id=1, source_target_pairs={{0,1},{1,0},{2,3},{3,2},{4,5},{5,4},{6,7},{7,6},{8,9},{9,8},{10,11... | collective-permute-start | bytes 98312 | tf_op jit(solution)/shard_map/ppermute | solution.py:403
  68.9 3.2 %collective-permute-start.21 = (bf16[64,384]{1,0:T(8,128)(2,1)S(1)}, bf16[64,384]{1,0:T(8,128)(2,1)S(1)}, u32[]{:S(2)}, u32[]{:S(2)}) collective-permute-start(bf16[64,384]{1,0:T(8,128)(2,1)S(1)} %pad_maximum_fusion.1), channel_id=1, source_target_pairs={{1,0},{5,1},{11,2},{15,3},{0,4},{4,5},{10,6},{14,7},{3,8},{7,9},{9... | collective-permute-start | bytes 147464 | tf_op jit(solution)/shard_map/ppermute | solution.py:445
  69.2 5.0 %collective-permute-start.22 = (bf16[64,384]{1,0:T(8,128)(2,1)S(1)}, bf16[64,384]{1,0:T(8,128)(2,1)S(1)}, u32[]{:S(2)}, u32[]{:S(2)}) collective-permute-start(bf16[64,384]{1,0:T(8,128)(2,1)S(1)} %pad_maximum_fusion.1), channel_id=1, source_target_pairs={{3,0},{7,1},{9,2},{13,3},{2,4},{6,5},{8,6},{12,7},{1,8},{5,9},{11,... | collective-permute-start | bytes 147464 | tf_op jit(solution)/shard_map/ppermute | solution.py:445

commit v4 on v3

--- a/solution.py
+++ b/solution.py
@@ -181,13 +181,14 @@
     sems,
 ):
     size = group_of(live_ref)
-    groups = feats_ref.shape[0] // size
+    bounds = sorted({0, size, feats_ref.shape[0]})
+    groups = len(bounds) - 1
     copies = [
         pltpu.make_async_copy(mask_hbm, mask_ref, sems.at[groups + 1]),
         pltpu.make_async_copy(weights_hbm.at[layer], weights_ref, sems.at[groups]),
     ]
     for index in range(groups):
-        at = pl.ds(index * size, size)
+        at = pl.ds(bounds[index], bounds[index + 1] - bounds[index])
         copies.append(
             pltpu.make_async_copy(feats_hbm.at[at], feats_ref.at[at], sems.at[index])
         )
@@ -200,8 +201,8 @@
     copies[1].wait()
     for index in range(groups):
         copies[2 + index].wait()
-        low = index * size
-        project_rows(plan, live_ref, feats_ref, weights_ref, own_ref, other_ref, low, low + size)
+        low, high = bounds[index], bounds[index + 1]
+        project_rows(plan, live_ref, feats_ref, weights_ref, own_ref, other_ref, low, high)
 
 
 def attend(plan, query, scale_ref, own_ref, recv_ref, chunk_refs, mix):

time: 76.8 us -> 76.5 us (level)
  the two profiles are of different devices: /device:TPU:0 before, /device:TPU:2 now
where the time goes in v4:
time: 76.5 us; the launch traced here: 76.2 us
  waiting for transfers between devices  34.6 us (45%)
  starting transfers between devices  20.3 us (27%)
  Pallas kernels  17.8 us (23%)
  local copies, waits for them, and re-layouts  1.86 us (2%)
  between operations  0.93 us (1%)
  other arithmetic  0.83 us (1%)
    ppermute x11, waiting for transfers between devices, swap(): return lax.ppermute(value, axis, [(i, i ^ 1) for i in range(size)])  20 us
    pallas_call x7, Pallas kernels, vmem_call(): pl.pallas_call(kernel, out_shape=out_shape, in_specs=specs, out_specs=[pl...  17.8 us
    ppermute x6, starting transfers between devices, exchange(): lax.ppermute(chunks[d], 'tiles', [(i, i ^ d) for i in range(plan.n_t)])  8.9 us
    ppermute x2, waiting for transfers between devices, collect(): received.append(lax.ppermute(block, axes, links))  6.36 us
    ppermute x4, starting transfers between devices, spread(): received.append(lax.ppermute(block, axes, links))  5.76 us
    ppermute x4, waiting for transfers between devices, spread(): received.append(lax.ppermute(block, axes, links))  4.3 us
    ppermute x11, starting transfers between devices, swap(): return lax.ppermute(value, axis, [(i, i ^ 1) for i in range(size)])  4.03 us
    ppermute x6, waiting for transfers between devices, exchange(): lax.ppermute(chunks[d], 'tiles', [(i, i ^ d) for i in range(plan.n_t)])  3.88 us
  transfers between devices with their start and end apart: 23, of which 12 were waited for; matrix products, arithmetic and copies ran while one was open for 1% of the time, Pallas kernels for 8%

profile of v4, /device:TPU:2, one launch (start us, length us, event | category | flops | bytes accessed | tf_op | source)
XLA Modules:
  0.0 76.2 jit_solution(7695330958236204277)
XLA Ops:
  0.0 0.0 copy-start.8
  0.7 4.6 %shard_map.91 = (bf16[1536,256]{1,0:T(8,128)(2,1)S(1)}, bf16[1536,256]{1,0:T(8,128)(2,1)S(1)}) custom-call(s32[1]{0:T(128)S(6)} %copy.13.count_ref, bf16[1536,1536]{1,0:T(8,128)(2,1)} %feats_hbm.3, bf16[2,1536,384]{2,1,0:T(8,128)(2,1)} %bitcast.4, s32[6,256]{1,0:T(8,128)} %mask_hbm.3), custom_call_target="tpu_custom_call" | custom-call | flops 1811939328 | bytes 1048576 | tf_op jit(solution)/shard_map/pallas_call | solution.py:377
  5.4 0.1 collective-permute-start.3
  5.4 0.0 copy-done.2
  5.5 0.1 collective-permute-start.1
  5.5 0.4 collective-permute-start
  5.9 4.7 %collective-permute-done.1.qx_ref = bf16[64,768]{1,0:T(8,128)(2,1)S(1)} collective-permute-done((bf16[64,768]{1,0:T(8,128)(2,1)S(1)}, bf16[64,768]{1,0:T(8,128)(2,1)S(1)}, u32[]{:S(2)}, u32[]{:S(2)}) %collective-permute-start.1) | collective-permute-done | bytes 98336 | tf_op jit(solution)/shard_map/ppermute | solution.py:404
  10.6 0.0 collective-permute-start.2
  10.6 0.0 collective-permute-done.qk_ref
  10.7 1.3 %collective-permute-done.2.qxk_ref = bf16[64,768]{1,0:T(8,128)(2,1)S(1)} collective-permute-done((bf16[64,768]{1,0:T(8,128)(2,1)S(1)}, bf16[64,768]{1,0:T(8,128)(2,1)S(1)}, u32[]{:S(2)}, u32[]{:S(2)}) %collective-permute-start.2) | collective-permute-done | bytes 98336 | tf_op jit(solution)/shard_map/ppermute | solution.py:404
  11.9 0.0 collective-permute-done.3.recv_ref
  12.0 0.0 copy-done
  12.0 0.0 copy-done.7
  12.0 0.0 copy-done.8
  12.0 0.0 copy-start.1
  12.0 2.7 %shard_map.92 = (f32[64,256]{1,0:T(8,128)S(1)}, bf16[64,256]{1,0:T(8,128)(2,1)S(1)}, bf16[64,256]{1,0:T(8,128)(2,1)S(1)}, bf16[64,256]{1,0:T(8,128)(2,1)S(1)}) custom-call(f32[6]{0:T(128)S(1)} %copy-done.8, bf16[64,768]{1,0:T(8,128)(2,1)S(1)} %copy-done.2, bf16[64,768]{1,0:T(8,128)(2,1)S(1)} %collective-permute-done.qk_ref, ...), custom_call_target="tpu_custom_call" | custom-call | flops 402653184 | bytes 1048576 | tf_op jit(solution)/shard_map/pallas_call | solution.py:377
  14.7 3.7 %collective-permute-start.4 = (bf16[64,256]{1,0:T(8,128)(2,1)S(1)}, bf16[64,256]{1,0:T(8,128)(2,1)S(1)}, u32[]{:S(2)}, u32[]{:S(2)}) collective-permute-start(bf16[64,256]{1,0:T(8,128)(2,1)S(1)} %get-tuple-element.21), channel_id=1, source_target_pairs={{0,12},{4,8},{8,4},{12,0},{1,13},{5,9},{9,5},{13,1},{2,14},{6,10},... | collective-permute-start | bytes 98312 | tf_op jit(solution)/shard_map/ppermute | solution.py:409
  18.4 0.0 collective-permute-start.5
  18.4 0.0 copy-done.3
  18.4 0.0 copy-done.5
  18.4 0.8 %collective-permute-start.6 = (bf16[64,256]{1,0:T(8,128)(2,1)S(1)}, bf16[64,256]{1,0:T(8,128)(2,1)S(1)}, u32[]{:S(2)}, u32[]{:S(2)}) collective-permute-start(bf16[64,256]{1,0:T(8,128)(2,1)S(1)} %get-tuple-element.23), channel_id=1, source_target_pairs={{0,4},{4,0},{8,12},{12,8},{1,5},{5,1},{9,13},{13,9},{2,6},{6,2},{1... | collective-permute-start | bytes 98312 | tf_op jit(solution)/shard_map/ppermute | solution.py:409
  19.1 5.5 %shard_map.94 = (bf16[1536,256]{1,0:T(8,128)(2,1)S(1)}, bf16[1536,256]{1,0:T(8,128)(2,1)}) custom-call(s32[1]{0:T(128)S(6)} %copy.13.count_ref, bf16[1536,1536]{1,0:T(8,128)(2,1)} %feats_hbm.3, bf16[2,1536,384]{2,1,0:T(8,128)(2,1)} %bitcast.5, s32[6,256]{1,0:T(8,128)} %mask_hbm.3), custom_call_target="tpu_custom_call" | custom-call | flops 1811939328 | bytes 1048576 | tf_op jit(solution)/shard_map/pallas_call | solution.py:377
  24.6 0.1 collective-permute-start.16
  24.7 0.5 collective-permute-start.14
  25.2 0.0 collective-permute-done.4.refs_1_
  25.2 0.0 collective-permute-done.5.refs_2_
  25.2 0.0 collective-permute-done.6.refs_3_
  25.2 0.7 shard_map.93
  25.9 0.1 collective-permute-start.7
  26.1 1.4 %collective-permute-done.7 = bf16[64,256]{1,0:T(8,128)(2,1)} collective-permute-done((bf16[64,256]{1,0:T(8,128)(2,1)}, bf16[64,256]{1,0:T(8,128)(2,1)}, u32[]{:S(2)}, u32[]{:S(2)}) %collective-permute-start.7) | collective-permute-done | bytes 32800 | tf_op jit(solution)/shard_map/ppermute | solution.py:404
  27.5 0.8 %broadcast_select_fusion.3 = (bf16[64,256]{1,0:T(8,128)(2,1)S(1)}, bf16[64,256]{1,0:T(8,128)(2,1)S(1)}) fusion(bf16[64,256]{1,0:T(8,128)(2,1)} %shard_map.93, bf16[64,256]{1,0:T(8,128)(2,1)} %collective-permute-done.7, pred[]{:T(512)S(6)} %eq.2), kind=kLoop, calls=%fused_computation.5 | loop fusion | flops 32768 | bytes 131073 | tf_op jit(solution)/shard_map/jit(_where)/select_n | solution.py:415
  28.3 1.5 %collective-permute-start.8 = (bf16[64,384]{1,0:T(8,128)(2,1)S(1)}, bf16[64,384]{1,0:T(8,128)(2,1)S(1)}, u32[]{:S(2)}, u32[]{:S(2)}) collective-permute-start(bf16[64,384]{1,0:T(8,128)(2,1)S(1)} %pad_maximum_fusion.block_ref), channel_id=1, source_target_pairs={{0,4},{1,7},{2,6},{3,5},{4,0},{5,3},{6,2},{7,1},{8,12},{9,15},{10,... | collective-permute-start | bytes 147464 | tf_op jit(solution)/shard_map/ppermute | solution.py:433
  29.8 0.8 %collective-permute-start.13 = (bf16[2,192,768]{2,1,0:T(8,128)(2,1)S(1)}, bf16[2,192,768]{2,1,0:T(8,128)(2,1)S(1)}, u32[]{:S(2)}, u32[]{:S(2)}) collective-permute-start(bf16[2,192,768]{2,1,0:T(8,128)(2,1)S(1)} %copy-done.1), channel_id=1, source_target_pairs={{0,1},{1,0},{2,3},{3,2},{4,5},{5,4},{6,7},{7,6},{8,9},{9,8},{10,11... | collective-permute-start | bytes 1769480 | tf_op jit(solution)/shard_map/ppermute | solution.py:404
  30.6 10.3 %collective-permute-done.14.wo2 = bf16[2,192,768]{2,1,0:T(8,128)(2,1)S(1)} collective-permute-done((bf16[2,192,768]{2,1,0:T(8,128)(2,1)S(1)}, bf16[2,192,768]{2,1,0:T(8,128)(2,1)S(1)}, u32[]{:S(2)}, u32[]{:S(2)}) %collective-permute-start.14) | collective-permute-done | bytes 589856 | tf_op jit(solution)/shard_map/ppermute | solution.py:404
  41.0 0.0 collective-permute-start.15
  41.0 3.6 %collective-permute-start.9 = (bf16[64,384]{1,0:T(8,128)(2,1)S(1)}, bf16[64,384]{1,0:T(8,128)(2,1)S(1)}, u32[]{:S(2)}, u32[]{:S(2)}) collective-permute-start(bf16[64,384]{1,0:T(8,128)(2,1)S(1)} %pad_maximum_fusion.block_ref), channel_id=1, source_target_pairs={{0,14},{1,13},{2,12},{3,15},{4,10},{5,9},{6,8},{7,11},{8,6},{9,5},... | collective-permute-start | bytes 147464 | tf_op jit(solution)/shard_map/ppermute | solution.py:433
  44.6 0.0 collective-permute-done.8
  44.6 0.0 collective-permute-start.10
  44.6 3.2 %collective-permute-done.9 = bf16[64,384]{1,0:T(8,128)(2,1)S(1)} collective-permute-done((bf16[64,384]{1,0:T(8,128)(2,1)S(1)}, bf16[64,384]{1,0:T(8,128)(2,1)S(1)}, u32[]{:S(2)}, u32[]{:S(2)}) %collective-permute-start.9) | collective-permute-done | bytes 49184 | tf_op jit(solution)/shard_map/ppermute | solution.py:433
  47.8 0.7 collective-permute-start.11
  48.5 1.1 %collective-permute-done.10 = bf16[64,384]{1,0:T(8,128)(2,1)S(1)} collective-permute-done((bf16[64,384]{1,0:T(8,128)(2,1)S(1)}, bf16[64,384]{1,0:T(8,128)(2,1)S(1)}, u32[]{:S(2)}, u32[]{:S(2)}) %collective-permute-start.10) | collective-permute-done | bytes 49184 | tf_op jit(solution)/shard_map/ppermute | solution.py:433
  49.6 0.0 collective-permute-done.11
  49.6 1.9 %collective-permute-start.12 = (bf16[256,384]{1,0:T(8,128)(2,1)S(1)}, bf16[256,384]{1,0:T(8,128)(2,1)S(1)}, u32[]{:S(2)}, u32[]{:S(2)}) collective-permute-start(bf16[256,384]{1,0:T(8,128)(2,1)S(1)} %constant_dynamic-update-slice_fusion.near_ref), channel_id=1, source_target_pairs={{0,1},{1,0},{2,3},{3,2},{4,5},{5,4},{6,7},{7,6},{8,9},{9,8},{10,11... | collective-permute-start | bytes 589832 | tf_op jit(solution)/shard_map/ppermute | solution.py:404
  51.5 0.0 collective-permute-done.13.wo1
  51.5 0.0 collective-permute-done.16.recv_ref
  51.5 1.1 %collective-permute-done.12.far_ref = bf16[256,384]{1,0:T(8,128)(2,1)S(1)} collective-permute-done((bf16[256,384]{1,0:T(8,128)(2,1)S(1)}, bf16[256,384]{1,0:T(8,128)(2,1)S(1)}, u32[]{:S(2)}, u32[]{:S(2)}) %collective-permute-start.12) | collective-permute-done | bytes 196640 | tf_op jit(solution)/shard_map/ppermute | solution.py:404
  52.6 0.0 collective-permute-done.15.wo3
  52.6 0.9 %copy-done.4 = bf16[64,768]{1,0:T(8,128)(2,1)S(1)} copy-done((bf16[64,768]{1,0:T(8,128)(2,1)S(1)}, bf16[64,768]{1,0:T(8,128)(2,1)}, u32[]{:S(2)}) %copy-start.4) | copy-done | bytes 98328
  53.5 0.9 %copy-done.6 = bf16[64,768]{1,0:T(8,128)(2,1)S(1)} copy-done((bf16[64,768]{1,0:T(8,128)(2,1)S(1)}, bf16[64,768]{1,0:T(8,128)(2,1)}, u32[]{:S(2)}) %copy-start.6) | copy-done | bytes 98328
  54.4 3.0 %shard_map.95 = (f32[64,256]{1,0:T(8,128)S(1)}, bf16[64,256]{1,0:T(8,128)(2,1)S(1)}, bf16[64,256]{1,0:T(8,128)(2,1)S(1)}, bf16[64,256]{1,0:T(8,128)(2,1)S(1)}, f32[64,768]{1,0:T(8,128)S(1)}) custom-call(f32[6]{0:T(128)S(1)} %copy-done.8, bf16[64,768]{1,0:T(8,128)(2,1)S(1)} %copy-done.2, bf16[64,768]{1,0:T(8,128)(2,1)S(1)} %copy-done.4, ...), custom_call_target="tpu_custom_call" | custom-call | flops 402653184 | bytes 1048576 | tf_op jit(solution)/shard_map/pallas_call | solution.py:377
  57.4 3.5 %collective-permute-start.17 = (bf16[64,256]{1,0:T(8,128)(2,1)S(1)}, bf16[64,256]{1,0:T(8,128)(2,1)S(1)}, u32[]{:S(2)}, u32[]{:S(2)}) collective-permute-start(bf16[64,256]{1,0:T(8,128)(2,1)S(1)} %get-tuple-element.28), channel_id=1, source_target_pairs={{0,12},{4,8},{8,4},{12,0},{1,13},{5,9},{9,5},{13,1},{2,14},{6,10},... | collective-permute-start | bytes 98312 | tf_op jit(solution)/shard_map/ppermute | solution.py:409
  60.9 0.0 collective-permute-start.18
  60.9 0.9 %collective-permute-start.19 = (bf16[64,256]{1,0:T(8,128)(2,1)S(1)}, bf16[64,256]{1,0:T(8,128)(2,1)S(1)}, u32[]{:S(2)}, u32[]{:S(2)}) collective-permute-start(bf16[64,256]{1,0:T(8,128)(2,1)S(1)} %get-tuple-element.30), channel_id=1, source_target_pairs={{0,4},{4,0},{8,12},{12,8},{1,5},{5,1},{9,13},{13,9},{2,6},{6,2},{1... | collective-permute-start | bytes 98312 | tf_op jit(solution)/shard_map/ppermute | solution.py:409
  61.9 1.4 %collective-permute-done.17.refs_1_ = bf16[64,256]{1,0:T(8,128)(2,1)S(1)} collective-permute-done((bf16[64,256]{1,0:T(8,128)(2,1)S(1)}, bf16[64,256]{1,0:T(8,128)(2,1)S(1)}, u32[]{:S(2)}, u32[]{:S(2)}) %collective-permute-start.17) | collective-permute-done | bytes 32800 | tf_op jit(solution)/shard_map/ppermute | solution.py:409
  63.3 2.4 %collective-permute-done.18.refs_2_ = bf16[64,256]{1,0:T(8,128)(2,1)S(1)} collective-permute-done((bf16[64,256]{1,0:T(8,128)(2,1)S(1)}, bf16[64,256]{1,0:T(8,128)(2,1)S(1)}, u32[]{:S(2)}, u32[]{:S(2)}) %collective-permute-start.18) | collective-permute-done | bytes 32800 | tf_op jit(solution)/shard_map/ppermute | solution.py:409
  65.7 0.0 collective-permute-done.19.refs_3_
  65.7 0.1 shard_map.96
  65.9 0.1 collective-permute-start.20
  66.0 1.2 %collective-permute-done.20 = bf16[64,256]{1,0:T(8,128)(2,1)S(1)} collective-permute-done((bf16[64,256]{1,0:T(8,128)(2,1)S(1)}, bf16[64,256]{1,0:T(8,128)(2,1)S(1)}, u32[]{:S(2)}, u32[]{:S(2)}) %collective-permute-start.20) | collective-permute-done | bytes 32800 | tf_op jit(solution)/shard_map/ppermute | solution.py:404
  67.2 1.6 %collective-permute-start.21 = (bf16[64,384]{1,0:T(8,128)(2,1)S(1)}, bf16[64,384]{1,0:T(8,128)(2,1)S(1)}, u32[]{:S(2)}, u32[]{:S(2)}) collective-permute-start(bf16[64,384]{1,0:T(8,128)(2,1)S(1)} %pad_maximum_fusion.1), channel_id=1, source_target_pairs={{1,0},{5,1},{11,2},{15,3},{0,4},{4,5},{10,6},{14,7},{3,8},{7,9},{9... | collective-permute-start | bytes 147464 | tf_op jit(solution)/shard_map/ppermute | solution.py:446
  68.8 0.0 collective-permute-start.22
  68.8 4.2 %collective-permute-done.21.near_ref = bf16[64,384]{1,0:T(8,128)(2,1)S(1)} collective-permute-done((bf16[64,384]{1,0:T(8,128)(2,1)S(1)}, bf16[64,384]{1,0:T(8,128)(2,1)S(1)}, u32[]{:S(2)}, u32[]{:S(2)}) %collective-permute-start.21) | collective-permute-done | bytes 49184 | tf_op jit(solution)/shard_map/ppermute | solution.py:446
  72.9 2.2 %collective-permute-done.22.far_ref = bf16[64,384]{1,0:T(8,128)(2,1)S(1)} collective-permute-done((bf16[64,384]{1,0:T(8,128)(2,1)S(1)}, bf16[64,384]{1,0:T(8,128)(2,1)S(1)}, u32[]{:S(2)}, u32[]{:S(2)}) %collective-permute-start.22) | collective-permute-done | bytes 49184 | tf_op jit(solution)/shard_map/ppermute | solution.py:446
  75.1 1.1 %shard_map.97 = f32[64,768]{1,0:T(8,128)} custom-call(f32[64,768]{1,0:T(8,128)S(1)} %get-tuple-element.26.kept_ref, bf16[64,384]{1,0:T(8,128)(2,1)S(1)} %collective-permute-done.21.near_ref, bf16[64,384]{1,0:T(8,128)(2,1)S(1)} %collective-permute-done.22.far_ref, bf16[2,192,768]{2,1,0:T(8,128)(2,1)S(1)} %copy-done.1, ...), custom_call_target="tpu_custom_call" | custom-call | flops 75497472 | bytes 1048576 | tf_op jit(solution)/shard_map/pallas_call | solution.py:377
  (18 shorter events, 0.1 us)
Async XLA Ops:
  0.0 5.4 %copy-start.2 = (bf16[64,768]{1,0:T(8,128)(2,1)S(1)}, bf16[64,768]{1,0:T(8,128)(2,1)}, u32[]{:S(2)}) copy-start(bf16[64,768]{1,0:T(8,128)(2,1)} %q_ref.3) | copy-start | bytes 294916
  0.0 12.0 %copy-start = (bf16[2,768,192]{1,2,0:T(8,128)(2,1)S(1)}, bf16[2,768,192]{1,2,0:T(8,128)(2,1)}, u32[]{:S(2)}) copy-start(bf16[2,768,192]{1,2,0:T(8,128)(2,1)} %param.15) | copy-start | bytes 1769476
  0.0 12.0 %copy-start.7 = (f32[2,768]{1,0:T(2,128)S(1)}, f32[2,768]{1,0:T(2,128)}, u32[]{:S(2)}) copy-start(f32[2,768]{1,0:T(2,128)} %gain_ref.3) | copy-start | bytes 18436
  0.0 12.0 %copy-start.8 = (f32[6]{0:T(128)S(1)}, f32[6]{0:T(128)}, u32[]{:S(2)}) copy-start(f32[6]{0:T(128)} %scale_ref.3) | copy-start | bytes 76
  5.4 6.6 %collective-permute-start.3 = (bf16[1536,256]{1,0:T(8,128)(2,1)S(1)}, bf16[1536,256]{1,0:T(8,128)(2,1)S(1)}, u32[]{:S(2)}, u32[]{:S(2)}) collective-permute-start(bf16[1536,256]{1,0:T(8,128)(2,1)S(1)} %get-tuple-element.19), channel_id=1, source_target_pairs={{0,1},{1,0},{2,3},{3,2},{4,5},{5,4},{6,7},{7,6},{8,9},{9,8},{10,11... | collective-permute-start | bytes 2359304 | tf_op jit(solution)/shard_map/ppermute | solution.py:404
  5.5 5.2 %collective-permute-start.1 = (bf16[64,768]{1,0:T(8,128)(2,1)S(1)}, bf16[64,768]{1,0:T(8,128)(2,1)S(1)}, u32[]{:S(2)}, u32[]{:S(2)}) collective-permute-start(bf16[64,768]{1,0:T(8,128)(2,1)S(1)} %copy-done.2), channel_id=1, source_target_pairs={{0,2},{2,0},{1,3},{3,1},{4,6},{6,4},{5,7},{7,5},{8,10},{10,8},{9,1... | collective-permute-start | bytes 294920 | tf_op jit(solution)/shard_map/ppermute | solution.py:404
  5.5 5.1 %collective-permute-start = (bf16[64,768]{1,0:T(8,128)(2,1)S(1)}, bf16[64,768]{1,0:T(8,128)(2,1)S(1)}, u32[]{:S(2)}, u32[]{:S(2)}) collective-permute-start(bf16[64,768]{1,0:T(8,128)(2,1)S(1)} %copy-done.2), channel_id=1, source_target_pairs={{0,1},{1,0},{2,3},{3,2},{4,5},{5,4},{6,7},{7,6},{8,9},{9,8},{10,11... | collective-permute-start | bytes 294920 | tf_op jit(solution)/shard_map/ppermute | solution.py:404
  10.6 1.3 %collective-permute-start.2 = (bf16[64,768]{1,0:T(8,128)(2,1)S(1)}, bf16[64,768]{1,0:T(8,128)(2,1)S(1)}, u32[]{:S(2)}, u32[]{:S(2)}) collective-permute-start(bf16[64,768]{1,0:T(8,128)(2,1)S(1)} %collective-permute-done.1.qx_ref), channel_id=1, source_target_pairs={{0,1},{1,0},{2,3},{3,2},{4,5},{5,4},{6,7},{7,6},{8,9},{9,8},{10,11... | collective-permute-start | bytes 294920 | tf_op jit(solution)/shard_map/ppermute | solution.py:404
  10.7 7.7 %copy-start.3 = (bf16[64,768]{1,0:T(8,128)(2,1)}, bf16[64,768]{1,0:T(8,128)(2,1)S(1)}, u32[]{:S(2)}) copy-start(bf16[64,768]{1,0:T(8,128)(2,1)S(1)} %collective-permute-done.qk_ref) | copy-start | bytes 294916
  11.9 6.4 %copy-start.5 = (bf16[64,768]{1,0:T(8,128)(2,1)}, bf16[64,768]{1,0:T(8,128)(2,1)S(1)}, u32[]{:S(2)}) copy-start(bf16[64,768]{1,0:T(8,128)(2,1)S(1)} %collective-permute-done.2.qxk_ref) | copy-start | bytes 294916
  12.0 12.7 %copy-start.1 = (bf16[2,192,768]{2,1,0:T(8,128)(2,1)S(1)}, bf16[2,192,768]{2,1,0:T(8,128)(2,1)}, u32[]{:S(2)}) copy-start(bf16[2,192,768]{2,1,0:T(8,128)(2,1)} %wo0.3) | copy-start | bytes 1769476
  14.7 10.5 %collective-permute-start.4 = (bf16[64,256]{1,0:T(8,128)(2,1)S(1)}, bf16[64,256]{1,0:T(8,128)(2,1)S(1)}, u32[]{:S(2)}, u32[]{:S(2)}) collective-permute-start(bf16[64,256]{1,0:T(8,128)(2,1)S(1)} %get-tuple-element.21), channel_id=1, source_target_pairs={{0,12},{4,8},{8,4},{12,0},{1,13},{5,9},{9,5},{13,1},{2,14},{6,10},... | collective-permute-start | bytes 98312 | tf_op jit(solution)/shard_map/ppermute | solution.py:409
  18.4 6.8 %collective-permute-start.5 = (bf16[64,256]{1,0:T(8,128)(2,1)S(1)}, bf16[64,256]{1,0:T(8,128)(2,1)S(1)}, u32[]{:S(2)}, u32[]{:S(2)}) collective-permute-start(bf16[64,256]{1,0:T(8,128)(2,1)S(1)} %get-tuple-element.22), channel_id=1, source_target_pairs={{0,8},{4,12},{8,0},{12,4},{1,9},{5,13},{9,1},{13,5},{2,10},{6,14},... | collective-permute-start | bytes 98312 | tf_op jit(solution)/shard_map/ppermute | solution.py:409
  18.4 6.8 %collective-permute-start.6 = (bf16[64,256]{1,0:T(8,128)(2,1)S(1)}, bf16[64,256]{1,0:T(8,128)(2,1)S(1)}, u32[]{:S(2)}, u32[]{:S(2)}) collective-permute-start(bf16[64,256]{1,0:T(8,128)(2,1)S(1)} %get-tuple-element.23), channel_id=1, source_target_pairs={{0,4},{4,0},{8,12},{12,8},{1,5},{5,1},{9,13},{13,9},{2,6},{6,2},{1... | collective-permute-start | bytes 98312 | tf_op jit(solution)/shard_map/ppermute | solution.py:409
  24.6 26.9 %collective-permute-start.16 = (bf16[1536,256]{1,0:T(8,128)(2,1)}, bf16[1536,256]{1,0:T(8,128)(2,1)S(1)}, u32[]{:S(2)}, u32[]{:S(2)}) collective-permute-start(bf16[1536,256]{1,0:T(8,128)(2,1)} %get-tuple-element.25), channel_id=1, source_target_pairs={{0,1},{1,0},{2,3},{3,2},{4,5},{5,4},{6,7},{7,6},{8,9},{9,8},{10,11... | collective-permute-start | bytes 2359304 | tf_op jit(solution)/shard_map/ppermute | solution.py:404
  24.7 16.2 %collective-permute-start.14 = (bf16[2,192,768]{2,1,0:T(8,128)(2,1)S(1)}, bf16[2,192,768]{2,1,0:T(8,128)(2,1)S(1)}, u32[]{:S(2)}, u32[]{:S(2)}) collective-permute-start(bf16[2,192,768]{2,1,0:T(8,128)(2,1)S(1)} %copy-done.1), channel_id=1, source_target_pairs={{0,2},{2,0},{1,3},{3,1},{4,6},{6,4},{5,7},{7,5},{8,10},{10,8},{9,1... | collective-permute-start | bytes 1769480 | tf_op jit(solution)/shard_map/ppermute | solution.py:404
  25.9 1.6 %collective-permute-start.7 = (bf16[64,256]{1,0:T(8,128)(2,1)}, bf16[64,256]{1,0:T(8,128)(2,1)}, u32[]{:S(2)}, u32[]{:S(2)}) collective-permute-start(bf16[64,256]{1,0:T(8,128)(2,1)} %shard_map.93), channel_id=1, source_target_pairs={{0,1},{1,0},{2,3},{3,2},{4,5},{5,4},{6,7},{7,6},{8,9},{9,8},{10,11... | collective-permute-start | bytes 98312 | tf_op jit(solution)/shard_map/ppermute | solution.py:404
  28.3 16.3 %collective-permute-start.8 = (bf16[64,384]{1,0:T(8,128)(2,1)S(1)}, bf16[64,384]{1,0:T(8,128)(2,1)S(1)}, u32[]{:S(2)}, u32[]{:S(2)}) collective-permute-start(bf16[64,384]{1,0:T(8,128)(2,1)S(1)} %pad_maximum_fusion.block_ref), channel_id=1, source_target_pairs={{0,4},{1,7},{2,6},{3,5},{4,0},{5,3},{6,2},{7,1},{8,12},{9,15},{10,... | collective-permute-start | bytes 147464 | tf_op jit(solution)/shard_map/ppermute | solution.py:433
  29.8 21.7 %collective-permute-start.13 = (bf16[2,192,768]{2,1,0:T(8,128)(2,1)S(1)}, bf16[2,192,768]{2,1,0:T(8,128)(2,1)S(1)}, u32[]{:S(2)}, u32[]{:S(2)}) collective-permute-start(bf16[2,192,768]{2,1,0:T(8,128)(2,1)S(1)} %copy-done.1), channel_id=1, source_target_pairs={{0,1},{1,0},{2,3},{3,2},{4,5},{5,4},{6,7},{7,6},{8,9},{9,8},{10,11... | collective-permute-start | bytes 1769480 | tf_op jit(solution)/shard_map/ppermute | solution.py:404
  41.0 11.6 %collective-permute-start.15 = (bf16[2,192,768]{2,1,0:T(8,128)(2,1)S(1)}, bf16[2,192,768]{2,1,0:T(8,128)(2,1)S(1)}, u32[]{:S(2)}, u32[]{:S(2)}) collective-permute-start(bf16[2,192,768]{2,1,0:T(8,128)(2,1)S(1)} %collective-permute-done.14.wo2), channel_id=1, source_target_pairs={{0,1},{1,0},{2,3},{3,2},{4,5},{5,4},{6,7},{7,6},{8,9},{9,8},{10,11... | collective-permute-start | bytes 1769480 | tf_op jit(solution)/shard_map/ppermute | solution.py:404
  41.0 6.8 %collective-permute-start.9 = (bf16[64,384]{1,0:T(8,128)(2,1)S(1)}, bf16[64,384]{1,0:T(8,128)(2,1)S(1)}, u32[]{:S(2)}, u32[]{:S(2)}) collective-permute-start(bf16[64,384]{1,0:T(8,128)(2,1)S(1)} %pad_maximum_fusion.block_ref), channel_id=1, source_target_pairs={{0,14},{1,13},{2,12},{3,15},{4,10},{5,9},{6,8},{7,11},{8,6},{9,5},... | collective-permute-start | bytes 147464 | tf_op jit(solution)/shard_map/ppermute | solution.py:433
  44.6 5.0 %collective-permute-start.10 = (bf16[64,384]{1,0:T(8,128)(2,1)S(1)}, bf16[64,384]{1,0:T(8,128)(2,1)S(1)}, u32[]{:S(2)}, u32[]{:S(2)}) collective-permute-start(bf16[64,384]{1,0:T(8,128)(2,1)S(1)} %pad_maximum_fusion.block_ref), channel_id=1, source_target_pairs={{0,8},{1,11},{2,10},{3,9},{4,12},{5,15},{6,14},{7,13},{8,0},{9,3},... | collective-permute-start | bytes 147464 | tf_op jit(solution)/shard_map/ppermute | solution.py:433
  47.8 1.8 %collective-permute-start.11 = (bf16[64,384]{1,0:T(8,128)(2,1)S(1)}, bf16[64,384]{1,0:T(8,128)(2,1)S(1)}, u32[]{:S(2)}, u32[]{:S(2)}) collective-permute-start(bf16[64,384]{1,0:T(8,128)(2,1)S(1)} %pad_maximum_fusion.block_ref), channel_id=1, source_target_pairs={{1,3},{3,1},{5,7},{7,5},{9,11},{11,9},{13,15},{15,13},{17,19},{19,... | collective-permute-start | bytes 147464 | tf_op jit(solution)/shard_map/ppermute | solution.py:433
  49.6 3.0 %collective-permute-start.12 = (bf16[256,384]{1,0:T(8,128)(2,1)S(1)}, bf16[256,384]{1,0:T(8,128)(2,1)S(1)}, u32[]{:S(2)}, u32[]{:S(2)}) collective-permute-start(bf16[256,384]{1,0:T(8,128)(2,1)S(1)} %constant_dynamic-update-slice_fusion.near_ref), channel_id=1, source_target_pairs={{0,1},{1,0},{2,3},{3,2},{4,5},{5,4},{6,7},{7,6},{8,9},{9,8},{10,11... | collective-permute-start | bytes 589832 | tf_op jit(solution)/shard_map/ppermute | solution.py:404
  52.6 0.9 %copy-start.4 = (bf16[64,768]{1,0:T(8,128)(2,1)S(1)}, bf16[64,768]{1,0:T(8,128)(2,1)}, u32[]{:S(2)}) copy-start(bf16[64,768]{1,0:T(8,128)(2,1)} %copy-done.3) | copy-start | bytes 294916
  53.5 0.9 %copy-start.6 = (bf16[64,768]{1,0:T(8,128)(2,1)S(1)}, bf16[64,768]{1,0:T(8,128)(2,1)}, u32[]{:S(2)}) copy-start(bf16[64,768]{1,0:T(8,128)(2,1)} %copy-done.5) | copy-start | bytes 294916
  57.4 5.9 %collective-permute-start.17 = (bf16[64,256]{1,0:T(8,128)(2,1)S(1)}, bf16[64,256]{1,0:T(8,128)(2,1)S(1)}, u32[]{:S(2)}, u32[]{:S(2)}) collective-permute-start(bf16[64,256]{1,0:T(8,128)(2,1)S(1)} %get-tuple-element.28), channel_id=1, source_target_pairs={{0,12},{4,8},{8,4},{12,0},{1,13},{5,9},{9,5},{13,1},{2,14},{6,10},... | collective-permute-start | bytes 98312 | tf_op jit(solution)/shard_map/ppermute | solution.py:409
  60.9 4.8 %collective-permute-start.18 = (bf16[64,256]{1,0:T(8,128)(2,1)S(1)}, bf16[64,256]{1,0:T(8,128)(2,1)S(1)}, u32[]{:S(2)}, u32[]{:S(2)}) collective-permute-start(bf16[64,256]{1,0:T(8,128)(2,1)S(1)} %get-tuple-element.29), channel_id=1, source_target_pairs={{0,8},{4,12},{8,0},{12,4},{1,9},{5,13},{9,1},{13,5},{2,10},{6,14},... | collective-permute-start | bytes 98312 | tf_op jit(solution)/shard_map/ppermute | solution.py:409
  60.9 4.8 %collective-permute-start.19 = (bf16[64,256]{1,0:T(8,128)(2,1)S(1)}, bf16[64,256]{1,0:T(8,128)(2,1)S(1)}, u32[]{:S(2)}, u32[]{:S(2)}) collective-permute-start(bf16[64,256]{1,0:T(8,128)(2,1)S(1)} %get-tuple-element.30), channel_id=1, source_target_pairs={{0,4},{4,0},{8,12},{12,8},{1,5},{5,1},{9,13},{13,9},{2,6},{6,2},{1... | collective-permute-start | bytes 98312 | tf_op jit(solution)/shard_map/ppermute | solution.py:409
  65.9 1.3 %collective-permute-start.20 = (bf16[64,256]{1,0:T(8,128)(2,1)S(1)}, bf16[64,256]{1,0:T(8,128)(2,1)S(1)}, u32[]{:S(2)}, u32[]{:S(2)}) collective-permute-start(bf16[64,256]{1,0:T(8,128)(2,1)S(1)} %shard_map.96), channel_id=1, source_target_pairs={{0,1},{1,0},{2,3},{3,2},{4,5},{5,4},{6,7},{7,6},{8,9},{9,8},{10,11... | collective-permute-start | bytes 98312 | tf_op jit(solution)/shard_map/ppermute | solution.py:404
  67.2 5.7 %collective-permute-start.21 = (bf16[64,384]{1,0:T(8,128)(2,1)S(1)}, bf16[64,384]{1,0:T(8,128)(2,1)S(1)}, u32[]{:S(2)}, u32[]{:S(2)}) collective-permute-start(bf16[64,384]{1,0:T(8,128)(2,1)S(1)} %pad_maximum_fusion.1), channel_id=1, source_target_pairs={{1,0},{5,1},{11,2},{15,3},{0,4},{4,5},{10,6},{14,7},{3,8},{7,9},{9... | collective-permute-start | bytes 147464 | tf_op jit(solution)/shard_map/ppermute | solution.py:446
  68.8 6.4 %collective-permute-start.22 = (bf16[64,384]{1,0:T(8,128)(2,1)S(1)}, bf16[64,384]{1,0:T(8,128)(2,1)S(1)}, u32[]{:S(2)}, u32[]{:S(2)}) collective-permute-start(bf16[64,384]{1,0:T(8,128)(2,1)S(1)} %pad_maximum_fusion.1), channel_id=1, source_target_pairs={{3,0},{7,1},{9,2},{13,3},{2,4},{6,5},{8,6},{12,7},{1,8},{5,9},{11,... | collective-permute-start | bytes 147464 | tf_op jit(solution)/shard_map/ppermute | solution.py:446
